TPU v7x, 768 devices: a whole 4x8x12 slice. The times are simulated.
768 devices in a mesh: dp: 12 (over x, z_hi), tensor: 64 (over y, z_lo, core).
Axes of the slice: x: 4, y: 8, z: 12 (z_hi: 3, z_lo: 4; z = z_hi * 4 + z_lo), core: 2. Of those that a mesh axis runs over, the one named last changes fastest.
Arguments:
- queries: bfloat16 [4608, 8192], P('dp', 'tensor'), may hold values from -180 to 180
- keys: bfloat16 [4608, 1024], P('dp'), may hold values from -4.5 to 4.5
- values: bfloat16 [4608, 1024], P('dp'), may hold values from -6 to 6
- grad_out: bfloat16 [4608, 8192], P('dp', 'tensor'), may hold values from -3 to 3
- weight: float32 [8256, 8192], P('dp', 'tensor'), as said below
- first_code: bfloat16 [8256, 8192], P('dp', 'tensor'), may hold values from -1 to 1, as said below
- first_rows: float32 [8256], P('dp'), may hold values from 0.2 to 5
- first_cols: float32 [8192], P('tensor'), may hold values from 0.2 to 5
- second_code: bfloat16 [8256, 8192], P('dp', 'tensor'), may hold values from 0 to 1, as said below
- second_rows: float32 [8256], P('dp'), may hold values from 0.5 to 20
- second_cols: float32 [8192], P('tensor'), may hold values from 0.5 to 20
Outputs:
- grad_queries: bfloat16 [4608, 8192], P('dp', 'tensor')
- new_weight: float32 [8256, 8192], P('dp', 'tensor')
- next_first_code: bfloat16 [8256, 8192], P('dp', 'tensor')
- next_first_rows: float32 [8256], P('dp')
- next_first_cols: float32 [8192], P('tensor')
- next_second_code: bfloat16 [8256, 8192], P('dp', 'tensor')
- next_second_rows: float32 [8256], P('dp')
- next_second_cols: float32 [8192], P('tensor')
Inputs may be any that keep to these rules, and one draw needn't show every extreme that they name: `weight`: rows 8192 onward are zero. `first_code`: rows 8192 onward are zero. `second_code`: rows 8192 onward are zero; all other entries are 0.05 or more.
All inputs are finite; a program needn't handle non-finite values.
Results may differ from a plain program's by a relative error of at most 0.023.
Values may be sent and summed in bfloat16 or wider, within the bound.
A program may use at most 64 MiB of HBM per device.

v0:
```python
import jax
import jax.numpy as jnp
from jax import lax
from jax.sharding import Mesh
from jax.sharding import PartitionSpec as P

H = 64
KVH = 8
HD = 128
DP = ("dp_0", "dp_1")
TENSOR = ("tensor_0", "tensor_1", "tensor_2")


beta_first = 0.9
beta_second = 0.95
learning = 0.01
decay_rate = 0.1
adam_eps = 1e-08
code_eps = 1e-06
correct_first = 1.0 - 0.9**10
correct_second = 1.0 - 0.95**10


def joined_along(parts, dim):
    shape = list(parts.shape[1:])
    shape[dim] *= parts.shape[0]
    return jnp.moveaxis(parts, 0, dim).reshape(shape)


def stacked_from(shard, axes, turns):
    parts = shard[None]
    for k in turns:
        parts = lax.all_gather(parts, axes[k], axis=0, tiled=True)
    held = [lax.axis_size(axes[k]) for k in reversed(turns)]
    parts = parts.reshape(*held, *shard.shape)
    turned = sorted(range(len(turns)), key=lambda place: turns[len(turns) - 1 - place])
    return parts.transpose(*turned, *range(len(turns), parts.ndim)).reshape(-1, *shard.shape)


def gather_axes(shard, axes, turns, dim):
    return joined_along(stacked_from(shard, axes, turns), dim)


def own_rows(terms, axes):
    so_far = terms.astype(jnp.bfloat16)
    for axis in axes:
        so_far = lax.psum_scatter(so_far, axis, scatter_dimension=0, tiled=True)
    return so_far.astype(jnp.float32)


def sent_to_all(shard, axis):
    copies = jnp.broadcast_to(shard, (lax.axis_size(axis), *shard.shape))
    return lax.all_to_all(copies, axis, split_axis=0, concat_axis=0, tiled=True)


def taken_together(shard, axis):
    return sent_to_all(shard, axis).max(axis=0)


def attend(queries, key_sel, value_sel, heads_dev):
    length = queries.shape[0]
    query_heads = queries.reshape(length, heads_dev, HD)
    scores = jnp.einsum(
        "qhd,kd->hqk", query_heads, key_sel, preferred_element_type=jnp.float32
    ) * HD ** (-0.5)
    future = lax.broadcasted_iota(jnp.int32, (length, length), 1) > lax.broadcasted_iota(
        jnp.int32, (length, length), 0
    )
    scores = jnp.where(future[None], -1e30, scores)
    highest = jnp.max(scores, axis=-1, keepdims=True)
    exponent = jnp.exp(scores - highest)
    probabilities = exponent / jnp.sum(exponent, axis=-1, keepdims=True)
    weights_half = probabilities.astype(jnp.bfloat16)
    attended = jnp.einsum(
        "hqk,kd->qhd", weights_half, value_sel, preferred_element_type=jnp.float32
    )
    return (probabilities, attended.astype(jnp.bfloat16).reshape(length, heads_dev * HD))


def attend_back(probabilities, attended, grad_half, key_sel, value_sel, heads_dev):
    length = grad_half.shape[0]
    grad_heads = grad_half.reshape(length, heads_dev, HD)
    grad_probs = jnp.einsum(
        "qhd,kd->hqk", grad_heads, value_sel, preferred_element_type=jnp.float32
    )
    row_dot = jnp.sum(
        grad_heads.astype(jnp.float32)
        * attended.reshape(length, heads_dev, HD).astype(jnp.float32),
        axis=-1,
    )
    grad_scores = (probabilities * (grad_probs - row_dot.T[:, :, None])).astype(jnp.bfloat16)
    grad_query = jnp.einsum(
        "hqk,kd->qhd", grad_scores, key_sel, preferred_element_type=jnp.float32
    ) * HD ** (-0.5)
    return grad_query.astype(jnp.bfloat16).reshape(length, heads_dev * HD)


def per_device(
    queries,
    keys,
    values,
    grad_out,
    weight,
    first_code,
    first_rows,
    first_cols,
    second_code,
    second_rows,
    second_cols,
):
    dp_count = lax.axis_size(DP)
    cols_dev = queries.shape[1]
    heads_dev = cols_dev // HD
    rows_dev = weight.shape[0]
    width_pad = dp_count * rows_dev
    tensor_index = lax.axis_index(TENSOR)
    kv_start = tensor_index * heads_dev // (H // KVH) * HD
    weight_half = weight.astype(jnp.bfloat16)
    full_grad = gather_axes(grad_out, TENSOR, (1, 0, 2), 1)
    padded = jnp.pad(full_grad, ((0, 0), (0, width_pad - full_grad.shape[1])))
    key_sel = lax.dynamic_slice_in_dim(keys, kv_start, HD, 1)
    value_sel = lax.dynamic_slice_in_dim(values, kv_start, HD, 1)
    probabilities, attended = attend(queries, key_sel, value_sel, heads_dev)
    block = padded
    grad_att = jnp.dot(
        block,
        lax.all_gather(weight_half, DP, axis=0, tiled=True),
        preferred_element_type=jnp.float32,
    )
    block = padded
    weight_grad = own_rows(
        jnp.einsum("sc,sh->ch", block, attended, preferred_element_type=jnp.float32), DP
    )
    grad_half = grad_att.astype(jnp.bfloat16)
    grad_queries = attend_back(probabilities, attended, grad_half, key_sel, value_sel, heads_dev)
    first = first_code.astype(jnp.float32) * jnp.minimum(first_rows[:, None], first_cols[None, :])
    second = second_code.astype(jnp.float32) * jnp.minimum(
        second_rows[:, None], second_cols[None, :]
    )
    first_new = beta_first * first + (1.0 - beta_first) * weight_grad
    second_new = beta_second * second + (1.0 - beta_second) * weight_grad * weight_grad
    step_size = first_new / correct_first / (jnp.sqrt(second_new / correct_second) + adam_eps)
    new_weight = weight - learning * (step_size + decay_rate * weight)
    first_abs = jnp.abs(first_new)
    second_abs = jnp.abs(second_new)
    local_rows_max = jnp.stack([jnp.max(first_abs, axis=1), jnp.max(second_abs, axis=1)])
    local_cols_max = jnp.stack([jnp.max(first_abs, axis=0), jnp.max(second_abs, axis=0)])
    rows_mine = taken_together(local_rows_max, TENSOR)
    cols_mine = taken_together(local_cols_max, DP)
    next_first_code = (
        first_new / (jnp.minimum(rows_mine[0][:, None], cols_mine[0][None, :]) + code_eps)
    ).astype(jnp.bfloat16)
    next_second_code = (
        second_new / (jnp.minimum(rows_mine[1][:, None], cols_mine[1][None, :]) + code_eps)
    ).astype(jnp.bfloat16)
    return (
        grad_queries,
        new_weight,
        next_first_code,
        rows_mine[0],
        cols_mine[0],
        next_second_code,
        rows_mine[1],
        cols_mine[1],
    )


def solution(mesh):
    finer = Mesh(
        mesh.devices.reshape(4, 3, 8, 4, 2), ("dp_0", "dp_1", "tensor_0", "tensor_1", "tensor_2")
    )
    placed = (
        P(DP, TENSOR),
        P(DP, None),
        P(DP, None),
        P(DP, TENSOR),
        P(DP, TENSOR),
        P(DP, TENSOR),
        P(DP),
        P(TENSOR),
        P(DP, TENSOR),
        P(DP),
        P(TENSOR),
    )
    return jax.shard_map(
        per_device,
        mesh=finer,
        in_specs=placed,
        out_specs=(
            P(DP, TENSOR),
            P(DP, TENSOR),
            P(DP, TENSOR),
            P(DP),
            P(TENSOR),
            P(DP, TENSOR),
            P(DP),
            P(TENSOR),
        ),
        check_vma=False,
    )
```

profile of v0, /device:TPU:1, one launch (start us, length us, event | category | flops | bytes accessed | tf_op | source)
XLA Modules:
  0.0 318.3 jit_solution(12744803033808711787)
XLA Ops:
  7.2 0.0 copy-start
  7.2 0.0 all-gather.5.cloned.1.call-start
  7.2 18.2 %all-gather = bf16[1536,128]{1,0:T(8,128)(2,1)} all-gather(bf16[384,128]{1,0:T(8,128)(2,1)} %param.14), channel_id=2, replica_groups=mesh['dp_0'=4,'dp_1'=3,'tensor_0'=8,'tensor_1'=4,'tensor_2'=2] {'tensor_1'}, dimensions={0}, use_global_device_ids=true | all-gather | bytes 491520 | tf_op jit(solution)/shard_map/all_gather | solution.py:33
  25.4 0.0 all-gather.5.cloned.1.call-update
  25.5 0.0 all-gather.7.cloned.1.call-start
  25.5 54.2 %all-gather.5.cloned.1.call-done = bf16[32,384,128]{2,1,0:T(8,128)(2,1)} async-done(((bf16[4,384,128]{2,1,0:T(8,128)(2,1)}), bf16[32,384,128]{2,1,0:T(8,128)(2,1)}) %all-gather.5.cloned.1.call-update) | async-done | bytes 3145744 | tf_op jit(solution)/shard_map/all_gather | solution.py:33
  79.7 0.0 all-gather.7.cloned.1.call-update
  79.8 0.0 reduce-scatter.3.cloned.1.call-start
  79.8 0.0 copy-done
  79.8 1.2 fusion.37
  81.0 0.1 fusion.16
  81.1 1.2 convolution_convert_fusion.1
  82.3 29.6 %all-gather.7.cloned.1.call-done = bf16[64,384,128]{2,1,0:T(8,128)(2,1)} async-done(((bf16[32,384,128]{2,1,0:T(8,128)(2,1)}), bf16[64,384,128]{2,1,0:T(8,128)(2,1)}) %all-gather.7.cloned.1.call-update) | async-done | bytes 6291472 | tf_op jit(solution)/shard_map/all_gather | solution.py:33
  111.9 6.2 %copy.31 = bf16[8,4,2,384,128]{4,3,2,1,0:T(8,128)(2,1)} copy(bf16[8,4,2,384,128]{4,3,1,0,2:T(8,128)(2,1)} %bitcast.74) | data formatting | bytes 12582912 | tf_op jit(solution)/shard_map/transpose | solution.py:37
  118.1 8.7 %copy.32 = bf16[384,64,128]{0,2,1:T(8,128)(2,1)} copy(bf16[384,64,128]{2,0,1:T(8,128)(2,1)} %bitcast.71) | data formatting | bytes 12582912 | tf_op jit(solution)/shard_map/transpose | solution.py:27
  126.7 0.0 copy-start.5
  126.7 0.0 copy-start.8
  126.8 0.0 copy-start.9
  126.8 6.0 %convolution_convert_fusion = bf16[8256,128]{1,0:T(8,128)(2,1)} fusion(bf16[384,8192]{0,1:T(8,128)(2,1)} %bitcast.72, bf16[128,384]{1,0:T(8,128)(2,1)S(1)} %convolution_convert_fusion.1), kind=kOutput, calls=%fused_computation | convolution fusion | flops 812654592 | bytes 8503296 | tf_op jit(solution)/shard_map/sc,sh->ch/dot_general | solution.py:132
  132.8 0.0 reduce-scatter.3.cloned.1.call-update
  132.8 0.0 reduce-scatter.5.cloned.1.call-start
  132.9 37.2 %reduce-scatter.3.cloned.1.call-done = bf16[2064,128]{1,0:T(8,128)(2,1)} async-done(((bf16[8256,128]{1,0:T(8,128)(2,1)}), bf16[2064,128]{1,0:T(8,128)(2,1)}) %reduce-scatter.3.cloned.1.call-update) | async-done | bytes 528400 | tf_op jit(solution)/shard_map/reduce_scatter | solution.py:47
  170.0 0.0 reduce-scatter.5.cloned.1.call-update
  170.1 0.0 all-gather.9.cloned.1.call-start
  170.1 41.9 %reduce-scatter.5.cloned.1.call-done = bf16[688,128]{1,0:T(8,128)(2,1)} async-done(((bf16[2064,128]{1,0:T(8,128)(2,1)}), bf16[688,128]{1,0:T(8,128)(2,1)}) %reduce-scatter.5.cloned.1.call-update) | async-done | bytes 176144 | tf_op jit(solution)/shard_map/reduce_scatter | solution.py:47
  212.0 0.0 copy-done.1
  212.0 0.0 copy-done.2
  212.0 0.0 copy-done.3
  212.0 0.0 copy-done.4
  212.0 0.0 copy-done.5
  212.0 2.4 abs_reduce_fusion.3
  214.4 0.0 all-gather.9.cloned.1.call-update
  214.5 0.6 broadcast_in_dim.23
  215.1 8.4 %all-to-all-start.1 = ((f32[12,2,128]{2,1,0:T(2,128)}), f32[12,2,128]{2,1,0:T(2,128)S(1)}, u32[]{:S(2)}, u32[]{:S(2)}) async-start(f32[12,2,128]{2,1,0:T(2,128)} %broadcast_in_dim.23), calls=%async_computation.3 | async-start | bytes 24576 | tf_op jit(solution)/shard_map/all_to_all | solution.py:53
  223.5 8.9 %all-to-all-done.1 = f32[12,2,128]{2,1,0:T(2,128)S(1)} async-done(((f32[12,2,128]{2,1,0:T(2,128)}), f32[12,2,128]{2,1,0:T(2,128)S(1)}, u32[]{:S(2)}, u32[]{:S(2)}) %all-to-all-start.1) | async-done | bytes 12320 | tf_op jit(solution)/shard_map/all_to_all | solution.py:53
  232.4 0.9 broadcast_in_dim.22
  233.3 9.4 %all-to-all-start = ((f32[64,2,688]{2,1,0:T(2,128)}), f32[64,2,688]{2,1,0:T(2,128)S(1)}, u32[]{:S(2)}, u32[]{:S(2)}) async-start(f32[64,2,688]{2,1,0:T(2,128)} %broadcast_in_dim.22), calls=%async_computation.2 | async-start | bytes 786432 | tf_op jit(solution)/shard_map/all_to_all | solution.py:53
  242.8 0.0 copy-start.10
  242.8 0.0 copy-start.11
  242.8 17.7 %all-to-all-done = f32[64,2,688]{2,1,0:T(2,128)S(1)} async-done(((f32[64,2,688]{2,1,0:T(2,128)}), f32[64,2,688]{2,1,0:T(2,128)S(1)}, u32[]{:S(2)}, u32[]{:S(2)}) %all-to-all-start) | async-done | bytes 352288 | tf_op jit(solution)/shard_map/all_to_all | solution.py:53
  260.5 0.2 reduce_max.66
  260.7 0.0 copy-start.6
  260.7 0.0 copy-start.7
  260.8 2.1 divide_convert_fusion
  262.8 42.0 %all-gather.9.cloned.1.call-done = bf16[8256,128]{1,0:T(8,128)(2,1)} async-done(((bf16[688,128]{1,0:T(8,128)(2,1)}), bf16[8256,128]{1,0:T(8,128)(2,1)}) %all-gather.9.cloned.1.call-update) | async-done | bytes 2113552 | tf_op jit(solution)/shard_map/all_gather | solution.py:127
  304.8 4.8 %fusion.22 = (f32[384]{0:T(512)S(1)}, bf16[384,128]{0,1:T(8,128)(2,1)S(1)}) fusion(bf16[128,384]{1,0:T(8,128)(2,1)S(1)} %convolution_convert_fusion.1, bf16[8256,128]{1,0:T(8,128)(2,1)} %all-gather.9.cloned.1.call-done, bf16[384,8192]{0,1:T(8,128)(2,1)} %bitcast.73), kind=kOutput, calls=%fused_computation.37 | convolution fusion | flops 811843200 | bytes 8603136 | tf_op jit(solution)/shard_map/dot_general | solution.py:125
  309.6 1.4 fusion.14
  311.0 0.8 copy.34
  (17 shorter events, 0.1 us)
Async XLA Ops:
  7.2 72.7 %copy-start = (bf16[384,1024]{1,0:T(8,128)(2,1)S(1)}, bf16[384,1024]{1,0:T(8,128)(2,1)}, u32[]{:S(2)}) copy-start(bf16[384,1024]{1,0:T(8,128)(2,1)} %param.12) | copy-start | bytes 2359300
  7.2 72.5 %all-gather.5.cloned.1.call-start = ((), (), s32[]{:S(2)}) async-start(), calls=%async_computation.4 | async-start | bytes 3538944 | tf_op jit(solution)/shard_map/all_gather | solution.py:33
  25.5 86.4 %all-gather.7.cloned.1.call-start = ((), (), s32[]{:S(2)}) async-start(), calls=%async_computation.5 | async-start | bytes 9437184 | tf_op jit(solution)/shard_map/all_gather | solution.py:33
  79.8 90.3 %reduce-scatter.3.cloned.1.call-start = ((), (), s32[]{:S(2)}) async-start(), calls=%async_computation.7 | async-start | bytes 2641920 | tf_op jit(solution)/shard_map/reduce_scatter | solution.py:47
  126.7 85.3 %copy-start.1 = (bf16[688,128]{1,0:T(8,128)(2,1)S(1)}, bf16[688,128]{1,0:T(8,128)(2,1)}, u32[]{:S(2)}) copy-start(bf16[688,128]{1,0:T(8,128)(2,1)} %param.16) | copy-start | bytes 528388
  126.7 85.3 %copy-start.2 = (bf16[688,128]{1,0:T(8,128)(2,1)S(1)}, bf16[688,128]{1,0:T(8,128)(2,1)}, u32[]{:S(2)}) copy-start(bf16[688,128]{1,0:T(8,128)(2,1)} %param.19) | copy-start | bytes 528388
  126.7 85.3 %copy-start.3 = (f32[688,128]{1,0:T(8,128)S(1)}, f32[688,128]{1,0:T(8,128)}, u32[]{:S(2)}) copy-start(f32[688,128]{1,0:T(8,128)} %param.15) | copy-start | bytes 1056772
  126.7 85.3 %copy-start.4 = (f32[688]{0:T(1024)S(1)}, f32[688]{0:T(1024)}, u32[]{:S(2)}) copy-start(f32[688]{0:T(1024)} %param.17) | copy-start | bytes 8260
  126.7 85.2 %copy-start.5 = (f32[688]{0:T(1024)S(1)}, f32[688]{0:T(1024)}, u32[]{:S(2)}) copy-start(f32[688]{0:T(1024)} %param.20) | copy-start | bytes 8260
  126.7 85.2 %copy-start.8 = (f32[128]{0:T(128)S(1)}, f32[128]{0:T(128)}, u32[]{:S(2)}) copy-start(f32[128]{0:T(128)} %param.18) | copy-start | bytes 1540
  126.8 85.2 %copy-start.9 = (f32[128]{0:T(128)S(1)}, f32[128]{0:T(128)}, u32[]{:S(2)}) copy-start(f32[128]{0:T(128)} %param.21) | copy-start | bytes 1540
  132.8 79.2 %reduce-scatter.5.cloned.1.call-start = ((), (), s32[]{:S(2)}) async-start(), calls=%async_computation.8 | async-start | bytes 704512 | tf_op jit(solution)/shard_map/reduce_scatter | solution.py:47
  170.1 134.8 %all-gather.9.cloned.1.call-start = ((), (), s32[]{:S(2)}) async-start(), calls=%async_computation.6 | async-start | bytes 2289664 | tf_op jit(solution)/shard_map/all_gather | solution.py:127
  215.1 17.3 %all-to-all-start.1 = ((f32[12,2,128]{2,1,0:T(2,128)}), f32[12,2,128]{2,1,0:T(2,128)S(1)}, u32[]{:S(2)}, u32[]{:S(2)}) async-start(f32[12,2,128]{2,1,0:T(2,128)} %broadcast_in_dim.23), calls=%async_computation.3 | async-start | bytes 24576 | tf_op jit(solution)/shard_map/all_to_all | solution.py:53
  233.3 27.2 %all-to-all-start = ((f32[64,2,688]{2,1,0:T(2,128)}), f32[64,2,688]{2,1,0:T(2,128)S(1)}, u32[]{:S(2)}, u32[]{:S(2)}) async-start(f32[64,2,688]{2,1,0:T(2,128)} %broadcast_in_dim.22), calls=%async_computation.2 | async-start | bytes 786432 | tf_op jit(solution)/shard_map/all_to_all | solution.py:53
  242.8 68.2 %copy-start.10 = (f32[128]{0:T(128)}, f32[128]{0:T(128)S(1)}, u32[]{:S(2)}) copy-start(f32[128]{0:T(128)S(1)} %get-tuple-element.68) | copy-start | bytes 1540
  242.8 68.2 %copy-start.11 = (f32[128]{0:T(128)}, f32[128]{0:T(128)S(1)}, u32[]{:S(2)}) copy-start(f32[128]{0:T(128)S(1)} %get-tuple-element.69) | copy-start | bytes 1540
  260.7 50.2 %copy-start.6 = (f32[688]{0:T(1024)}, f32[688]{0:T(1024)S(1)}, u32[]{:S(2)}) copy-start(f32[688]{0:T(1024)S(1)} %get-tuple-element.62) | copy-start | bytes 8260
  260.7 50.2 %copy-start.7 = (f32[688]{0:T(1024)}, f32[688]{0:T(1024)S(1)}, u32[]{:S(2)}) copy-start(f32[688]{0:T(1024)S(1)} %get-tuple-element.63) | copy-start | bytes 8260
Sparse Core Ops, SparseCore 0:
  25.6 54.0 all-gather.4
  82.1 29.7 all-gather.6
  132.9 37.0 reduce-scatter.2
  173.0 38.8 reduce-scatter.4
  215.8 89.0 all-gather.8
where the time goes:
time: 322 us; the launch traced here: 318 us
  waiting for transfers between devices  232 us (72%)
  blocking collectives  18.2 us (6%)
  starting transfers between devices  18 us (6%)
  local copies, waits for them, and re-layouts  17.2 us (5%)
  matrix products  14.4 us (4%)
  between operations  14 us (4%)
  other arithmetic  4.86 us (2%)
    all_gather x2, waiting for transfers between devices, stacked_from(): parts = lax.all_gather(parts, axes[k], axis=0, tiled=True)  83.8 us
    reduce_scatter x2, waiting for transfers between devices, own_rows(): so_far = lax.psum_scatter(so_far, axis, scatter_dimension=0, tiled=True)  79 us
    all_gather x1, waiting for transfers between devices, per_device(): lax.all_gather(weight_half, DP, axis=0, tiled=True)  42 us
    all_to_all x2, waiting for transfers between devices, sent_to_all(): return lax.all_to_all(copies, axis, split_axis=0, concat_axis=0, tiled=True)  26.7 us
    all_gather x1, blocking collectives, stacked_from(): parts = lax.all_gather(parts, axes[k], axis=0, tiled=True)  18.2 us
    all_to_all x2, starting transfers between devices, sent_to_all(): return lax.all_to_all(copies, axis, split_axis=0, concat_axis=0, tiled=True)  17.8 us
    transpose x1, local copies, waits for them, and re-layouts, joined_along(): return jnp.moveaxis(parts, 0, dim).reshape(shape)  8.67 us
  transfers between devices with their start and end apart: 7, of which 7 were waited for; matrix products, arithmetic and copies ran while one was open for 2% of the time, Pallas kernels for 0%

commit v1 on v0

v1 whole, which is shorter than its diff:
```python
import functools

import jax
import jax.numpy as jnp
from jax import lax
from jax.experimental import pallas as pl
from jax.experimental.pallas import tpu as pltpu
from jax.sharding import Mesh
from jax.sharding import PartitionSpec as P

NX, NZH, NY, NZL, NC = 4, 3, 8, 4, 2
AXES = ("x", "zh", "y", "zl", "core")
DP = ("x", "zh")
TENSOR = ("y", "zl", "core")
MESH = pl.DeviceIdType.MESH

HD = 128
SEQ = 384
ROWS = 688
UNIT = 16
UNITS = ROWS // UNIT
ALL_UNITS = 512
QUART = 11
QROWS = QUART * UNIT
PADROWS = 4 * QROWS
SCALE = HD ** (-0.5)

beta_first = 0.9
beta_second = 0.95
learning = 0.01
decay_rate = 0.1
adam_eps = 1e-08
code_eps = 1e-06
correct_first = 1.0 - 0.9**10
correct_second = 1.0 - 0.95**10

F32 = jnp.float32
BF16 = jnp.bfloat16
NT = (((1,), (1,)), ((), ()))


def mod(a, n):
    return lax.rem(a + n, n)


def row_chunks():
    return [(c, 128 * c, min(128, ROWS - 128 * c)) for c in range(6)]


def lane_rows(values):
    highest = jnp.max(values, axis=1, keepdims=True)
    out = []
    for c, start, size in row_chunks():
        eye = lax.broadcasted_iota(jnp.int32, (size, 128), 0) == lax.broadcasted_iota(
            jnp.int32, (size, 128), 1
        )
        out.append(
            jnp.max(jnp.where(eye, highest[start : start + size], 0.0), axis=0, keepdims=True)
        )
    out.append(jnp.zeros((2, 128), F32))
    return jnp.concatenate(out, axis=0)


def down_rows(row):
    return jnp.broadcast_to(row, (128, 128)).T


def body(
    q_hbm,
    k_hbm,
    v_hbm,
    g_hbm,
    w_hbm,
    fc_hbm,
    frow,
    fcol,
    sc_hbm,
    srow,
    scol,
    gq_out,
    nw_out,
    nfc_out,
    nfr_out,
    nfcol_out,
    nsc_out,
    nsr_out,
    nscol_out,
    q,
    kk,
    vv,
    g,
    w,
    fc,
    sc,
    gt,
    gz,
    wt,
    att,
    prob,
    acct,
    ga_stage,
    ga_in,
    dwacc,
    dw_stage,
    dw_in,
    fnew,
    snew,
    st,
    st_in,
    y_in,
    zl_in,
    mine,
    fin,
    cst,
    c_in,
    in_sem,
    r_send,
    r_recv,
    ring_send,
    ring_recv,
    d_send,
    d_recv,
    att_send,
    att_recv,
    w_send,
    w_recv,
    ga_send,
    ga_recv,
    dw_send,
    dw_recv,
    core_send,
    core_recv,
    y_send,
    y_recv,
    zl_send,
    zl_recv,
    c_send,
    c_recv,
):
    x, zh, y, zl, k = (lax.axis_index(a) for a in AXES)
    t = 8 * y + 2 * zl + k
    pair = lax.div(y, 2)

    def rcopy(src, dst, send, recv, **dev):
        return pltpu.make_async_remote_copy(
            src_ref=src, dst_ref=dst, send_sem=send, recv_sem=recv, device_id=dev, device_id_type=MESH
        )

    heads = pl.ds(pl.multiple_of(y * HD, HD), HD)
    loads = [
        pltpu.make_async_copy(src, dst, in_sem.at[i])
        for i, (src, dst) in enumerate(
            [
                (g_hbm, g),
                (q_hbm, q),
                (k_hbm.at[:, heads], kk),
                (v_hbm.at[:, heads], vv),
                (w_hbm, w),
                (fc_hbm, fc),
                (sc_hbm, sc),
            ]
        )
    ]
    for load in loads:
        load.start()

    barrier = pltpu.get_barrier_semaphore()

    def greet(i, carry):
        dy = lax.div(i, 24)
        rest = lax.rem(i, 24)
        oz = lax.div(rest, 8)
        ol = lax.div(lax.rem(rest, 8), 2)
        ok = lax.rem(rest, 2)
        ny = mod(y + dy - 1, NY)

        @pl.when(jnp.logical_not((ny == y) & (oz == zh) & (ol == zl) & (ok == k)))
        def _():
            pl.semaphore_signal(
                barrier, inc=1, device_id={"zh": oz, "y": ny, "zl": ol, "core": ok}, device_id_type=MESH
            )

        return carry

    lax.fori_loop(0, 72, greet, 0)
    for dy in range(2, 7):
        pl.semaphore_signal(barrier, inc=1, device_id={"y": mod(y + dy, NY)}, device_id_type=MESH)
    for dx in range(1, NX):
        for dz in range(NZH):
            pl.semaphore_signal(
                barrier,
                inc=1,
                device_id={"x": mod(x + dx, NX), "zh": mod(zh + dz, NZH)},
                device_id_type=MESH,
            )

    loads[0].wait()
    gt[...] = g[...].T

    my_d = 3 * pair + zh
    my_q = 2 * lax.rem(y, 2) + k
    for i in range(QUART):
        r = QUART * my_q + i

        @pl.when((r >= UNITS) | (UNITS * my_d + r >= ALL_UNITS))
        def _():
            for jj in range(NZH):
                gz[jj, pair, pl.ds(pl.multiple_of(UNIT * r, UNIT), UNIT), :] = jnp.zeros(
                    (UNIT, SEQ), BF16
                )

    for i in (1, 2, 3):
        loads[i].wait()
    for i in range(3):
        rows, cols = pl.ds(128 * i, 128), pl.ds(0, 128 * (i + 1))
        scores = (
            lax.dot_general(q[rows, :], kk[cols, :], NT, preferred_element_type=F32) * SCALE
        )
        future = lax.broadcasted_iota(jnp.int32, scores.shape, 1) > (
            lax.broadcasted_iota(jnp.int32, scores.shape, 0) + 128 * i
        )
        scores = jnp.where(future, -1e30, scores)
        exponent = jnp.exp(scores - jnp.max(scores, axis=-1, keepdims=True))
        probabilities = exponent / jnp.sum(exponent, axis=-1, keepdims=True)
        prob[rows, cols] = probabilities
        att[0, rows, :] = jnp.dot(
            probabilities.astype(BF16), vv[cols, :], preferred_element_type=F32
        ).astype(BF16)

    loads[4].wait()
    wt[x] = w[...].astype(BF16).T

    pl.semaphore_wait(barrier, 71 + 5 + 9)

    def spread(u, carry):
        unit = 8 * t + u
        d = lax.div(unit, UNITS)
        r = unit - UNITS * d
        quarter = lax.div(r, QUART)
        i = r - QUART * quarter
        zd = lax.rem(d, NZH)
        xd = lax.div(d, NZH)
        yd = 2 * xd + lax.div(quarter, 2)
        kd = lax.rem(quarter, 2)
        jj = mod(zh - zd, NZH)
        src = gt.at[pl.ds(pl.multiple_of(UNIT * u, UNIT), UNIT), :]
        place = pl.ds(pl.multiple_of(UNIT * r, UNIT), UNIT)
        home = (zd == zh) & (yd == y) & (kd == k)

        @pl.when(home)
        def _():
            gz[0, xd, place, :] = gt[pl.ds(pl.multiple_of(UNIT * u, UNIT), UNIT), :]

        for o in range(NZL):
            copy = rcopy(
                src,
                gz.at[jj, xd, place, :],
                r_send.at[u, o],
                r_recv.at[jj, i],
                zh=zd,
                y=yd,
                zl=mod(zl + o, NZL),
                core=kd,
            )
            if o == 0:
                pl.when(jnp.logical_not(home))(copy.start)
            else:
                copy.start()
        return carry

    lax.fori_loop(0, 8, spread, 0)

    sends = []
    for dz in (1, 2):
        copy = rcopy(
            att.at[0], att.at[NZH - dz], att_send.at[dz - 1], att_recv.at[NZH - dz - 1], zh=mod(zh + dz, NZH)
        )
        copy.start()
        sends.append(copy)
    for dx in (1, 3, 2):
        copy = rcopy(wt.at[x], wt.at[x], w_send.at[dx - 1], w_recv.at[NX - dx - 1], x=mod(x + dx, NX))
        copy.start()
        sends.append(copy)

    def home_ready(jj):
        def one(i, carry):
            r = QUART * my_q + i
            unit = UNITS * my_d + r
            own = lax.div(unit, 8) == t
            there = (r < UNITS) & (unit < ALL_UNITS)
            if jj == 0:
                there = there & jnp.logical_not(own)

            @pl.when(there)
            def _():
                piece = gz.at[jj, pair, pl.ds(pl.multiple_of(UNIT * r, UNIT), UNIT), :]
                rcopy(piece, piece, r_send.at[0, 0], r_recv.at[jj, i], core=k).wait_recv()

            return carry

        lax.fori_loop(0, QUART, one, 0)

    HALF = 96

    def part(jj, source, r):
        quarter = 2 * lax.rem(source, 2) + k
        start, size = 0, QROWS
        if jj == 2 and r[1] == 4:
            start, size = (0, HALF) if r[0] == 0 else (HALF, QROWS - HALF)
        return gz.at[
            jj, lax.div(source, 2), pl.ds(pl.multiple_of(QROWS * quarter + start, UNIT), size), :
        ]

    def from_source(way, hops):
        return mod(y - hops, NY) if way == 0 else mod(y + hops, NY)

    def forward(way, jj, hops):
        piece = part(jj, from_source(way, hops), (way, hops + 1))
        copy = rcopy(
            piece,
            piece,
            ring_send.at[way, jj, hops],
            ring_recv.at[way, jj, hops],
            y=mod(y + 1, NY) if way == 0 else mod(y - 1, NY),
        )
        copy.start()
        sends.append(copy)

    def arrived(way, jj, hops):
        piece = part(jj, from_source(way, hops), (way, hops))
        rcopy(
            piece, piece, ring_send.at[way, jj, hops - 1], ring_recv.at[way, jj, hops - 1], y=y
        ).wait_recv()

    def to_partner(way, jj, hops):
        piece = part(jj, from_source(way, hops), (way, hops))
        copy = rcopy(piece, piece, d_send.at[way, jj, hops], d_recv.at[way, jj, hops], core=1 - k)
        copy.start()
        sends.append(copy)

    def from_partner(way, jj, hops):
        source = from_source(way, hops)
        quarter = 2 * lax.rem(source, 2) + (1 - k)
        start, size = 0, QROWS
        if jj == 2 and hops == 4:
            start, size = (0, HALF) if way == 0 else (HALF, QROWS - HALF)
        piece = gz.at[
            jj, lax.div(source, 2), pl.ds(pl.multiple_of(QROWS * quarter + start, UNIT), size), :
        ]
        rcopy(
            piece, piece, d_send.at[way, jj, hops], d_recv.at[way, jj, hops], core=1 - k
        ).wait_recv()

    reach = {(0, 0): 4, (1, 0): 3, (0, 1): 3, (1, 1): 4, (0, 2): 4, (1, 2): 4}

    def start_ring(jj):
        home_ready(jj)
        forward(0, jj, 0)
        forward(1, jj, 0)
        to_partner(0, jj, 0)

    def pass_on(jj, hops):
        for way in (0, 1):
            if hops <= reach[way, jj]:
                arrived(way, jj, hops)
                if hops < reach[way, jj]:
                    forward(way, jj, hops)
                to_partner(way, jj, hops)

    def partner_has(jj, hops):
        for way in (0, 1):
            if hops == 0 and way == 1:
                continue
            if hops <= reach[way, jj]:
                from_partner(way, jj, hops)

    def multiply(jj, xo):
        block = gz[jj, xo, 0:ROWS, :]
        term = jnp.dot(wt[xo], block, preferred_element_type=F32)
        acct[jj] = term if jj not in started else acct[jj] + term
        started.add(jj)

    def weight_term(jj, xo):
        term = jnp.dot(gz[jj, xo, 0:ROWS, :], att[jj], preferred_element_type=F32)
        if jj == 0:
            dwacc[xo] = term
        else:
            dwacc[xo] = dwacc[xo] + term

    started = set()

    def xo_of(off):
        return mod(pair + off, NX)

    start_ring(0)
    pass_on(0, 1)
    start_ring(1)
    pass_on(0, 2)
    pass_on(1, 1)
    start_ring(2)
    for dx in (1, 2, 3):
        rcopy(wt.at[0], wt.at[mod(x + dx, NX)], w_send.at[0], w_recv.at[dx - 1], x=x).wait_recv()
    pass_on(0, 3)
    pass_on(1, 2)
    partner_has(0, 0)
    partner_has(0, 1)
    multiply(0, xo_of(0))
    weight_term(0, xo_of(0))
    pass_on(2, 1)
    pass_on(0, 4)
    partner_has(0, 2)
    partner_has(0, 3)
    multiply(0, xo_of(1))
    weight_term(0, xo_of(1))
    pass_on(1, 3)
    multiply(0, xo_of(3))
    weight_term(0, xo_of(3))
    pass_on(2, 2)
    partner_has(0, 4)
    multiply(0, xo_of(2))
    weight_term(0, xo_of(2))
    pass_on(1, 4)
    for dz in (1, 2):
        rcopy(att.at[0], att.at[dz], att_send.at[0], att_recv.at[dz - 1], zh=zh).wait_recv()
    for hops in range(5):
        partner_has(1, hops)
    for off in (0, 1, 3, 2):
        multiply(1, xo_of(off))
        weight_term(1, xo_of(off))

    def send_grad(jj):
        ga_stage[jj - 1] = acct[jj].astype(BF16)
        copy = rcopy(
            ga_stage.at[jj - 1],
            ga_in.at[NZH - jj - 1],
            ga_send.at[jj - 1],
            ga_recv.at[NZH - jj - 1],
            zh=mod(zh + jj, NZH),
        )
        copy.start()
        sends.append(copy)

    def send_term(off):
        xo = xo_of(off)

        @pl.when(xo != x)
        def _():
            dw_stage[xo] = dwacc[xo].astype(BF16)
            rcopy(
                dw_stage.at[xo],
                dw_in.at[mod(x - xo, NX) - 1],
                dw_send.at[xo],
                dw_recv.at[mod(x - xo, NX) - 1],
                x=xo,
            ).start()

    send_grad(1)
    pass_on(2, 3)
    partner_has(2, 0)
    partner_has(2, 1)
    weight_term(2, xo_of(0))
    send_term(0)
    partner_has(2, 2)
    partner_has(2, 3)
    for off in (1, 3):
        weight_term(2, xo_of(off))
        send_term(off)
    pass_on(2, 4)
    partner_has(2, 4)
    weight_term(2, xo_of(2))
    send_term(2)
    for off in (0, 1, 3, 2):
        multiply(2, xo_of(off))
    send_grad(2)

    for i in (5, 6):
        loads[i].wait()
    for dx in (1, 2, 3):
        rcopy(dw_stage.at[0], dw_in.at[dx - 1], dw_send.at[0], dw_recv.at[dx - 1], x=x).wait_recv()
    for c, start, size in row_chunks():
        rows = pl.ds(start, size)
        grad = (
            (dwacc[x, rows, :] + dw_in[0, rows, :].astype(F32))
            + dw_in[1, rows, :].astype(F32)
            + dw_in[2, rows, :].astype(F32)
        )
        tile = pl.ds(128 * c, size)
        low_first = jnp.minimum(
            down_rows(frow[0:1, 128 * c : 128 * c + 128])[:size] if size == 128
            else down_rows(jnp.concatenate([frow[0:1, tile], jnp.zeros((1, 128 - size), F32)], axis=1))[:size],
            fcol[...],
        )
        low_second = jnp.minimum(
            down_rows(srow[0:1, 128 * c : 128 * c + 128])[:size] if size == 128
            else down_rows(jnp.concatenate([srow[0:1, tile], jnp.zeros((1, 128 - size), F32)], axis=1))[:size],
            scol[...],
        )
        first = fc[rows, :].astype(F32) * low_first
        second = sc[rows, :].astype(F32) * low_second
        first_new = beta_first * first + (1.0 - beta_first) * grad
        second_new = beta_second * second + (1.0 - beta_second) * grad * grad
        step_size = first_new / correct_first / (jnp.sqrt(second_new / correct_second) + adam_eps)
        weight = w[rows, :]
        nw_out[rows, :] = weight - learning * (step_size + decay_rate * weight)
        fnew[rows, :] = first_new
        snew[rows, :] = second_new

    first_abs, second_abs = jnp.abs(fnew[...]), jnp.abs(snew[...])
    st[0] = lane_rows(first_abs)
    st[1] = lane_rows(second_abs)
    cst[0:1, :] = jnp.max(first_abs, axis=0, keepdims=True)
    cst[1:2, :] = jnp.max(second_abs, axis=0, keepdims=True)

    copy = rcopy(st.at[1 - k], st_in, core_send.at[0], core_recv.at[0], core=1 - k)
    copy.start()
    sends.append(copy)
    for rel in range(1, NX * NZH):
        dx, dz = rel // NZH, rel % NZH
        back = ((NX - dx) % NX) * NZH + (NZH - dz) % NZH
        copy = rcopy(
            cst,
            c_in.at[back - 1],
            c_send.at[rel - 1],
            c_recv.at[back - 1],
            x=mod(x + dx, NX),
            zh=mod(zh + dz, NZH),
        )
        copy.start()
        sends.append(copy)
    rcopy(st.at[0], st_in, core_send.at[0], core_recv.at[0], core=k).wait_recv()
    mine[0] = jnp.maximum(st[k], st_in[...])
    for dy in range(1, NY):
        copy = rcopy(
            mine.at[0], y_in.at[NY - dy - 1], y_send.at[dy - 1], y_recv.at[NY - dy - 1], y=mod(y + dy, NY)
        )
        copy.start()
        sends.append(copy)

    def back_rows(i):
        rows, cols = pl.ds(128 * i, 128), pl.ds(0, 128 * (i + 1))
        total = acct[0, :, rows]
        for s in range(2):
            total = total + ga_in[s, :, rows].astype(F32)
        grad_half = total.astype(BF16).T
        grad_probs = lax.dot_general(grad_half, vv[cols, :], NT, preferred_element_type=F32)
        row_dot = jnp.sum(
            grad_half.astype(F32) * att[0, rows, :].astype(F32), axis=-1, keepdims=True
        )
        grad_scores = (prob[rows, cols] * (grad_probs - row_dot)).astype(BF16)
        gq_out[rows, :] = (
            jnp.dot(grad_scores, kk[cols, :], preferred_element_type=F32) * SCALE
        ).astype(BF16)

    for s in range(2):
        rcopy(ga_stage.at[0], ga_in.at[s], ga_send.at[0], ga_recv.at[s], zh=zh).wait_recv()
    back_rows(0)
    back_rows(1)

    for dy in range(1, NY):
        rcopy(mine.at[0], y_in.at[dy - 1], y_send.at[0], y_recv.at[dy - 1], y=y).wait_recv()
    mine[1] = jnp.maximum(mine[0], jnp.max(y_in[...], axis=0))
    for dl in range(1, NZL):
        copy = rcopy(
            mine.at[1],
            zl_in.at[NZL - dl - 1],
            zl_send.at[dl - 1],
            zl_recv.at[NZL - dl - 1],
            zl=mod(zl + dl, NZL),
        )
        copy.start()
        sends.append(copy)
    back_rows(2)
    for rel in range(1, NX * NZH):
        rcopy(cst, c_in.at[rel - 1], c_send.at[0], c_recv.at[rel - 1], x=x).wait_recv()
    cols_max = jnp.maximum(cst[...], jnp.max(c_in[...], axis=0))
    nfcol_out[...] = cols_max[0:1]
    nscol_out[...] = cols_max[1:2]
    for dl in range(1, NZL):
        rcopy(mine.at[1], zl_in.at[dl - 1], zl_send.at[0], zl_recv.at[dl - 1], zl=zl).wait_recv()
    fin[k] = jnp.maximum(mine[1], jnp.max(zl_in[...], axis=0))
    copy = rcopy(fin.at[k], fin.at[k], core_send.at[1], core_recv.at[1], core=1 - k)
    copy.start()
    sends.append(copy)
    rcopy(fin.at[k], fin.at[1 - k], core_send.at[1], core_recv.at[1], core=k).wait_recv()

    for c, start, size in row_chunks():
        rows = pl.ds(start, size)
        nfr_out[0:1, start : start + size] = fin[0, c : c + 1, 0:size]
        nsr_out[0:1, start : start + size] = fin[1, c : c + 1, 0:size]
        low_first = jnp.minimum(down_rows(fin[0, c : c + 1, :])[:size], cols_max[0:1])
        low_second = jnp.minimum(down_rows(fin[1, c : c + 1, :])[:size], cols_max[1:2])
        nfc_out[rows, :] = (fnew[rows, :] / (low_first + code_eps)).astype(BF16)
        nsc_out[rows, :] = (snew[rows, :] / (low_second + code_eps)).astype(BF16)

    def drain(u, carry):
        unit = 8 * t + u
        d = lax.div(unit, UNITS)
        quarter = lax.div(unit - UNITS * d, QUART)
        home = (
            (lax.rem(d, NZH) == zh)
            & (2 * lax.div(d, NZH) + lax.div(quarter, 2) == y)
            & (lax.rem(quarter, 2) == k)
        )
        src = gt.at[pl.ds(pl.multiple_of(UNIT * u, UNIT), UNIT), :]
        for o in range(NZL):
            copy = rcopy(src, src, r_send.at[u, o], r_recv.at[0, 0], core=k)
            if o == 0:
                pl.when(jnp.logical_not(home))(copy.wait_send)
            else:
                copy.wait_send()
        return carry

    lax.fori_loop(0, 8, drain, 0)
    for copy in sends:
        copy.wait_send()
    for xo in range(NX):

        @pl.when(xo != x)
        def _():
            rcopy(dw_stage.at[xo], dw_in.at[0], dw_send.at[xo], dw_recv.at[0], x=x).wait_send()


def per_device(queries, keys, values, grad_out, weight, fc, frow, fcol, sc, srow, scol):
    shape = jax.ShapeDtypeStruct
    vmem = pl.BlockSpec(memory_space=pltpu.VMEM)
    anywhere = pl.BlockSpec(memory_space=pl.ANY)
    dma = pltpu.SemaphoreType.DMA
    outs = pl.pallas_call(
        body,
        name="whole",
        out_shape=(
            shape((SEQ, HD), BF16),
            shape((ROWS, HD), F32),
            shape((ROWS, HD), BF16),
            shape((1, ROWS), F32),
            shape((1, HD), F32),
            shape((ROWS, HD), BF16),
            shape((1, ROWS), F32),
            shape((1, HD), F32),
        ),
        in_specs=[anywhere] * 6 + [vmem, vmem, anywhere, vmem, vmem],
        out_specs=[vmem] * 8,
        scratch_shapes=[
            pltpu.VMEM((SEQ, HD), BF16),
            pltpu.VMEM((SEQ, HD), BF16),
            pltpu.VMEM((SEQ, HD), BF16),
            pltpu.VMEM((SEQ, HD), BF16),
            pltpu.VMEM((ROWS, HD), F32),
            pltpu.VMEM((ROWS, HD), BF16),
            pltpu.VMEM((ROWS, HD), BF16),
            pltpu.VMEM((HD, SEQ), BF16),
            pltpu.VMEM((NZH, NX, PADROWS, SEQ), BF16),
            pltpu.VMEM((NX, HD, ROWS), BF16),
            pltpu.VMEM((NZH, SEQ, HD), BF16),
            pltpu.VMEM((SEQ, SEQ), F32),
            pltpu.VMEM((NZH, HD, SEQ), F32),
            pltpu.VMEM((2, HD, SEQ), BF16),
            pltpu.VMEM((2, HD, SEQ), BF16),
            pltpu.VMEM((NX, ROWS, HD), F32),
            pltpu.VMEM((NX, ROWS, HD), BF16),
            pltpu.VMEM((NX - 1, ROWS, HD), BF16),
            pltpu.VMEM((ROWS, HD), F32),
            pltpu.VMEM((ROWS, HD), F32),
            pltpu.VMEM((2, 8, HD), F32),
            pltpu.VMEM((8, HD), F32),
            pltpu.VMEM((NY - 1, 8, HD), F32),
            pltpu.VMEM((NZL - 1, 8, HD), F32),
            pltpu.VMEM((2, 8, HD), F32),
            pltpu.VMEM((2, 8, HD), F32),
            pltpu.VMEM((2, HD), F32),
            pltpu.VMEM((NX * NZH - 1, 2, HD), F32),
            dma((7,)),
            dma((8, NZL)),
            dma((NZH, QUART)),
            dma((2, NZH, 4)),
            dma((2, NZH, 4)),
            dma((2, NZH, 5)),
            dma((2, NZH, 5)),
            dma((2,)),
            dma((2,)),
            dma((3,)),
            dma((3,)),
            dma((2,)),
            dma((2,)),
            dma((NX,)),
            dma((3,)),
            dma((2,)),
            dma((2,)),
            dma((NY - 1,)),
            dma((NY - 1,)),
            dma((NZL - 1,)),
            dma((NZL - 1,)),
            dma((NX * NZH - 1,)),
            dma((NX * NZH - 1,)),
        ],
        compiler_params=pltpu.CompilerParams(
            collective_id=0, has_side_effects=True, vmem_limit_bytes=48 * 1024 * 1024
        ),
    )(
        queries,
        keys,
        values,
        grad_out,
        weight,
        fc,
        frow.reshape(1, ROWS),
        fcol.reshape(1, HD),
        sc,
        srow.reshape(1, ROWS),
        scol.reshape(1, HD),
    )
    gq, nw, nfc, nfr, nfcol, nsc, nsr, nscol = outs
    return (
        gq,
        nw,
        nfc,
        nfr.reshape(ROWS),
        nfcol.reshape(HD),
        nsc,
        nsr.reshape(ROWS),
        nscol.reshape(HD),
    )


def solution(mesh):
    finer = Mesh(mesh.devices.reshape(NX, NZH, NY, NZL, NC), AXES)
    placed = (
        P(DP, TENSOR),
        P(DP, None),
        P(DP, None),
        P(DP, TENSOR),
        P(DP, TENSOR),
        P(DP, TENSOR),
        P(DP),
        P(TENSOR),
        P(DP, TENSOR),
        P(DP),
        P(TENSOR),
    )
    return jax.shard_map(
        per_device,
        mesh=finer,
        in_specs=placed,
        out_specs=(
            P(DP, TENSOR),
            P(DP, TENSOR),
            P(DP, TENSOR),
            P(DP),
            P(TENSOR),
            P(DP, TENSOR),
            P(DP),
            P(TENSOR),
        ),
        check_vma=False,
    )
```

time: 322 us -> 127 us (0.39)
  waiting for transfers between devices: 232 us -> 0 us
  Pallas kernels: 0 us -> 113 us
  blocking collectives: 18.2 us -> 0 us
  starting transfers between devices: 18 us -> 0 us
  matrix products: 14.4 us -> 0 us
  between operations: 14 us -> 0.68 us
  local copies, waits for them, and re-layouts: 17.2 us -> 12 us
  other arithmetic: 4.86 us -> 1.21 us
    all_gather x3 -> x0, waiting for transfers between devices: 126 us -> none  [the longest x2 83.8 us: stacked_from(): parts = lax.all_gather(parts, axes[k], axis=0, tiled=True)]
    pallas_call x0 -> x1, Pallas kernels: none -> 113 us  [per_device(): pl.pallas_call(body, name='whole', out_shape=(shape((SEQ, HD), BF16), sha...]
    reduce_scatter x2 -> x0, waiting for transfers between devices: 79 us -> none  [own_rows(): so_far = lax.psum_scatter(so_far, axis, scatter_dimension=0, tiled=True)]
    all_to_all x2 -> x0, waiting for transfers between devices: 26.7 us -> none  [sent_to_all(): return lax.all_to_all(copies, axis, split_axis=0, concat_axis=0, tiled=True)]
    all_gather x1 -> x0, blocking collectives: 18.2 us -> none  [stacked_from(): parts = lax.all_gather(parts, axes[k], axis=0, tiled=True)]
    all_to_all x2 -> x0, starting transfers between devices: 17.8 us -> none  [sent_to_all(): return lax.all_to_all(copies, axis, split_axis=0, concat_axis=0, tiled=True)]
    transpose x2 -> x0, local copies, waits for them, and re-layouts: 14.9 us -> none  [the longest x1 8.67 us: joined_along(): return jnp.moveaxis(parts, 0, dim).reshape(shape)]
    dot_general x5 -> x0, matrix products: 14.4 us -> none  [the longest x1 6.02 us: per_device(): jnp.einsum('sc,sh->ch', block, attended, preferred_element_type=jnp.float32)]
  transfers between devices with their start and end apart: 7 -> 0, of which waited for: 7 -> 0; matrix products, arithmetic and copies ran while one was open for 2% -> 0% of each run, Pallas kernels for 0% -> 0%
where the time goes in v1:
time: 127 us; the launch traced here: 126 us
  Pallas kernels  113 us (89%)
  local copies, waits for them, and re-layouts  12 us (9%)
    pallas_call x1, Pallas kernels, per_device(): pl.pallas_call(body, name='whole', out_shape=(shape((SEQ, HD), BF16), sha...  113 us
    unnamed x26, local copies, waits for them, and re-layouts  11.3 us

profile of v1, /device:TPU:1, one launch (start us, length us, event | category | flops | bytes accessed | tf_op | source)
XLA Modules:
  0.0 126.5 jit_solution(13931877479798349364)
XLA Ops:
  0.6 0.0 copy-start.9
  0.6 0.7 reshape.40.frow
  1.3 0.0 copy-done.9
  1.3 0.0 copy-start.7
  1.4 0.0 copy-start.8
  1.4 0.6 copy-done.7
  2.0 0.0 copy-done.8
  2.0 0.0 copy-start
  2.0 1.1 copy-done
  3.2 0.0 copy-start.1
  3.2 1.1 copy-done.1
  4.3 0.0 copy-start.2
  4.3 1.0 copy-done.2
  5.3 0.0 copy-start.3
  5.3 0.9 copy-done.3
  6.2 0.0 copy-start.4
  6.2 0.9 copy-done.4
  7.1 0.0 copy-start.5
  7.1 0.9 copy-done.5
  8.0 0.0 copy-start.6
  8.0 0.9 copy-done.6
  8.9 112.6 %whole.1 = (bf16[384,128]{1,0:T(8,128)(2,1)S(1)}, f32[688,128]{1,0:T(8,128)S(1)}, bf16[688,128]{1,0:T(8,128)(2,1)S(1)}, f32[1,688]{1,0:T(1,128)S(1)}, f32[1,128]...) custom-call(bf16[384,128]{1,0:T(8,128)(2,1)S(1)} %copy-done.5, ...), custom_call_target="tpu_custom_call" | custom-call | tf_op jit(solution)/shard_map/whole/pallas_call | solution.py:628
  121.5 0.6 reduce
  122.1 0.6 reduce.1
  122.7 0.6 copy.25
  123.4 0.7 copy.26
  124.1 0.7 copy.27
  124.8 0.5 copy.28
  125.3 0.7 copy.29
  125.9 0.5 copy.30
  (1 shorter events, 0.0 us)
Async XLA Ops:
  0.6 0.7 copy-start.9
  1.3 0.7 copy-start.7
  1.4 0.7 copy-start.8
  2.0 1.1 copy-start
  3.2 1.1 copy-start.1
  4.3 1.0 copy-start.2
  5.3 0.9 copy-start.3
  6.2 0.9 copy-start.4
  7.1 0.9 copy-start.5
  8.0 0.9 copy-start.6

commit v2 on v1

v2 whole, which is shorter than its diff:
```python
import functools

import jax
import jax.numpy as jnp
from jax import lax
from jax.experimental import pallas as pl
from jax.experimental.pallas import tpu as pltpu
from jax.sharding import Mesh
from jax.sharding import PartitionSpec as P

NX, NZH, NY, NZL, NC = 4, 3, 8, 4, 2
AXES = ("x", "zh", "y", "zl", "core")
DP = ("x", "zh")
TENSOR = ("y", "zl", "core")
MESH = pl.DeviceIdType.MESH

HD = 128
SEQ = 384
ROWS = 688
UNIT = 16
UNITS = ROWS // UNIT
ALL_UNITS = 512
QUART = 11
QROWS = QUART * UNIT
PADROWS = 4 * QROWS
HALF_ROWS = 2 * QROWS
SCALE = HD ** (-0.5)

beta_first = 0.9
beta_second = 0.95
learning = 0.01
decay_rate = 0.1
adam_eps = 1e-08
code_eps = 1e-06
correct_first = 1.0 - 0.9**10
correct_second = 1.0 - 0.95**10

F32 = jnp.float32
BF16 = jnp.bfloat16
NT = (((1,), (1,)), ((), ()))


def mod(a, n):
    return lax.rem(a + n, n)


def row_chunks():
    return [(c, 128 * c, min(128, ROWS - 128 * c)) for c in range(6)]


def lane_rows(values):
    highest = jnp.max(values, axis=1, keepdims=True)
    out = []
    for c, start, size in row_chunks():
        eye = lax.broadcasted_iota(jnp.int32, (size, 128), 0) == lax.broadcasted_iota(
            jnp.int32, (size, 128), 1
        )
        out.append(
            jnp.max(jnp.where(eye, highest[start : start + size], 0.0), axis=0, keepdims=True)
        )
    out.append(jnp.zeros((2, 128), F32))
    return jnp.concatenate(out, axis=0)


def down(vector, start, size):
    row = vector[pl.ds(start, size)].reshape(1, size)
    if size < 128:
        row = jnp.concatenate([row, jnp.zeros((1, 128 - size), F32)], axis=1)
    return down_rows(row)[:size]


def down_rows(row):
    return jnp.broadcast_to(row, (128, 128)).T


def body(
    q_hbm,
    k_hbm,
    v_hbm,
    g_hbm,
    w_hbm,
    fc_hbm,
    frow_hbm,
    fcol_hbm,
    sc_hbm,
    srow_hbm,
    scol_hbm,
    gq_out,
    nw_out,
    fnew_out,
    snew_out,
    rows_out,
    cols_out,
    q,
    kk,
    vv,
    g,
    w,
    fc,
    sc,
    frow,
    fcol,
    srow,
    scol,
    gt,
    gz,
    wt,
    att,
    prob,
    acct,
    ga_stage,
    ga_in,
    dwacc,
    dw_stage,
    dw_in,
    st,
    y_in,
    zl_in,
    mine,
    cst,
    x_in,
    zh_in,
    in_sem,
    r_send,
    r_recv,
    up_send,
    down_send,
    ring_send,
    ring_recv,
    d_send,
    d_recv,
    att_send,
    att_recv,
    w_send,
    w_recv,
    ga_send,
    ga_recv,
    dw_send,
    dw_recv,
    y_send,
    y_recv,
    zl_send,
    zl_recv,
    x_send,
    x_recv,
    zh_send,
    zh_recv,
):
    x, zh, y, zl, k = (lax.axis_index(a) for a in AXES)
    t = 8 * y + 2 * zl + k
    pair = lax.div(y, 2)

    def rcopy(src, dst, send, recv, **dev):
        return pltpu.make_async_remote_copy(
            src_ref=src, dst_ref=dst, send_sem=send, recv_sem=recv, device_id=dev, device_id_type=MESH
        )

    def slot_of(source, plane):
        return jnp.where(source == plane, 0, source + (source < plane).astype(jnp.int32))

    def other(slot):
        return slot - 1 + (slot - 1 >= zh).astype(jnp.int32)

    heads = pl.ds(pl.multiple_of(y * HD, HD), HD)
    loads = [
        pltpu.make_async_copy(src, dst, in_sem.at[i])
        for i, (src, dst) in enumerate(
            [
                (g_hbm, g),
                (q_hbm, q),
                (k_hbm.at[:, heads], kk),
                (v_hbm.at[:, heads], vv),
                (w_hbm, w),
                (fc_hbm, fc),
                (sc_hbm, sc),
                (frow_hbm, frow),
                (fcol_hbm, fcol),
                (srow_hbm, srow),
                (scol_hbm, scol),
            ]
        )
    ]
    for load in loads:
        load.start()

    barrier = pltpu.get_barrier_semaphore()

    def greet(**dev):
        pl.semaphore_signal(barrier, inc=1, device_id=dev, device_id_type=MESH)

    for dz in range(NZH):
        for dy in (0, 1, NY - 1):
            for dk in range(NC):
                if (dz, dy, dk) != (0, 0, 0):
                    greet(zh=mod(zh + dz, NZH), y=mod(y + dy, NY), core=lax.rem(k + dk, NC))
    for dl in range(1, NZL):
        greet(zl=mod(zl + dl, NZL))
        greet(zl=mod(zl + dl, NZL), core=1 - k)
    for dy in range(2, NY - 1):
        greet(y=mod(y + dy, NY))
    for dx in range(1, NX):
        greet(x=mod(x + dx, NX))
    greeted = 17 + 6 + 5 + 3

    loads[0].wait()
    gt[...] = g[...].T

    my_d = 3 * pair + zh
    my_q = 2 * lax.rem(y, 2) + k
    for i in range(QUART):
        r = QUART * my_q + i

        @pl.when((r >= UNITS) | (UNITS * my_d + r >= ALL_UNITS))
        def _():
            for jj in range(NZH):
                gz[jj, pair, pl.ds(pl.multiple_of(UNIT * r, UNIT), UNIT), :] = jnp.zeros(
                    (UNIT, SEQ), BF16
                )

    for i in (1, 2, 3):
        loads[i].wait()
    for i in range(3):
        rows, cols = pl.ds(128 * i, 128), pl.ds(0, 128 * (i + 1))
        scores = (
            lax.dot_general(q[rows, :], kk[cols, :], NT, preferred_element_type=F32) * SCALE
        )
        future = lax.broadcasted_iota(jnp.int32, scores.shape, 1) > (
            lax.broadcasted_iota(jnp.int32, scores.shape, 0) + 128 * i
        )
        scores = jnp.where(future, -1e30, scores)
        exponent = jnp.exp(scores - jnp.max(scores, axis=-1, keepdims=True))
        probabilities = exponent / jnp.sum(exponent, axis=-1, keepdims=True)
        prob[rows, cols] = probabilities
        att[0, rows, :] = jnp.dot(
            probabilities.astype(BF16), vv[cols, :], preferred_element_type=F32
        ).astype(BF16)

    loads[4].wait()
    wt[x] = w[...].astype(BF16).T

    pl.semaphore_wait(barrier, greeted)

    def unit_home(u):
        unit = 8 * t + u
        d = lax.div(unit, UNITS)
        r = unit - UNITS * d
        quarter = lax.div(r, QUART)
        zd, xd = lax.rem(d, NZH), lax.div(d, NZH)
        yd, kd = 2 * xd + lax.div(quarter, 2), lax.rem(quarter, 2)
        home = (zd == zh) & (yd == y) & (kd == k)
        return r, r - QUART * quarter, zd, xd, yd, kd, home

    def spread(u, carry):
        r, i, zd, xd, yd, kd, home = unit_home(u)
        src = gt.at[pl.ds(pl.multiple_of(UNIT * u, UNIT), UNIT), :]
        place = pl.ds(pl.multiple_of(UNIT * r, UNIT), UNIT)
        slot = slot_of(zh, zd)

        @pl.when(home)
        def _():
            gz[0, xd, place, :] = gt[pl.ds(pl.multiple_of(UNIT * u, UNIT), UNIT), :]

        @pl.when(jnp.logical_not(home))
        def _():
            rcopy(
                src, gz.at[slot, xd, place, :], r_send.at[u], r_recv.at[slot, i], zh=zd, y=yd, core=kd
            ).start()

        return carry

    lax.fori_loop(0, 8, spread, 0)

    sends = []
    def send_att():
        for slot in (1, 2):
            o = other(slot)
            there = slot_of(zh, o)
            copy = rcopy(
                att.at[0], att.at[there], att_send.at[slot - 1], att_recv.at[there - 1], zh=o
            )
            copy.start()
            sends.append(copy)

    for dx in (1, 3, 2):
        copy = rcopy(wt.at[x], wt.at[x], w_send.at[dx - 1], w_recv.at[NX - dx - 1], x=mod(x + dx, NX))
        copy.start()
        sends.append(copy)

    def chain_unit(jj, i):
        r = QUART * my_q + i
        unit = UNITS * my_d + r
        source = lax.div(unit, 8)
        from_zl = lax.rem(lax.div(source, 2), NZL)
        there = (r < UNITS) & (unit < ALL_UNITS)
        own = (source == t) & (jj == 0)
        piece = gz.at[jj, pair, pl.ds(pl.multiple_of(UNIT * r, UNIT), UNIT), :]
        up = there & (zl < NZL - 1) & (zl >= from_zl)
        down = there & (zl > 0) & (zl <= from_zl)
        up_copy = rcopy(piece, piece, up_send.at[jj, i], r_recv.at[jj, i], zl=lax.rem(zl + 1, NZL))
        down_copy = rcopy(
            piece, piece, down_send.at[jj, i], r_recv.at[jj, i], zl=lax.rem(zl + NZL - 1, NZL)
        )
        return there & jnp.logical_not(own), up, down, up_copy, down_copy

    def home_ready(jj):
        def one(i, carry):
            comes, up, down, up_copy, down_copy = chain_unit(jj, i)
            pl.when(comes)(up_copy.wait_recv)
            pl.when(up)(up_copy.start)
            pl.when(down)(down_copy.start)
            return carry

        lax.fori_loop(0, QUART, one, 0)

    HALF = 96

    def part(jj, source, r):
        quarter = 2 * lax.rem(source, 2) + k
        start, size = 0, QROWS
        if jj == 2 and r[1] == 4:
            start, size = (0, HALF) if r[0] == 0 else (HALF, QROWS - HALF)
        return gz.at[
            jj, lax.div(source, 2), pl.ds(pl.multiple_of(QROWS * quarter + start, UNIT), size), :
        ]

    def from_source(way, hops):
        return mod(y - hops, NY) if way == 0 else mod(y + hops, NY)

    def forward(way, jj, hops):
        piece = part(jj, from_source(way, hops), (way, hops + 1))
        copy = rcopy(
            piece,
            piece,
            ring_send.at[way, jj, hops],
            ring_recv.at[way, jj, hops],
            y=mod(y + 1, NY) if way == 0 else mod(y - 1, NY),
        )
        copy.start()
        sends.append(copy)

    def arrived(way, jj, hops):
        piece = part(jj, from_source(way, hops), (way, hops))
        rcopy(
            piece, piece, ring_send.at[way, jj, hops - 1], ring_recv.at[way, jj, hops - 1], y=y
        ).wait_recv()

    def to_partner(way, jj, hops):
        piece = part(jj, from_source(way, hops), (way, hops))
        copy = rcopy(piece, piece, d_send.at[way, jj, hops], d_recv.at[way, jj, hops], core=1 - k)
        copy.start()
        sends.append(copy)

    def from_partner(way, jj, hops):
        source = from_source(way, hops)
        quarter = 2 * lax.rem(source, 2) + (1 - k)
        start, size = 0, QROWS
        if jj == 2 and hops == 4:
            start, size = (0, HALF) if way == 0 else (HALF, QROWS - HALF)
        piece = gz.at[
            jj, lax.div(source, 2), pl.ds(pl.multiple_of(QROWS * quarter + start, UNIT), size), :
        ]
        rcopy(
            piece, piece, d_send.at[way, jj, hops], d_recv.at[way, jj, hops], core=1 - k
        ).wait_recv()

    reach = {(0, 0): 4, (1, 0): 3, (0, 1): 3, (1, 1): 4, (0, 2): 4, (1, 2): 4}

    def start_ring(jj):
        home_ready(jj)
        forward(0, jj, 0)
        forward(1, jj, 0)
        to_partner(0, jj, 0)

    def pass_on(jj, hops):
        for way in (0, 1):
            if hops <= reach[way, jj]:
                arrived(way, jj, hops)
                if hops < reach[way, jj]:
                    forward(way, jj, hops)
                to_partner(way, jj, hops)

    def partner_has(jj, hops):
        for way in (0, 1):
            if hops == 0 and way == 1:
                continue
            if hops <= reach[way, jj]:
                from_partner(way, jj, hops)

    def multiply(jj, xo):
        block = gz[jj, xo, 0:ROWS, :]
        term = jnp.dot(wt[xo], block, preferred_element_type=F32)
        acct[jj] = term if jj not in started else acct[jj] + term
        started.add(jj)

    def weight_term(jj, source):
        xo = lax.div(source, 2)
        rows = pl.ds(pl.multiple_of(HALF_ROWS * lax.rem(source, 2), UNIT), HALF_ROWS)
        term = jnp.dot(gz[jj, xo, rows, :], att[jj], preferred_element_type=F32)
        dwacc[xo, rows, :] = term if jj == 0 else dwacc[xo, rows, :] + term
        if jj == 2:

            @pl.when(xo != x)
            def _():
                dw_stage[xo, rows, :] = dwacc[xo, rows, :].astype(BF16)
                rel = mod(x - xo, NX) - 1
                half = lax.rem(source, 2)
                rcopy(
                    dw_stage.at[xo, rows, :],
                    dw_in.at[rel, rows, :],
                    dw_send.at[xo, half],
                    dw_recv.at[rel, half],
                    x=xo,
                ).start()

    def finish(jj, hops):
        partner_has(jj, hops)
        weight_term(jj, mod(y - hops, NY))
        if hops in (1, 2, 3):
            weight_term(jj, mod(y + hops, NY))

    started = set()

    def xo_of(off):
        return mod(pair + off, NX)

    def multiply_all(jj):
        for off in (0, 1, 3, 2):
            multiply(jj, xo_of(off))

    def send_grad(jj):
        ga_stage[jj - 1] = acct[jj].astype(BF16)
        o = other(jj)
        there = slot_of(zh, o) - 1
        copy = rcopy(
            ga_stage.at[jj - 1], ga_in.at[there], ga_send.at[jj - 1], ga_recv.at[there], zh=o
        )
        copy.start()
        sends.append(copy)

    start_ring(0)
    pass_on(0, 1)
    start_ring(1)
    send_att()
    pass_on(0, 2)
    finish(0, 0)
    pass_on(1, 1)
    finish(0, 1)
    start_ring(2)
    pass_on(0, 3)
    finish(0, 2)
    pass_on(1, 2)
    pass_on(2, 1)
    finish(0, 3)
    pass_on(0, 4)
    for dx in (1, 2, 3):
        rcopy(wt.at[0], wt.at[mod(x + dx, NX)], w_send.at[0], w_recv.at[dx - 1], x=x).wait_recv()
    pass_on(1, 3)
    finish(0, 4)
    multiply_all(0)
    pass_on(2, 2)
    for slot in (1, 2):
        rcopy(att.at[0], att.at[slot], att_send.at[0], att_recv.at[slot - 1], zh=zh).wait_recv()
    finish(1, 0)
    finish(1, 1)
    finish(1, 2)
    pass_on(1, 4)
    finish(1, 3)
    pass_on(2, 3)
    finish(1, 4)
    multiply_all(1)
    send_grad(1)
    finish(2, 0)
    finish(2, 1)
    finish(2, 2)
    finish(2, 3)
    pass_on(2, 4)
    finish(2, 4)
    multiply_all(2)
    send_grad(2)

    for load in loads[5:]:
        load.wait()
    for half in (0, 1):
        rows = pl.ds(HALF_ROWS * half, HALF_ROWS)
        for dx in (1, 2, 3):
            rcopy(
                dw_stage.at[0, rows, :],
                dw_in.at[dx - 1, rows, :],
                dw_send.at[0, half],
                dw_recv.at[dx - 1, half],
                x=x,
            ).wait_recv()
    for c, start, size in row_chunks():
        rows = pl.ds(start, size)
        grad = (
            (dwacc[x, rows, :] + dw_in[0, rows, :].astype(F32))
            + dw_in[1, rows, :].astype(F32)
            + dw_in[2, rows, :].astype(F32)
        )
        low_first = jnp.minimum(down(frow, start, size), fcol[...].reshape(1, HD))
        low_second = jnp.minimum(down(srow, start, size), scol[...].reshape(1, HD))
        first = fc[rows, :].astype(F32) * low_first
        second = sc[rows, :].astype(F32) * low_second
        first_new = beta_first * first + (1.0 - beta_first) * grad
        second_new = beta_second * second + (1.0 - beta_second) * grad * grad
        step_size = first_new / correct_first / (jnp.sqrt(second_new / correct_second) + adam_eps)
        weight = w[rows, :]
        nw_out[rows, :] = weight - learning * (step_size + decay_rate * weight)
        fnew_out[rows, :] = first_new
        snew_out[rows, :] = second_new

    first_abs, second_abs = jnp.abs(fnew_out[...]), jnp.abs(snew_out[...])
    st[0] = lane_rows(first_abs)
    st[1] = lane_rows(second_abs)
    for dy in range(1, NY):
        copy = rcopy(
            st, y_in.at[NY - dy - 1], y_send.at[dy - 1], y_recv.at[NY - dy - 1], y=mod(y + dy, NY)
        )
        copy.start()
        sends.append(copy)
    cst[0, 0:1, :] = jnp.max(first_abs, axis=0, keepdims=True)
    cst[0, 1:2, :] = jnp.max(second_abs, axis=0, keepdims=True)
    for dx in range(1, NX):
        copy = rcopy(
            cst.at[0], x_in.at[NX - dx - 1], x_send.at[dx - 1], x_recv.at[NX - dx - 1], x=mod(x + dx, NX)
        )
        copy.start()
        sends.append(copy)

    def back_rows(i):
        rows, cols = pl.ds(128 * i, 128), pl.ds(0, 128 * (i + 1))
        total = acct[0, :, rows]
        for s in range(2):
            total = total + ga_in[s, :, rows].astype(F32)
        grad_half = total.astype(BF16).T
        grad_probs = lax.dot_general(grad_half, vv[cols, :], NT, preferred_element_type=F32)
        row_dot = jnp.sum(
            grad_half.astype(F32) * att[0, rows, :].astype(F32), axis=-1, keepdims=True
        )
        grad_scores = (prob[rows, cols] * (grad_probs - row_dot)).astype(BF16)
        gq_out[rows, :] = (
            jnp.dot(grad_scores, kk[cols, :], preferred_element_type=F32) * SCALE
        ).astype(BF16)

    for s in range(2):
        rcopy(ga_stage.at[0], ga_in.at[s], ga_send.at[0], ga_recv.at[s], zh=zh).wait_recv()
    back_rows(0)
    back_rows(1)

    for dx in range(1, NX):
        rcopy(cst.at[0], x_in.at[dx - 1], x_send.at[0], x_recv.at[dx - 1], x=x).wait_recv()
    cst[1] = jnp.maximum(cst[0], jnp.max(x_in[...], axis=0))
    for slot in (1, 2):
        o = other(slot)
        there = slot_of(zh, o) - 1
        copy = rcopy(cst.at[1], zh_in.at[there], zh_send.at[slot - 1], zh_recv.at[there], zh=o)
        copy.start()
        sends.append(copy)
    for dy in range(1, NY):
        rcopy(st, y_in.at[dy - 1], y_send.at[0], y_recv.at[dy - 1], y=y).wait_recv()
    mine[...] = jnp.maximum(st[...], jnp.max(y_in[...], axis=0))
    for rel in range(1, NZL * NC):
        dl, dk = rel // NC, rel % NC
        back = NC * ((NZL - dl) % NZL) + dk - 1
        copy = rcopy(
            mine,
            zl_in.at[back],
            zl_send.at[rel - 1],
            zl_recv.at[back],
            zl=mod(zl + dl, NZL),
            core=lax.rem(k + dk, NC),
        )
        copy.start()
        sends.append(copy)
    back_rows(2)
    for slot in (1, 2):
        rcopy(cst.at[1], zh_in.at[slot - 1], zh_send.at[0], zh_recv.at[slot - 1], zh=zh).wait_recv()
    cols_out[...] = jnp.maximum(cst[1], jnp.max(zh_in[...], axis=0))
    for rel in range(1, NZL * NC):
        rcopy(mine, zl_in.at[rel - 1], zl_send.at[0], zl_recv.at[rel - 1], zl=zl).wait_recv()
    rows_out[...] = jnp.maximum(mine[...], jnp.max(zl_in[...], axis=0))

    def drain(u, carry):
        home = unit_home(u)[-1]
        src = gt.at[pl.ds(pl.multiple_of(UNIT * u, UNIT), UNIT), :]
        pl.when(jnp.logical_not(home))(rcopy(src, src, r_send.at[u], r_recv.at[0, 0], core=k).wait_send)
        return carry

    lax.fori_loop(0, 8, drain, 0)

    def drain_chain(jj):
        def one(i, carry):
            comes, up, down, up_copy, down_copy = chain_unit(jj, i)
            pl.when(up)(up_copy.wait_send)
            pl.when(down)(down_copy.wait_send)
            return carry

        lax.fori_loop(0, QUART, one, 0)

    for jj in range(NZH):
        drain_chain(jj)
    for copy in sends:
        copy.wait_send()
    for xo in range(NX):

        @pl.when(xo != x)
        def _():
            for half in (0, 1):
                rows = pl.ds(HALF_ROWS * half, HALF_ROWS)
                rcopy(
                    dw_stage.at[xo, rows, :],
                    dw_in.at[0, rows, :],
                    dw_send.at[xo, half],
                    dw_recv.at[0, half],
                    x=x,
                ).wait_send()


def codes(gq, nw, fnew, snew, rows, cols, gq_out, nw_out, nfc_out, nfr_out, nfcol_out, nsc_out, nsr_out, nscol_out):
    gq_out[...] = gq[...]
    nw_out[...] = nw[...]
    nfcol_out[...] = cols[0]
    nscol_out[...] = cols[1]
    for c, start, size in row_chunks():
        at = pl.ds(start, size)
        nfr_out[at] = rows[0, c, 0:size]
        nsr_out[at] = rows[1, c, 0:size]
        low_first = jnp.minimum(down_rows(rows[0, c : c + 1, :])[:size], cols[0:1])
        low_second = jnp.minimum(down_rows(rows[1, c : c + 1, :])[:size], cols[1:2])
        nfc_out[at, :] = (fnew[at, :] / (low_first + code_eps)).astype(BF16)
        nsc_out[at, :] = (snew[at, :] / (low_second + code_eps)).astype(BF16)


def per_device(queries, keys, values, grad_out, weight, fc, frow, fcol, sc, srow, scol):
    shape = jax.ShapeDtypeStruct
    vmem = pl.BlockSpec(memory_space=pltpu.VMEM)
    hbm = pl.BlockSpec(memory_space=pltpu.HBM)
    dma = pltpu.SemaphoreType.DMA
    gq, nw, fnew, snew, rows, cols = pl.pallas_call(
        body,
        name="whole",
        out_shape=(
            shape((SEQ, HD), BF16),
            shape((ROWS, HD), F32),
            shape((ROWS, HD), F32),
            shape((ROWS, HD), F32),
            shape((2, 8, HD), F32),
            shape((2, HD), F32),
        ),
        in_specs=[hbm] * 11,
        out_specs=[vmem] * 6,
        scratch_shapes=[
            pltpu.VMEM((SEQ, HD), BF16),
            pltpu.VMEM((SEQ, HD), BF16),
            pltpu.VMEM((SEQ, HD), BF16),
            pltpu.VMEM((SEQ, HD), BF16),
            pltpu.VMEM((ROWS, HD), F32),
            pltpu.VMEM((ROWS, HD), BF16),
            pltpu.VMEM((ROWS, HD), BF16),
            pltpu.VMEM((ROWS,), F32),
            pltpu.VMEM((HD,), F32),
            pltpu.VMEM((ROWS,), F32),
            pltpu.VMEM((HD,), F32),
            pltpu.VMEM((HD, SEQ), BF16),
            pltpu.VMEM((NZH, NX, PADROWS, SEQ), BF16),
            pltpu.VMEM((NX, HD, ROWS), BF16),
            pltpu.VMEM((NZH, SEQ, HD), BF16),
            pltpu.VMEM((SEQ, SEQ), F32),
            pltpu.VMEM((NZH, HD, SEQ), F32),
            pltpu.VMEM((2, HD, SEQ), BF16),
            pltpu.VMEM((2, HD, SEQ), BF16),
            pltpu.VMEM((NX, PADROWS, HD), F32),
            pltpu.VMEM((NX, PADROWS, HD), BF16),
            pltpu.VMEM((NX - 1, PADROWS, HD), BF16),
            pltpu.VMEM((2, 8, HD), F32),
            pltpu.VMEM((NY - 1, 2, 8, HD), F32),
            pltpu.VMEM((NZL * NC - 1, 2, 8, HD), F32),
            pltpu.VMEM((2, 8, HD), F32),
            pltpu.VMEM((2, 2, HD), F32),
            pltpu.VMEM((NX - 1, 2, HD), F32),
            pltpu.VMEM((NZH - 1, 2, HD), F32),
            dma((11,)),
            dma((8,)),
            dma((NZH, QUART)),
            dma((NZH, QUART)),
            dma((NZH, QUART)),
            dma((2, NZH, 4)),
            dma((2, NZH, 4)),
            dma((2, NZH, 5)),
            dma((2, NZH, 5)),
            dma((2,)),
            dma((2,)),
            dma((3,)),
            dma((3,)),
            dma((2,)),
            dma((2,)),
            dma((NX, 2)),
            dma((NX - 1, 2)),
            dma((NY - 1,)),
            dma((NY - 1,)),
            dma((NZL * NC - 1,)),
            dma((NZL * NC - 1,)),
            dma((NX - 1,)),
            dma((NX - 1,)),
            dma((2,)),
            dma((2,)),
        ],
        compiler_params=pltpu.CompilerParams(
            collective_id=0, has_side_effects=True, vmem_limit_bytes=48 * 1024 * 1024
        ),
    )(
        *(
            pltpu.with_memory_space_constraint(a, pltpu.HBM)
            for a in (queries, keys, values, grad_out, weight, fc, frow, fcol, sc, srow, scol)
        )
    )
    return pl.pallas_call(
        codes,
        name="codes",
        out_shape=(
            shape((SEQ, HD), BF16),
            shape((ROWS, HD), F32),
            shape((ROWS, HD), BF16),
            shape((ROWS,), F32),
            shape((HD,), F32),
            shape((ROWS, HD), BF16),
            shape((ROWS,), F32),
            shape((HD,), F32),
        ),
        compiler_params=pltpu.CompilerParams(vmem_limit_bytes=8 * 1024 * 1024),
        in_specs=[vmem] * 6,
        out_specs=[vmem] * 8,
    )(gq, nw, fnew, snew, rows, cols)


def solution(mesh):
    finer = Mesh(mesh.devices.reshape(NX, NZH, NY, NZL, NC), AXES)
    placed = (
        P(DP, TENSOR),
        P(DP, None),
        P(DP, None),
        P(DP, TENSOR),
        P(DP, TENSOR),
        P(DP, TENSOR),
        P(DP),
        P(TENSOR),
        P(DP, TENSOR),
        P(DP),
        P(TENSOR),
    )
    return jax.shard_map(
        per_device,
        mesh=finer,
        in_specs=placed,
        out_specs=(
            P(DP, TENSOR),
            P(DP, TENSOR),
            P(DP, TENSOR),
            P(DP),
            P(TENSOR),
            P(DP, TENSOR),
            P(DP),
            P(TENSOR),
        ),
        check_vma=False,
    )
```

time: 127 us -> 106 us (0.83)
  local copies, waits for them, and re-layouts: 12 us -> 0 us
  Pallas kernels: 113 us -> 104 us
    unnamed x26 -> x0, local copies, waits for them, and re-layouts: 11.3 us -> none
    pallas_call x1, Pallas kernels: 113 us -> 103 us  [per_device(): pl.pallas_call(body, name='whole', out_shape=(shape((SEQ, HD), BF16), sha...]
where the time goes in v2:
time: 106 us; the launch traced here: 105 us
  Pallas kernels  104 us (98%)
    pallas_call x1, Pallas kernels, per_device(): pl.pallas_call(body, name='whole', out_shape=(shape((SEQ, HD), BF16), sha...  103 us

profile of v2, /device:TPU:1, one launch (start us, length us, event | category | flops | bytes accessed | tf_op | source)
XLA Modules:
  0.0 105.1 jit_solution(11738206914854151200)
XLA Ops:
  0.6 103.3 %whole.1 = (bf16[384,128]{1,0:T(8,128)(2,1)S(1)}, f32[688,128]{1,0:T(8,128)S(1)}, f32[688,128]{1,0:T(8,128)S(1)}, f32[688,128]{1,0:T(8,128)S(1)}, f32[2,8,128]{2,1,0:T(8,128)S(1)}, /*index=5*/f32[2,128]{1,0:T(2,128)S(1)}) custom-call(bf16[384,128]{1,0:T(8,128)(2,1)} %q_hbm.1, bf16[384,1024]{1,0:T(8,128)(2,1)} %k_hbm.1, bf16[384,1024]{1,0:T(8,128)(2,1)} %v_hbm.1, ...), custom_call_target="tpu_custom_call" | custom-call | tf_op jit(solution)/shard_map/whole/pallas_call | solution.py:639
  104.0 1.1 %codes.1 = (bf16[384,128]{1,0:T(8,128)(2,1)}, f32[688,128]{1,0:T(8,128)}, bf16[688,128]{1,0:T(8,128)(2,1)}, f32[688]{0:T(1024)}, f32[128]{0:T(128)}, /*index=5*/...) custom-call(bf16[384,128]{1,0:T(8,128)(2,1)S(1)} %get-tuple-element.14.gq, f32[688,128]{1,0:T(8,128)S(1)} %get-tuple-element.15.nw, ...), custom_call_target="tpu_custom_call" | custom-call | tf_op jit(solution)/shard_map/codes/pallas_call | solution.py:717

commit v3 on v2

v3 whole, which is shorter than its diff:
```python
import functools

import jax
import jax.numpy as jnp
from jax import lax
from jax.experimental import pallas as pl
from jax.experimental.pallas import tpu as pltpu
from jax.sharding import Mesh
from jax.sharding import PartitionSpec as P

NX, NZH, NY, NZL, NC = 4, 3, 8, 4, 2
AXES = ("x", "zh", "y", "zl", "core")
DP = ("x", "zh")
TENSOR = ("y", "zl", "core")
MESH = pl.DeviceIdType.MESH

HD = 128
SEQ = 384
ROWS = 688
UNIT = 16
UNITS = ROWS // UNIT
ALL_UNITS = 512
QUART = 11
QROWS = QUART * UNIT
PADROWS = 4 * QROWS
HALF_ROWS = 2 * QROWS
SCALE = HD ** (-0.5)

beta_first = 0.9
beta_second = 0.95
learning = 0.01
decay_rate = 0.1
adam_eps = 1e-08
code_eps = 1e-06
correct_first = 1.0 - 0.9**10
correct_second = 1.0 - 0.95**10

F32 = jnp.float32
BF16 = jnp.bfloat16
NT = (((1,), (1,)), ((), ()))


def mod(a, n):
    return lax.rem(a + n, n)


def row_chunks():
    return [(c, 128 * c, min(128, ROWS - 128 * c)) for c in range(6)]


def lane_rows(values):
    highest = jnp.max(values, axis=1, keepdims=True)
    out = []
    for c, start, size in row_chunks():
        eye = lax.broadcasted_iota(jnp.int32, (size, 128), 0) == lax.broadcasted_iota(
            jnp.int32, (size, 128), 1
        )
        out.append(
            jnp.max(jnp.where(eye, highest[start : start + size], 0.0), axis=0, keepdims=True)
        )
    out.append(jnp.zeros((2, 128), F32))
    return jnp.concatenate(out, axis=0)


def down(vector, start, size):
    row = vector[pl.ds(start, size)].reshape(1, size)
    if size < 128:
        row = jnp.concatenate([row, jnp.zeros((1, 128 - size), F32)], axis=1)
    return down_rows(row)[:size]


def down_rows(row):
    return jnp.broadcast_to(row, (128, 128)).T


def body(
    q_hbm,
    k_hbm,
    v_hbm,
    g_hbm,
    w_hbm,
    fc_hbm,
    frow_hbm,
    fcol_hbm,
    sc_hbm,
    srow_hbm,
    scol_hbm,
    gq_out,
    nw_out,
    fnew_out,
    snew_out,
    rows_out,
    cols_out,
    q,
    kk,
    vv,
    g,
    w,
    fc,
    sc,
    frow,
    fcol,
    srow,
    scol,
    gt,
    gz,
    wt,
    att,
    prob,
    acct,
    ga_stage,
    ga_in,
    dwacc,
    dw_stage,
    dw_in,
    dwsum,
    st,
    y_in,
    zl_in,
    mine,
    cst,
    x_in,
    zh_in,
    in_sem,
    spread_send,
    up_send,
    down_send,
    relay_send,
    r_recv,
    far_recv,
    near_recv,
    ring_send,
    ring_recv,
    core_send,
    core_recv,
    att_send,
    att_recv,
    w_send,
    w_recv,
    ga_send,
    ga_recv,
    dw_send,
    dw_recv,
    y_send,
    y_recv,
    zl_send,
    zl_recv,
    x_send,
    x_recv,
    zh_send,
    zh_recv,
):
    x, zh, y, zl, k = (lax.axis_index(a) for a in AXES)
    t = 8 * y + 2 * zl + k
    pair = lax.div(y, 2)

    def rcopy(src, dst, send, recv, **dev):
        return pltpu.make_async_remote_copy(
            src_ref=src, dst_ref=dst, send_sem=send, recv_sem=recv, device_id=dev, device_id_type=MESH
        )

    def slot_of(source, plane):
        return jnp.where(source == plane, 0, source + (source < plane).astype(jnp.int32))

    def other(slot):
        return slot - 1 + (slot - 1 >= zh).astype(jnp.int32)

    heads = pl.ds(pl.multiple_of(y * HD, HD), HD)
    loads = [
        pltpu.make_async_copy(src, dst, in_sem.at[i])
        for i, (src, dst) in enumerate(
            [
                (g_hbm, g),
                (q_hbm, q),
                (k_hbm.at[:, heads], kk),
                (v_hbm.at[:, heads], vv),
                (w_hbm, w),
                (fc_hbm, fc),
                (sc_hbm, sc),
                (frow_hbm, frow),
                (fcol_hbm, fcol),
                (srow_hbm, srow),
                (scol_hbm, scol),
            ]
        )
    ]
    for load in loads:
        load.start()

    barrier = pltpu.get_barrier_semaphore()

    def greet(**dev):
        pl.semaphore_signal(barrier, inc=1, device_id=dev, device_id_type=MESH)

    across = lax.rem(zl + 2, NZL)
    for dz in (1, 2, 0):
        for dy in (0, 1, NY - 1):
            for dk in range(NC):
                there = dict(zh=mod(zh + dz, NZH), y=mod(y + dy, NY), core=lax.rem(k + dk, NC))
                greet(zl=across, **there)
                if (dz, dy, dk) != (0, 0, 0):
                    greet(**there)
    for dl in (1, 3):
        for dk in range(NC):
            greet(zl=mod(zl + dl, NZL), core=lax.rem(k + dk, NC))
    for dy in range(2, NY - 1):
        greet(y=mod(y + dy, NY))
    for dx in range(1, NX):
        greet(x=mod(x + dx, NX))
    greeted = 35 + 4 + 5 + 3

    loads[0].wait()
    gt[...] = g[...].T

    my_d = 3 * pair + zh
    my_q = 2 * lax.rem(y, 2) + k
    my_piece = 4 * pair + my_q

    def unit_of(i):
        r = QUART * my_q + i
        unit = UNITS * my_d + r
        return lax.div(unit, 8), lax.rem(unit, 8), (r < UNITS) & (unit < ALL_UNITS)

    def rows_of(i):
        return pl.ds(pl.multiple_of(UNIT * i, UNIT), UNIT)

    for i in range(QUART):

        @pl.when(jnp.logical_not(unit_of(i)[2]))
        def _():
            for jj in range(NZH):
                gz[jj, my_piece, rows_of(i), :] = jnp.zeros((UNIT, SEQ), BF16)

    pl.semaphore_wait(barrier, greeted)

    def unit_home(u):
        unit = 8 * t + u
        d = lax.div(unit, UNITS)
        r = unit - UNITS * d
        quarter = lax.div(r, QUART)
        zd, xd = lax.rem(d, NZH), lax.div(d, NZH)
        yd, kd = 2 * xd + lax.div(quarter, 2), lax.rem(quarter, 2)
        home = (zd == zh) & (yd == y) & (kd == k)
        return r - QUART * quarter, 4 * xd + quarter, zd, yd, kd, home

    def spread(u, stayed):
        i, piece, zd, yd, kd, home = unit_home(u)
        src = gt.at[rows_of(u), :]
        slot = slot_of(zh, zd)

        @pl.when(home)
        def _():
            gz[0, piece, rows_of(i), :] = gt[rows_of(u), :]

        @pl.when((zd == zh) & jnp.logical_not(home))
        def _():
            rcopy(src, gz.at[0, piece, rows_of(i), :], spread_send, r_recv.at[i], y=yd, core=kd).start()

        @pl.when(zd != zh)
        def _():
            rcopy(
                src,
                gz.at[slot, piece, rows_of(i), :],
                spread_send,
                far_recv.at[slot - 1],
                zh=zd,
                y=yd,
                zl=lax.rem(zl + 2 * lax.rem(u, 2), NZL),
                core=kd,
            ).start()

        return stayed + home.astype(jnp.int32)

    stayed = lax.fori_loop(0, 8, spread, jnp.int32(0))

    loads[4].wait()
    wt[x] = w[...].astype(BF16).T

    for dx in (1, 3, 2):
        rcopy(wt.at[x], wt.at[x], w_send, w_recv, x=mod(x + dx, NX)).start()

    for i in (1, 2, 3):
        loads[i].wait()
    for i in range(3):
        rows, cols = pl.ds(128 * i, 128), pl.ds(0, 128 * (i + 1))
        scores = (
            lax.dot_general(q[rows, :], kk[cols, :], NT, preferred_element_type=F32) * SCALE
        )
        future = lax.broadcasted_iota(jnp.int32, scores.shape, 1) > (
            lax.broadcasted_iota(jnp.int32, scores.shape, 0) + 128 * i
        )
        scores = jnp.where(future, -1e30, scores)
        exponent = jnp.exp(scores - jnp.max(scores, axis=-1, keepdims=True))
        probabilities = exponent / jnp.sum(exponent, axis=-1, keepdims=True)
        prob[rows, cols] = probabilities
        att[0, rows, :] = jnp.dot(
            probabilities.astype(BF16), vv[cols, :], preferred_element_type=F32
        ).astype(BF16)

    def send_att():
        for slot in (1, 2):
            o = other(slot)
            there = slot_of(zh, o)
            rcopy(att.at[0], att.at[there], att_send, att_recv.at[there - 1], zh=o).start()

    def wait_units(n, most, wait):
        for c in range(1, most + 1):
            pl.when(n == c)(functools.partial(wait, c))

    def chain_unit(i):
        source, u, there = unit_of(i)
        from_zl = lax.rem(lax.div(source, 2), NZL)
        piece = gz.at[0, my_piece, rows_of(i), :]
        up = there & (zl < NZL - 1) & (zl >= from_zl)
        down = there & (zl > 0) & (zl <= from_zl)
        up_copy = rcopy(piece, piece, up_send, r_recv.at[i], zl=lax.rem(zl + 1, NZL))
        down_copy = rcopy(piece, piece, down_send, r_recv.at[i], zl=lax.rem(zl + NZL - 1, NZL))
        return there & (source != t), up, down, up_copy, down_copy

    def chain(i, counts):
        comes, up, down, up_copy, down_copy = chain_unit(i)
        pl.when(comes)(up_copy.wait_recv)
        pl.when(up)(up_copy.start)
        pl.when(down)(down_copy.start)
        return counts[0] + up.astype(jnp.int32), counts[1] + down.astype(jnp.int32)

    def lands_here(i):
        source, u, there = unit_of(i)
        from_zl = lax.rem(lax.div(source, 2), NZL)
        here = lax.rem(from_zl + 2 * lax.rem(u, 2), NZL) == zl
        return there & here, there & jnp.logical_not(here)

    landing = sum(lands_here(i)[0].astype(jnp.int32) for i in range(QUART))
    coming = sum(lands_here(i)[1].astype(jnp.int32) for i in range(QUART))

    def units_came(sem, c):
        piece = gz.at[0, 0, 0 : UNIT * c, :]
        rcopy(piece, piece, spread_send, sem, zl=zl).wait_recv()

    def relay(jj):
        wait_units(landing, 6, functools.partial(units_came, far_recv.at[jj - 1]))

        def give(i, carry):
            piece = gz.at[jj, my_piece, rows_of(i), :]

            @pl.when(lands_here(i)[0])
            def _():
                for dl in (1, 3, 2):
                    rcopy(
                        piece, piece, relay_send, near_recv.at[jj - 1], zl=mod(zl + dl, NZL)
                    ).start()

            return carry

        lax.fori_loop(0, QUART, give, 0)

    HALF = 96

    def part(jj, source, core, way, hops):
        start, size = 0, QROWS
        if jj == 2 and hops == 4:
            start, size = (0, HALF) if way == 0 else (HALF, QROWS - HALF)
        return gz.at[jj, 2 * source + core, pl.ds(start, size), :]

    def from_source(way, hops):
        return mod(y - hops, NY) if way == 0 else mod(y + hops, NY)

    def forward(way, jj, hops):
        piece = part(jj, from_source(way, hops), k, way, hops + 1)
        rcopy(
            piece,
            piece,
            ring_send,
            ring_recv.at[way, jj, hops],
            y=mod(y + 1, NY) if way == 0 else mod(y - 1, NY),
        ).start()

    def arrived(way, jj, hops):
        piece = part(jj, from_source(way, hops), k, way, hops)
        rcopy(piece, piece, ring_send, ring_recv.at[way, jj, hops - 1], y=y).wait_recv()

    def to_partner(way, jj, hops):
        piece = part(jj, from_source(way, hops), k, way, hops)
        rcopy(piece, piece, core_send, core_recv.at[jj, hops], core=1 - k).start()

    def partner_has(jj, hops):
        pieces = gz.at[0, 0 : 2 if hops in (1, 2, 3) else 1]
        rcopy(pieces, pieces, core_send, core_recv.at[jj, hops], core=k).wait_recv()

    reach = {(0, 0): 4, (1, 0): 3, (0, 1): 3, (1, 1): 4, (0, 2): 4, (1, 2): 4}

    def start_ring(jj):
        if jj > 0:
            wait_units(coming, QUART, functools.partial(units_came, near_recv.at[jj - 1]))
        forward(0, jj, 0)
        forward(1, jj, 0)
        to_partner(0, jj, 0)

    def pass_on(jj, hops):
        for way in (0, 1):
            if hops <= reach[way, jj]:
                arrived(way, jj, hops)
                if hops < reach[way, jj]:
                    forward(way, jj, hops)
                to_partner(way, jj, hops)

    def multiply(jj, xo):
        block = gz[jj, pl.ds(4 * xo, 4)].reshape(PADROWS, SEQ)[:ROWS]
        term = jnp.dot(wt[xo], block, preferred_element_type=F32)
        acct[jj] = term if jj not in started else acct[jj] + term
        started.add(jj)

    def weight_term(jj, source):
        block = gz[jj, pl.ds(2 * source, 2)].reshape(HALF_ROWS, SEQ)
        term = jnp.dot(block, att[jj], preferred_element_type=F32)
        dwacc[source] = term if jj == 0 else dwacc[source] + term
        if jj == 2:
            xo, half = lax.div(source, 2), lax.rem(source, 2)

            @pl.when(xo != x)
            def _():
                dw_stage[source] = dwacc[source].astype(BF16)
                rel = mod(x - xo, NX) - 1
                rcopy(
                    dw_stage.at[source], dw_in.at[rel, half], dw_send, dw_recv.at[half], x=xo
                ).start()

    def finish(jj, hops):
        partner_has(jj, hops)
        weight_term(jj, mod(y - hops, NY))
        if hops in (1, 2, 3):
            weight_term(jj, mod(y + hops, NY))

    started = set()

    def xo_of(off):
        return mod(pair + off, NX)

    def multiply_all(jj):
        for off in (0, 1, 3, 2):
            multiply(jj, xo_of(off))

    def send_grad(jj):
        ga_stage[jj - 1] = acct[jj].astype(BF16)
        o = other(jj)
        rcopy(ga_stage.at[jj - 1], ga_in.at[slot_of(zh, o) - 1], ga_send, ga_recv, zh=o).start()

    ups, downs = lax.fori_loop(0, QUART, chain, (jnp.int32(0), jnp.int32(0)))
    start_ring(0)
    relay(1)
    relay(2)
    pass_on(0, 1)
    send_att()
    start_ring(1)
    pass_on(0, 2)
    finish(0, 0)
    pass_on(1, 1)
    finish(0, 1)
    start_ring(2)
    pass_on(0, 3)
    finish(0, 2)
    pass_on(1, 2)
    pass_on(2, 1)
    finish(0, 3)
    pass_on(0, 4)
    rcopy(wt.at[0:3], wt.at[0:3], w_send, w_recv, x=x).wait_recv()
    pass_on(1, 3)
    finish(0, 4)
    multiply_all(0)
    pass_on(2, 2)
    for slot in (1, 2):
        rcopy(att.at[0], att.at[slot], att_send, att_recv.at[slot - 1], zh=zh).wait_recv()
    finish(1, 0)
    finish(1, 1)
    finish(1, 2)
    pass_on(1, 4)
    finish(1, 3)
    pass_on(2, 3)
    finish(1, 4)
    multiply_all(1)
    send_grad(1)
    finish(2, 0)
    finish(2, 1)
    finish(2, 2)
    finish(2, 3)
    pass_on(2, 4)
    finish(2, 4)
    multiply_all(2)
    send_grad(2)

    for load in loads[5:]:
        load.wait()
    for half in (0, 1):
        piece = dw_in.at[:, half]
        rcopy(piece, piece, dw_send, dw_recv.at[half], x=x).wait_recv()
    for half in (0, 1):
        total = dwacc[2 * x + half]
        for rel in range(NX - 1):
            total = total + dw_in[rel, half].astype(F32)
        dwsum[pl.ds(HALF_ROWS * half, HALF_ROWS), :] = total
    for c, start, size in row_chunks():
        rows = pl.ds(start, size)
        grad = dwsum[rows, :]
        low_first = jnp.minimum(down(frow, start, size), fcol[...].reshape(1, HD))
        low_second = jnp.minimum(down(srow, start, size), scol[...].reshape(1, HD))
        first = fc[rows, :].astype(F32) * low_first
        second = sc[rows, :].astype(F32) * low_second
        first_new = beta_first * first + (1.0 - beta_first) * grad
        second_new = beta_second * second + (1.0 - beta_second) * grad * grad
        step_size = first_new / correct_first / (jnp.sqrt(second_new / correct_second) + adam_eps)
        weight = w[rows, :]
        nw_out[rows, :] = weight - learning * (step_size + decay_rate * weight)
        fnew_out[rows, :] = first_new
        snew_out[rows, :] = second_new

    first_abs, second_abs = jnp.abs(fnew_out[...]), jnp.abs(snew_out[...])
    st[0] = lane_rows(first_abs)
    st[1] = lane_rows(second_abs)
    for dy in range(1, NY):
        rcopy(st, y_in.at[NY - dy - 1], y_send, y_recv, y=mod(y + dy, NY)).start()
    cst[0, 0:1, :] = jnp.max(first_abs, axis=0, keepdims=True)
    cst[0, 1:2, :] = jnp.max(second_abs, axis=0, keepdims=True)
    for dx in range(1, NX):
        rcopy(cst.at[0], x_in.at[NX - dx - 1], x_send, x_recv, x=mod(x + dx, NX)).start()

    def back_rows(i):
        rows, cols = pl.ds(128 * i, 128), pl.ds(0, 128 * (i + 1))
        total = acct[0, :, rows]
        for s in range(2):
            total = total + ga_in[s, :, rows].astype(F32)
        grad_half = total.astype(BF16).T
        grad_probs = lax.dot_general(grad_half, vv[cols, :], NT, preferred_element_type=F32)
        row_dot = jnp.sum(
            grad_half.astype(F32) * att[0, rows, :].astype(F32), axis=-1, keepdims=True
        )
        grad_scores = (prob[rows, cols] * (grad_probs - row_dot)).astype(BF16)
        gq_out[rows, :] = (
            jnp.dot(grad_scores, kk[cols, :], preferred_element_type=F32) * SCALE
        ).astype(BF16)

    rcopy(ga_in, ga_in, ga_send, ga_recv, zh=zh).wait_recv()
    back_rows(0)
    back_rows(1)

    rcopy(x_in, x_in, x_send, x_recv, x=x).wait_recv()
    cst[1] = jnp.maximum(cst[0], jnp.max(x_in[...], axis=0))
    for slot in (1, 2):
        o = other(slot)
        rcopy(cst.at[1], zh_in.at[slot_of(zh, o) - 1], zh_send, zh_recv, zh=o).start()
    rcopy(y_in, y_in, y_send, y_recv, y=y).wait_recv()
    mine[...] = jnp.maximum(st[...], jnp.max(y_in[...], axis=0))
    for rel in range(1, NZL * NC):
        dl, dk = rel // NC, rel % NC
        back = NC * ((NZL - dl) % NZL) + dk - 1
        rcopy(
            mine, zl_in.at[back], zl_send, zl_recv, zl=mod(zl + dl, NZL), core=lax.rem(k + dk, NC)
        ).start()
    back_rows(2)
    rcopy(zh_in, zh_in, zh_send, zh_recv, zh=zh).wait_recv()
    cols_out[...] = jnp.maximum(cst[1], jnp.max(zh_in[...], axis=0))
    rcopy(zl_in, zl_in, zl_send, zl_recv, zl=zl).wait_recv()
    rows_out[...] = jnp.maximum(mine[...], jnp.max(zl_in[...], axis=0))

    def units_left(sem, each, c):
        pieces = gz.at[0, 0:c, 0 : UNIT * each, :]
        rcopy(pieces, pieces, sem, r_recv.at[0], zl=zl).wait_send()

    wait_units(8 - stayed, 8, functools.partial(units_left, spread_send, 1))
    wait_units(ups, QUART, functools.partial(units_left, up_send, 1))
    wait_units(downs, QUART, functools.partial(units_left, down_send, 1))
    wait_units(landing, 6, functools.partial(units_left, relay_send, 6))
    for whole, sem in (
        (gz.at[:, 0:7], ring_send),
        (gz.at[:, 0:8], core_send),
        (att.at[0:2], att_send),
        (wt.at[0:3], w_send),
        (ga_in, ga_send),
        (dw_in, dw_send),
        (y_in, y_send),
        (zl_in, zl_send),
        (x_in, x_send),
        (zh_in, zh_send),
    ):
        rcopy(whole, whole, sem, r_recv.at[0], zl=zl).wait_send()


def codes(gq, nw, fnew, snew, rows, cols, gq_out, nw_out, nfc_out, nfr_out, nfcol_out, nsc_out, nsr_out, nscol_out):
    gq_out[...] = gq[...]
    nw_out[...] = nw[...]
    nfcol_out[...] = cols[0]
    nscol_out[...] = cols[1]
    for c, start, size in row_chunks():
        at = pl.ds(start, size)
        nfr_out[at] = rows[0, c, 0:size]
        nsr_out[at] = rows[1, c, 0:size]
        low_first = jnp.minimum(down_rows(rows[0, c : c + 1, :])[:size], cols[0:1])
        low_second = jnp.minimum(down_rows(rows[1, c : c + 1, :])[:size], cols[1:2])
        nfc_out[at, :] = (fnew[at, :] / (low_first + code_eps)).astype(BF16)
        nsc_out[at, :] = (snew[at, :] / (low_second + code_eps)).astype(BF16)


def per_device(queries, keys, values, grad_out, weight, fc, frow, fcol, sc, srow, scol):
    shape = jax.ShapeDtypeStruct
    vmem = pl.BlockSpec(memory_space=pltpu.VMEM)
    hbm = pl.BlockSpec(memory_space=pltpu.HBM)
    dma = pltpu.SemaphoreType.DMA
    gq, nw, fnew, snew, rows, cols = pl.pallas_call(
        body,
        name="whole",
        out_shape=(
            shape((SEQ, HD), BF16),
            shape((ROWS, HD), F32),
            shape((ROWS, HD), F32),
            shape((ROWS, HD), F32),
            shape((2, 8, HD), F32),
            shape((2, HD), F32),
        ),
        in_specs=[hbm] * 11,
        out_specs=[vmem] * 6,
        scratch_shapes=[
            pltpu.VMEM((SEQ, HD), BF16),
            pltpu.VMEM((SEQ, HD), BF16),
            pltpu.VMEM((SEQ, HD), BF16),
            pltpu.VMEM((SEQ, HD), BF16),
            pltpu.VMEM((ROWS, HD), F32),
            pltpu.VMEM((ROWS, HD), BF16),
            pltpu.VMEM((ROWS, HD), BF16),
            pltpu.VMEM((ROWS,), F32),
            pltpu.VMEM((HD,), F32),
            pltpu.VMEM((ROWS,), F32),
            pltpu.VMEM((HD,), F32),
            pltpu.VMEM((HD, SEQ), BF16),
            pltpu.VMEM((NZH, 4 * NX, QROWS, SEQ), BF16),
            pltpu.VMEM((NX, HD, ROWS), BF16),
            pltpu.VMEM((NZH, SEQ, HD), BF16),
            pltpu.VMEM((SEQ, SEQ), F32),
            pltpu.VMEM((NZH, HD, SEQ), F32),
            pltpu.VMEM((2, HD, SEQ), BF16),
            pltpu.VMEM((2, HD, SEQ), BF16),
            pltpu.VMEM((2 * NX, HALF_ROWS, HD), F32),
            pltpu.VMEM((2 * NX, HALF_ROWS, HD), BF16),
            pltpu.VMEM((NX - 1, 2, HALF_ROWS, HD), BF16),
            pltpu.VMEM((PADROWS, HD), F32),
            pltpu.VMEM((2, 8, HD), F32),
            pltpu.VMEM((NY - 1, 2, 8, HD), F32),
            pltpu.VMEM((NZL * NC - 1, 2, 8, HD), F32),
            pltpu.VMEM((2, 8, HD), F32),
            pltpu.VMEM((2, 2, HD), F32),
            pltpu.VMEM((NX - 1, 2, HD), F32),
            pltpu.VMEM((NZH - 1, 2, HD), F32),
            dma((11,)),
            dma,
            dma,
            dma,
            dma,
            dma((QUART,)),
            dma((2,)),
            dma((2,)),
            dma,
            dma((2, NZH, 4)),
            dma,
            dma((NZH, 5)),
            dma,
            dma((2,)),
            dma,
            dma,
            dma,
            dma,
            dma,
            dma((2,)),
            dma,
            dma,
            dma,
            dma,
            dma,
            dma,
            dma,
            dma,
        ],
        compiler_params=pltpu.CompilerParams(
            collective_id=0, has_side_effects=True, vmem_limit_bytes=48 * 1024 * 1024
        ),
    )(
        *(
            pltpu.with_memory_space_constraint(a, pltpu.HBM)
            for a in (queries, keys, values, grad_out, weight, fc, frow, fcol, sc, srow, scol)
        )
    )
    return pl.pallas_call(
        codes,
        name="codes",
        out_shape=(
            shape((SEQ, HD), BF16),
            shape((ROWS, HD), F32),
            shape((ROWS, HD), BF16),
            shape((ROWS,), F32),
            shape((HD,), F32),
            shape((ROWS, HD), BF16),
            shape((ROWS,), F32),
            shape((HD,), F32),
        ),
        compiler_params=pltpu.CompilerParams(vmem_limit_bytes=8 * 1024 * 1024),
        in_specs=[vmem] * 6,
        out_specs=[vmem] * 8,
    )(gq, nw, fnew, snew, rows, cols)


def solution(mesh):
    finer = Mesh(mesh.devices.reshape(NX, NZH, NY, NZL, NC), AXES)
    placed = (
        P(DP, TENSOR),
        P(DP, None),
        P(DP, None),
        P(DP, TENSOR),
        P(DP, TENSOR),
        P(DP, TENSOR),
        P(DP),
        P(TENSOR),
        P(DP, TENSOR),
        P(DP),
        P(TENSOR),
    )
    return jax.shard_map(
        per_device,
        mesh=finer,
        in_specs=placed,
        out_specs=(
            P(DP, TENSOR),
            P(DP, TENSOR),
            P(DP, TENSOR),
            P(DP),
            P(TENSOR),
            P(DP, TENSOR),
            P(DP),
            P(TENSOR),
        ),
        check_vma=False,
    )
```

time: 106 us -> 94.6 us (0.89)
  Pallas kernels: 104 us -> 93.8 us
    pallas_call x1, Pallas kernels: 103 us -> 92.7 us  [per_device(): pl.pallas_call(body, name='whole', out_shape=(shape((SEQ, HD), BF16), sha...]
where the time goes in v3:
time: 94.6 us; the launch traced here: 94.4 us
  Pallas kernels  93.8 us (99%)
    pallas_call x1, Pallas kernels, per_device(): pl.pallas_call(body, name='whole', out_shape=(shape((SEQ, HD), BF16), sha...  92.7 us

profile of v3, /device:TPU:1, one launch (start us, length us, event | category | flops | bytes accessed | tf_op | source)
XLA Modules:
  0.0 94.4 jit_solution(420578162099038849)
XLA Ops:
  0.6 92.7 %whole.1 = (bf16[384,128]{1,0:T(8,128)(2,1)S(1)}, f32[688,128]{1,0:T(8,128)S(1)}, f32[688,128]{1,0:T(8,128)S(1)}, f32[688,128]{1,0:T(8,128)S(1)}, f32[2,8,128]{2,1,0:T(8,128)S(1)}, /*index=5*/f32[2,128]{1,0:T(2,128)S(1)}) custom-call(bf16[384,128]{1,0:T(8,128)(2,1)} %q_hbm.1, bf16[384,1024]{1,0:T(8,128)(2,1)} %k_hbm.1, bf16[384,1024]{1,0:T(8,128)(2,1)} %v_hbm.1, ...), custom_call_target="tpu_custom_call" | custom-call | tf_op jit(solution)/shard_map/whole/pallas_call | solution.py:607
  93.3 1.1 %codes.1 = (bf16[384,128]{1,0:T(8,128)(2,1)}, f32[688,128]{1,0:T(8,128)}, bf16[688,128]{1,0:T(8,128)(2,1)}, f32[688]{0:T(1024)}, f32[128]{0:T(128)}, /*index=5*/...) custom-call(bf16[384,128]{1,0:T(8,128)(2,1)S(1)} %get-tuple-element.14.gq, f32[688,128]{1,0:T(8,128)S(1)} %get-tuple-element.15.nw, ...), custom_call_target="tpu_custom_call" | custom-call | tf_op jit(solution)/shard_map/codes/pallas_call | solution.py:689

commit v4 on v3

--- a/solution.py
+++ b/solution.py
@@ -123,10 +123,7 @@
     zh_in,
     in_sem,
     spread_send,
-    up_send,
-    down_send,
     relay_send,
-    r_recv,
     far_recv,
     near_recv,
     ring_send,
@@ -240,38 +237,35 @@
         quarter = lax.div(r, QUART)
         zd, xd = lax.rem(d, NZH), lax.div(d, NZH)
         yd, kd = 2 * xd + lax.div(quarter, 2), lax.rem(quarter, 2)
-        home = (zd == zh) & (yd == y) & (kd == k)
-        return r - QUART * quarter, 4 * xd + quarter, zd, yd, kd, home
-
-    def spread(u, stayed):
-        i, piece, zd, yd, kd, home = unit_home(u)
-        src = gt.at[rows_of(u), :]
+        zld = lax.rem(zl + 2 * lax.rem(u, 2), NZL)
+        home = (zd == zh) & (yd == y) & (kd == k) & (zld == zl)
+        return r - QUART * quarter, 4 * xd + quarter, zd, yd, zld, kd, home
+
+    def spread(wanted, u, stayed):
+        i, piece, zd, yd, zld, kd, home = unit_home(u)
         slot = slot_of(zh, zd)
 
-        @pl.when(home)
+        @pl.when(wanted(zd) & home)
         def _():
             gz[0, piece, rows_of(i), :] = gt[rows_of(u), :]
 
-        @pl.when((zd == zh) & jnp.logical_not(home))
-        def _():
-            rcopy(src, gz.at[0, piece, rows_of(i), :], spread_send, r_recv.at[i], y=yd, core=kd).start()
-
-        @pl.when(zd != zh)
+        @pl.when(wanted(zd) & jnp.logical_not(home))
         def _():
             rcopy(
-                src,
+                gt.at[rows_of(u), :],
                 gz.at[slot, piece, rows_of(i), :],
                 spread_send,
-                far_recv.at[slot - 1],
+                far_recv.at[slot],
                 zh=zd,
                 y=yd,
-                zl=lax.rem(zl + 2 * lax.rem(u, 2), NZL),
+                zl=zld,
                 core=kd,
             ).start()
 
         return stayed + home.astype(jnp.int32)
 
-    stayed = lax.fori_loop(0, 8, spread, jnp.int32(0))
+    stayed = lax.fori_loop(0, 8, functools.partial(spread, lambda zd: zd == zh), jnp.int32(0))
+    lax.fori_loop(0, 8, functools.partial(spread, lambda zd: zd > zh), jnp.int32(0))
 
     loads[4].wait()
     wt[x] = w[...].astype(BF16).T
@@ -307,23 +301,6 @@
         for c in range(1, most + 1):
             pl.when(n == c)(functools.partial(wait, c))
 
-    def chain_unit(i):
-        source, u, there = unit_of(i)
-        from_zl = lax.rem(lax.div(source, 2), NZL)
-        piece = gz.at[0, my_piece, rows_of(i), :]
-        up = there & (zl < NZL - 1) & (zl >= from_zl)
-        down = there & (zl > 0) & (zl <= from_zl)
-        up_copy = rcopy(piece, piece, up_send, r_recv.at[i], zl=lax.rem(zl + 1, NZL))
-        down_copy = rcopy(piece, piece, down_send, r_recv.at[i], zl=lax.rem(zl + NZL - 1, NZL))
-        return there & (source != t), up, down, up_copy, down_copy
-
-    def chain(i, counts):
-        comes, up, down, up_copy, down_copy = chain_unit(i)
-        pl.when(comes)(up_copy.wait_recv)
-        pl.when(up)(up_copy.start)
-        pl.when(down)(down_copy.start)
-        return counts[0] + up.astype(jnp.int32), counts[1] + down.astype(jnp.int32)
-
     def lands_here(i):
         source, u, there = unit_of(i)
         from_zl = lax.rem(lax.div(source, 2), NZL)
@@ -338,7 +315,9 @@
         rcopy(piece, piece, spread_send, sem, zl=zl).wait_recv()
 
     def relay(jj):
-        wait_units(landing, 6, functools.partial(units_came, far_recv.at[jj - 1]))
+        wait_units(
+            landing - stayed if jj == 0 else landing, 6, functools.partial(units_came, far_recv.at[jj])
+        )
 
         def give(i, carry):
             piece = gz.at[jj, my_piece, rows_of(i), :]
@@ -346,9 +325,7 @@
             @pl.when(lands_here(i)[0])
             def _():
                 for dl in (1, 3, 2):
-                    rcopy(
-                        piece, piece, relay_send, near_recv.at[jj - 1], zl=mod(zl + dl, NZL)
-                    ).start()
+                    rcopy(piece, piece, relay_send, near_recv.at[jj], zl=mod(zl + dl, NZL)).start()
 
             return carry
 
@@ -358,7 +335,7 @@
 
     def part(jj, source, core, way, hops):
         start, size = 0, QROWS
-        if jj == 2 and hops == 4:
+        if jj == 0 and hops == 4:
             start, size = (0, HALF) if way == 0 else (HALF, QROWS - HALF)
         return gz.at[jj, 2 * source + core, pl.ds(start, size), :]
 
@@ -387,11 +364,10 @@
         pieces = gz.at[0, 0 : 2 if hops in (1, 2, 3) else 1]
         rcopy(pieces, pieces, core_send, core_recv.at[jj, hops], core=k).wait_recv()
 
-    reach = {(0, 0): 4, (1, 0): 3, (0, 1): 3, (1, 1): 4, (0, 2): 4, (1, 2): 4}
+    reach = {(0, 0): 4, (1, 0): 4, (0, 1): 4, (1, 1): 3, (0, 2): 3, (1, 2): 4}
 
     def start_ring(jj):
-        if jj > 0:
-            wait_units(coming, QUART, functools.partial(units_came, near_recv.at[jj - 1]))
+        wait_units(coming, QUART, functools.partial(units_came, near_recv.at[jj]))
         forward(0, jj, 0)
         forward(1, jj, 0)
         to_partner(0, jj, 0)
@@ -410,11 +386,11 @@
         acct[jj] = term if jj not in started else acct[jj] + term
         started.add(jj)
 
-    def weight_term(jj, source):
+    def weight_term(jj, source, first, last):
         block = gz[jj, pl.ds(2 * source, 2)].reshape(HALF_ROWS, SEQ)
         term = jnp.dot(block, att[jj], preferred_element_type=F32)
-        dwacc[source] = term if jj == 0 else dwacc[source] + term
-        if jj == 2:
+        dwacc[source] = term if first else dwacc[source] + term
+        if last:
             xo, half = lax.div(source, 2), lax.rem(source, 2)
 
             @pl.when(xo != x)
@@ -427,10 +403,11 @@
 
     def finish(jj, hops):
         partner_has(jj, hops)
-        weight_term(jj, mod(y - hops, NY))
-        if hops in (1, 2, 3):
-            weight_term(jj, mod(y + hops, NY))
-
+        done[hops] += 1
+        for way in (0, 1) if hops in (1, 2, 3) else (0,):
+            weight_term(jj, from_source(way, hops), done[hops] == 1, done[hops] == NZH)
+
+    done = [0] * 5
     started = set()
 
     def xo_of(off):
@@ -445,11 +422,12 @@
         o = other(jj)
         rcopy(ga_stage.at[jj - 1], ga_in.at[slot_of(zh, o) - 1], ga_send, ga_recv, zh=o).start()
 
-    ups, downs = lax.fori_loop(0, QUART, chain, (jnp.int32(0), jnp.int32(0)))
+    relay(0)
+    lax.fori_loop(0, 8, functools.partial(spread, lambda zd: zd < zh), jnp.int32(0))
     start_ring(0)
     relay(1)
+    pass_on(0, 1)
     relay(2)
-    pass_on(0, 1)
     send_att()
     start_ring(1)
     pass_on(0, 2)
@@ -457,36 +435,38 @@
     pass_on(1, 1)
     finish(0, 1)
     start_ring(2)
-    pass_on(0, 3)
     finish(0, 2)
     pass_on(1, 2)
     pass_on(2, 1)
-    finish(0, 3)
-    pass_on(0, 4)
-    rcopy(wt.at[0:3], wt.at[0:3], w_send, w_recv, x=x).wait_recv()
-    pass_on(1, 3)
-    finish(0, 4)
-    multiply_all(0)
-    pass_on(2, 2)
-    for slot in (1, 2):
-        rcopy(att.at[0], att.at[slot], att_send, att_recv.at[slot - 1], zh=zh).wait_recv()
+    rcopy(att.at[0], att.at[1], att_send, att_recv.at[0], zh=zh).wait_recv()
     finish(1, 0)
     finish(1, 1)
+    pass_on(1, 3)
     finish(1, 2)
+    pass_on(2, 2)
+    rcopy(att.at[0], att.at[2], att_send, att_recv.at[1], zh=zh).wait_recv()
+    finish(2, 0)
+    finish(2, 1)
     pass_on(1, 4)
+    rcopy(wt.at[0:3], wt.at[0:3], w_send, w_recv, x=x).wait_recv()
     finish(1, 3)
     pass_on(2, 3)
+    finish(2, 2)
+    pass_on(0, 3)
     finish(1, 4)
     multiply_all(1)
     send_grad(1)
-    finish(2, 0)
-    finish(2, 1)
-    finish(2, 2)
+    finish(0, 3)
     finish(2, 3)
+    for off in (0, 1, 3):
+        multiply(0, xo_of(off))
     pass_on(2, 4)
     finish(2, 4)
     multiply_all(2)
     send_grad(2)
+    pass_on(0, 4)
+    finish(0, 4)
+    multiply(0, xo_of(2))
 
     for load in loads[5:]:
         load.wait()
@@ -538,10 +518,6 @@
             jnp.dot(grad_scores, kk[cols, :], preferred_element_type=F32) * SCALE
         ).astype(BF16)
 
-    rcopy(ga_in, ga_in, ga_send, ga_recv, zh=zh).wait_recv()
-    back_rows(0)
-    back_rows(1)
-
     rcopy(x_in, x_in, x_send, x_recv, x=x).wait_recv()
     cst[1] = jnp.maximum(cst[0], jnp.max(x_in[...], axis=0))
     for slot in (1, 2):
@@ -555,7 +531,9 @@
         rcopy(
             mine, zl_in.at[back], zl_send, zl_recv, zl=mod(zl + dl, NZL), core=lax.rem(k + dk, NC)
         ).start()
-    back_rows(2)
+    rcopy(ga_in, ga_in, ga_send, ga_recv, zh=zh).wait_recv()
+    for i in range(3):
+        back_rows(i)
     rcopy(zh_in, zh_in, zh_send, zh_recv, zh=zh).wait_recv()
     cols_out[...] = jnp.maximum(cst[1], jnp.max(zh_in[...], axis=0))
     rcopy(zl_in, zl_in, zl_send, zl_recv, zl=zl).wait_recv()
@@ -563,12 +541,10 @@
 
     def units_left(sem, each, c):
         pieces = gz.at[0, 0:c, 0 : UNIT * each, :]
-        rcopy(pieces, pieces, sem, r_recv.at[0], zl=zl).wait_send()
+        rcopy(pieces, pieces, sem, w_recv, zl=zl).wait_send()
 
     wait_units(8 - stayed, 8, functools.partial(units_left, spread_send, 1))
-    wait_units(ups, QUART, functools.partial(units_left, up_send, 1))
-    wait_units(downs, QUART, functools.partial(units_left, down_send, 1))
-    wait_units(landing, 6, functools.partial(units_left, relay_send, 6))
+    wait_units(landing, 6, functools.partial(units_left, relay_send, 9))
     for whole, sem in (
         (gz.at[:, 0:7], ring_send),
         (gz.at[:, 0:8], core_send),
@@ -581,7 +557,7 @@
         (x_in, x_send),
         (zh_in, zh_send),
     ):
-        rcopy(whole, whole, sem, r_recv.at[0], zl=zl).wait_send()
+        rcopy(whole, whole, sem, w_recv, zl=zl).wait_send()
 
 
 def codes(gq, nw, fnew, snew, rows, cols, gq_out, nw_out, nfc_out, nfr_out, nfcol_out, nsc_out, nsr_out, nscol_out):
@@ -651,11 +627,8 @@
             dma((11,)),
             dma,
             dma,
-            dma,
-            dma,
-            dma((QUART,)),
-            dma((2,)),
-            dma((2,)),
+            dma((NZH,)),
+            dma((NZH,)),
             dma,
             dma((2, NZH, 4)),
             dma,

time: 94.6 us -> 94.8 us (level)
  no operation moved by 1% of the time
where the time goes in v4:
time: 94.8 us; the launch traced here: 94.6 us
  Pallas kernels  94 us (99%)
    pallas_call x1, Pallas kernels, per_device(): pl.pallas_call(body, name='whole', out_shape=(shape((SEQ, HD), BF16), sha...  92.9 us

profile of v4, /device:TPU:1, one launch (start us, length us, event | category | flops | bytes accessed | tf_op | source)
XLA Modules:
  0.0 94.6 jit_solution(10189379067060864925)
XLA Ops:
  0.6 92.9 %whole.1 = (bf16[384,128]{1,0:T(8,128)(2,1)S(1)}, f32[688,128]{1,0:T(8,128)S(1)}, f32[688,128]{1,0:T(8,128)S(1)}, f32[688,128]{1,0:T(8,128)S(1)}, f32[2,8,128]{2,1,0:T(8,128)S(1)}, /*index=5*/f32[2,128]{1,0:T(2,128)S(1)}) custom-call(bf16[384,128]{1,0:T(8,128)(2,1)} %q_hbm.1, bf16[384,1024]{1,0:T(8,128)(2,1)} %k_hbm.1, bf16[384,1024]{1,0:T(8,128)(2,1)} %v_hbm.1, ...), custom_call_target="tpu_custom_call" | custom-call | tf_op jit(solution)/shard_map/whole/pallas_call | solution.py:583
  93.5 1.1 %codes.1 = (bf16[384,128]{1,0:T(8,128)(2,1)}, f32[688,128]{1,0:T(8,128)}, bf16[688,128]{1,0:T(8,128)(2,1)}, f32[688]{0:T(1024)}, f32[128]{0:T(128)}, /*index=5*/...) custom-call(bf16[384,128]{1,0:T(8,128)(2,1)S(1)} %get-tuple-element.14.gq, f32[688,128]{1,0:T(8,128)S(1)} %get-tuple-element.15.nw, ...), custom_call_target="tpu_custom_call" | custom-call | tf_op jit(solution)/shard_map/codes/pallas_call | solution.py:662

commit v5 on v4

--- a/solution.py
+++ b/solution.py
@@ -107,13 +107,12 @@
     wt,
     att,
     prob,
-    acct,
+    own,
+    gx_stage,
+    gx_in,
     ga_stage,
     ga_in,
     dwacc,
-    dw_stage,
-    dw_in,
-    dwsum,
     st,
     y_in,
     zl_in,
@@ -132,12 +131,12 @@
     core_recv,
     att_send,
     att_recv,
-    w_send,
-    w_recv,
+    attx_send,
+    attx_recv,
+    gx_send,
+    gx_recv,
     ga_send,
     ga_recv,
-    dw_send,
-    dw_recv,
     y_send,
     y_recv,
     zl_send,
@@ -155,6 +154,9 @@
         return pltpu.make_async_remote_copy(
             src_ref=src, dst_ref=dst, send_sem=send, recv_sem=recv, device_id=dev, device_id_type=MESH
         )
+
+    def came(ref, recv):
+        rcopy(ref, ref, core_send, recv, core=k).wait_recv()
 
     def slot_of(source, plane):
         return jnp.where(source == plane, 0, source + (source < plane).astype(jnp.int32))
@@ -184,38 +186,54 @@
     for load in loads:
         load.start()
 
+    home_pair = lax.rem(x + 2, NX)
+    home_x = lax.rem(pair + 2, NX)
+    across = lax.rem(zl + 2, NZL)
+
     barrier = pltpu.get_barrier_semaphore()
 
     def greet(**dev):
         pl.semaphore_signal(barrier, inc=1, device_id=dev, device_id_type=MESH)
 
-    across = lax.rem(zl + 2, NZL)
+    gives_over = (lax.rem(y, 2) == 0) & (y > 0) & (zl == 0) & (k == 0)
+    takes_over = (x < NX - 1) & (zh == NZH - 1) & (lax.rem(y, 2) == 1) & (lax.rem(zl, 2) == 0) & (k == 1)
     for dz in (1, 2, 0):
-        for dy in (0, 1, NY - 1):
-            for dk in range(NC):
-                there = dict(zh=mod(zh + dz, NZH), y=mod(y + dy, NY), core=lax.rem(k + dk, NC))
-                greet(zl=across, **there)
-                if (dz, dy, dk) != (0, 0, 0):
-                    greet(**there)
-    for dl in (1, 3):
-        for dk in range(NC):
-            greet(zl=mod(zl + dl, NZL), core=lax.rem(k + dk, NC))
-    for dy in range(2, NY - 1):
-        greet(y=mod(y + dy, NY))
+        for half in (0, 1):
+            for line in (zl, across):
+                for dk in range(NC):
+                    there = dict(zh=mod(zh + dz, NZH), zl=line, core=lax.rem(k + dk, NC))
+                    greet(x=pair, y=2 * home_pair + half, **there)
+                    greet(x=home_x, y=2 * x + half, **there)
+
+    @pl.when(gives_over)
+    def _():
+        for line in (0, 2):
+            greet(x=pair - 1, y=2 * home_pair + 1, zh=NZH - 1, zl=line, core=1)
+
+    @pl.when(takes_over)
+    def _():
+        for z in range(NZH):
+            greet(x=home_x, y=2 * x + 2, zh=z, zl=0, core=0)
+
+    for dz in (1, 2):
+        greet(zh=mod(zh + dz, NZH))
     for dx in range(1, NX):
         greet(x=mod(x + dx, NX))
-    greeted = 35 + 4 + 5 + 3
+    for dy in range(1, NY):
+        greet(y=mod(y + dy, NY))
+    for rel in range(1, NZL * NC):
+        greet(zl=mod(zl + rel // NC, NZL), core=lax.rem(k + rel % NC, NC))
+    greeted = 48 + 2 + 3 + 7 + 7 + 2 * gives_over.astype(jnp.int32) + 3 * takes_over.astype(jnp.int32)
 
     loads[0].wait()
     gt[...] = g[...].T
 
-    my_d = 3 * pair + zh
     my_q = 2 * lax.rem(y, 2) + k
-    my_piece = 4 * pair + my_q
+    my_piece = 2 * y + k
 
     def unit_of(i):
         r = QUART * my_q + i
-        unit = UNITS * my_d + r
+        unit = UNITS * (NZH * x + zh) + r
         return lax.div(unit, 8), lax.rem(unit, 8), (r < UNITS) & (unit < ALL_UNITS)
 
     def rows_of(i):
@@ -230,48 +248,36 @@
 
     pl.semaphore_wait(barrier, greeted)
 
-    def unit_home(u):
+    def spread(wanted, u, carry):
         unit = 8 * t + u
         d = lax.div(unit, UNITS)
         r = unit - UNITS * d
         quarter = lax.div(r, QUART)
-        zd, xd = lax.rem(d, NZH), lax.div(d, NZH)
-        yd, kd = 2 * xd + lax.div(quarter, 2), lax.rem(quarter, 2)
-        zld = lax.rem(zl + 2 * lax.rem(u, 2), NZL)
-        home = (zd == zh) & (yd == y) & (kd == k) & (zld == zl)
-        return r - QUART * quarter, 4 * xd + quarter, zd, yd, zld, kd, home
-
-    def spread(wanted, u, stayed):
-        i, piece, zd, yd, zld, kd, home = unit_home(u)
+        i = r - QUART * quarter
+        zd = lax.rem(d, NZH)
         slot = slot_of(zh, zd)
 
-        @pl.when(wanted(zd) & home)
-        def _():
-            gz[0, piece, rows_of(i), :] = gt[rows_of(u), :]
-
-        @pl.when(wanted(zd) & jnp.logical_not(home))
+        @pl.when(wanted(zd))
         def _():
             rcopy(
                 gt.at[rows_of(u), :],
-                gz.at[slot, piece, rows_of(i), :],
+                gz.at[slot, 4 * home_pair + quarter, rows_of(i), :],
                 spread_send,
                 far_recv.at[slot],
+                x=lax.div(d, NZH),
                 zh=zd,
-                y=yd,
-                zl=zld,
-                core=kd,
+                y=2 * home_pair + lax.div(quarter, 2),
+                zl=lax.rem(zl + 2 * lax.rem(u, 2), NZL),
+                core=lax.rem(quarter, 2),
             ).start()
 
-        return stayed + home.astype(jnp.int32)
-
-    stayed = lax.fori_loop(0, 8, functools.partial(spread, lambda zd: zd == zh), jnp.int32(0))
-    lax.fori_loop(0, 8, functools.partial(spread, lambda zd: zd > zh), jnp.int32(0))
-
-    loads[4].wait()
-    wt[x] = w[...].astype(BF16).T
-
-    for dx in (1, 3, 2):
-        rcopy(wt.at[x], wt.at[x], w_send, w_recv, x=mod(x + dx, NX)).start()
+        return carry
+
+    def spread_where(wanted):
+        lax.fori_loop(0, 8, functools.partial(spread, wanted), 0)
+
+    spread_where(lambda zd: zd == zh)
+    spread_where(lambda zd: zd > zh)
 
     for i in (1, 2, 3):
         loads[i].wait()
@@ -287,7 +293,7 @@
         exponent = jnp.exp(scores - jnp.max(scores, axis=-1, keepdims=True))
         probabilities = exponent / jnp.sum(exponent, axis=-1, keepdims=True)
         prob[rows, cols] = probabilities
-        att[0, rows, :] = jnp.dot(
+        att[0, x, rows, :] = jnp.dot(
             probabilities.astype(BF16), vv[cols, :], preferred_element_type=F32
         ).astype(BF16)
 
@@ -295,7 +301,18 @@
         for slot in (1, 2):
             o = other(slot)
             there = slot_of(zh, o)
-            rcopy(att.at[0], att.at[there], att_send, att_recv.at[there - 1], zh=o).start()
+            rcopy(att.at[0, x], att.at[there, x], att_send, att_recv.at[there - 1], zh=o).start()
+
+    def att_over_x(slot):
+        if slot > 0:
+            came(att.at[slot, x], att_recv.at[slot - 1])
+        for dx in (1, 3, 2):
+            rcopy(
+                att.at[slot, x], att.at[slot, x], attx_send, attx_recv.at[slot], x=mod(x + dx, NX)
+            ).start()
+
+    def att_ready(slot):
+        came(att.at[slot, 0:3], attx_recv.at[slot])
 
     def wait_units(n, most, wait):
         for c in range(1, most + 1):
@@ -310,14 +327,11 @@
     landing = sum(lands_here(i)[0].astype(jnp.int32) for i in range(QUART))
     coming = sum(lands_here(i)[1].astype(jnp.int32) for i in range(QUART))
 
-    def units_came(sem, c):
-        piece = gz.at[0, 0, 0 : UNIT * c, :]
-        rcopy(piece, piece, spread_send, sem, zl=zl).wait_recv()
+    def units_came(recv, c):
+        came(gz.at[0, 0, 0 : UNIT * c, :], recv)
 
     def relay(jj):
-        wait_units(
-            landing - stayed if jj == 0 else landing, 6, functools.partial(units_came, far_recv.at[jj])
-        )
+        wait_units(landing, 6, functools.partial(units_came, far_recv.at[jj]))
 
         def give(i, carry):
             piece = gz.at[jj, my_piece, rows_of(i), :]
@@ -331,156 +345,171 @@
 
         lax.fori_loop(0, QUART, give, 0)
 
-    HALF = 96
-
-    def part(jj, source, core, way, hops):
-        start, size = 0, QROWS
-        if jj == 0 and hops == 4:
-            start, size = (0, HALF) if way == 0 else (HALF, QROWS - HALF)
-        return gz.at[jj, 2 * source + core, pl.ds(start, size), :]
+    PARTS = ((0, 96), (96, QROWS - 96))
+
+    def reach(way, jj, part):
+        return 4 if way == (part if jj == 0 else jj - 1) else 3
+
+    def piece_of(jj, source, part):
+        start, size = PARTS[part]
+        return gz.at[jj, 2 * source + k, pl.ds(start, size), :]
 
     def from_source(way, hops):
         return mod(y - hops, NY) if way == 0 else mod(y + hops, NY)
 
-    def forward(way, jj, hops):
-        piece = part(jj, from_source(way, hops), k, way, hops + 1)
+    def forward(way, jj, hops, part):
+        piece = piece_of(jj, from_source(way, hops), part)
         rcopy(
             piece,
             piece,
             ring_send,
-            ring_recv.at[way, jj, hops],
+            ring_recv.at[way, jj, hops, part],
             y=mod(y + 1, NY) if way == 0 else mod(y - 1, NY),
         ).start()
 
-    def arrived(way, jj, hops):
-        piece = part(jj, from_source(way, hops), k, way, hops)
-        rcopy(piece, piece, ring_send, ring_recv.at[way, jj, hops - 1], y=y).wait_recv()
-
-    def to_partner(way, jj, hops):
-        piece = part(jj, from_source(way, hops), k, way, hops)
+    def to_partner(way, jj, hops, part):
+        piece = piece_of(jj, from_source(way, hops), part)
         rcopy(piece, piece, core_send, core_recv.at[jj, hops], core=1 - k).start()
-
-    def partner_has(jj, hops):
-        pieces = gz.at[0, 0 : 2 if hops in (1, 2, 3) else 1]
-        rcopy(pieces, pieces, core_send, core_recv.at[jj, hops], core=k).wait_recv()
-
-    reach = {(0, 0): 4, (1, 0): 4, (0, 1): 4, (1, 1): 3, (0, 2): 3, (1, 2): 4}
 
     def start_ring(jj):
         wait_units(coming, QUART, functools.partial(units_came, near_recv.at[jj]))
-        forward(0, jj, 0)
-        forward(1, jj, 0)
-        to_partner(0, jj, 0)
+        for part in (0, 1):
+            for way in (0, 1):
+                forward(way, jj, 0, part)
+        for part in (0, 1):
+            to_partner(0, jj, 0, part)
 
     def pass_on(jj, hops):
-        for way in (0, 1):
-            if hops <= reach[way, jj]:
-                arrived(way, jj, hops)
-                if hops < reach[way, jj]:
-                    forward(way, jj, hops)
-                to_partner(way, jj, hops)
-
-    def multiply(jj, xo):
-        block = gz[jj, pl.ds(4 * xo, 4)].reshape(PADROWS, SEQ)[:ROWS]
-        term = jnp.dot(wt[xo], block, preferred_element_type=F32)
-        acct[jj] = term if jj not in started else acct[jj] + term
-        started.add(jj)
-
-    def weight_term(jj, source, first, last):
+        for part in (0, 1):
+            for way in (0, 1):
+                if hops <= reach(way, jj, part):
+                    came(
+                        piece_of(jj, from_source(way, hops), part),
+                        ring_recv.at[way, jj, hops - 1, part],
+                    )
+                    if hops < reach(way, jj, part):
+                        forward(way, jj, hops, part)
+                    to_partner(way, jj, hops, part)
+
+    def partner_has(jj, hops):
+        came(gz.at[0, 0 : 2 if hops in (1, 2, 3) else 1], core_recv.at[jj, hops])
+
+    def weight_term(jj, source):
         block = gz[jj, pl.ds(2 * source, 2)].reshape(HALF_ROWS, SEQ)
-        term = jnp.dot(block, att[jj], preferred_element_type=F32)
-        dwacc[source] = term if first else dwacc[source] + term
-        if last:
-            xo, half = lax.div(source, 2), lax.rem(source, 2)
-
-            @pl.when(xo != x)
-            def _():
-                dw_stage[source] = dwacc[source].astype(BF16)
-                rel = mod(x - xo, NX) - 1
-                rcopy(
-                    dw_stage.at[source], dw_in.at[rel, half], dw_send, dw_recv.at[half], x=xo
-                ).start()
+        sequence = lax.rem(lax.div(source, 2) + 2, NX)
+        term = jnp.dot(block, att[jj, sequence], preferred_element_type=F32)
+        rows = pl.ds(pl.multiple_of(HALF_ROWS * lax.rem(source, 2), UNIT), HALF_ROWS)
+        dwacc[rows, :] = dwacc[rows, :] + term
 
     def finish(jj, hops):
-        partner_has(jj, hops)
-        done[hops] += 1
         for way in (0, 1) if hops in (1, 2, 3) else (0,):
-            weight_term(jj, from_source(way, hops), done[hops] == 1, done[hops] == NZH)
-
-    done = [0] * 5
-    started = set()
-
-    def xo_of(off):
-        return mod(pair + off, NX)
-
-    def multiply_all(jj):
-        for off in (0, 1, 3, 2):
-            multiply(jj, xo_of(off))
-
-    def send_grad(jj):
-        ga_stage[jj - 1] = acct[jj].astype(BF16)
-        o = other(jj)
-        rcopy(ga_stage.at[jj - 1], ga_in.at[slot_of(zh, o) - 1], ga_send, ga_recv, zh=o).start()
-
+            weight_term(jj, from_source(way, hops))
+
+    def multiply(jj, off):
+        p = mod(pair + off, NX)
+        sequence = lax.rem(p + 2, NX)
+        block = gz[jj, pl.ds(4 * p, 4)].reshape(PADROWS, SEQ)[:ROWS]
+        share = jnp.dot(wt[...], block, preferred_element_type=F32)
+
+        @pl.when(sequence == x)
+        def _():
+            own[jj] = share
+
+        @pl.when(sequence != x)
+        def _():
+            gx_stage[jj, sequence] = share.astype(BF16)
+            rel = mod(x - sequence, NX) - 1
+            rcopy(
+                gx_stage.at[jj, sequence], gx_in.at[jj, rel], gx_send, gx_recv.at[jj], x=sequence
+            ).start()
+
+    def over_x(jj):
+        came(gx_in.at[jj], gx_recv.at[jj])
+        total = own[jj]
+        for rel in range(NX - 1):
+            total = total + gx_in[jj, rel].astype(F32)
+        if jj == 0:
+            own[0] = total
+        else:
+            ga_stage[jj - 1] = total.astype(BF16)
+            o = other(jj)
+            rcopy(ga_stage.at[jj - 1], ga_in.at[slot_of(zh, o) - 1], ga_send, ga_recv, zh=o).start()
+
+    att_over_x(0)
     relay(0)
-    lax.fori_loop(0, 8, functools.partial(spread, lambda zd: zd < zh), jnp.int32(0))
+    spread_where(lambda zd: zd < zh)
+
+    loads[4].wait()
+    wt[...] = w[...].astype(BF16).T
+    dwacc[...] = jnp.zeros_like(dwacc)
+
     start_ring(0)
     relay(1)
+    send_att()
     pass_on(0, 1)
+    start_ring(1)
     relay(2)
-    send_att()
-    start_ring(1)
-    pass_on(0, 2)
+    att_ready(0)
+    partner_has(0, 0)
     finish(0, 0)
     pass_on(1, 1)
+    partner_has(0, 1)
     finish(0, 1)
     start_ring(2)
+    multiply(0, 0)
+    pass_on(1, 2)
+    att_over_x(1)
+    att_over_x(2)
+    pass_on(2, 1)
+    for hops in (0, 1, 2):
+        partner_has(1, hops)
+    pass_on(1, 3)
+    multiply(1, 0)
+    pass_on(2, 2)
+    partner_has(1, 3)
+    multiply(1, 1)
+    multiply(1, 3)
+    pass_on(1, 4)
+    pass_on(2, 3)
+    partner_has(1, 4)
+    multiply(1, 2)
+    for hops in (0, 1, 2):
+        partner_has(2, hops)
+    multiply(2, 0)
+    pass_on(0, 2)
+    partner_has(2, 3)
+    multiply(2, 1)
+    multiply(2, 3)
+    pass_on(2, 4)
+    partner_has(2, 4)
+    multiply(2, 2)
+    att_ready(1)
+    for hops in range(3):
+        finish(1, hops)
+    pass_on(0, 3)
+    over_x(1)
+    for hops in (3, 4):
+        finish(1, hops)
+    att_ready(2)
+    for hops in range(5):
+        finish(2, hops)
+    partner_has(0, 2)
     finish(0, 2)
-    pass_on(1, 2)
-    pass_on(2, 1)
-    rcopy(att.at[0], att.at[1], att_send, att_recv.at[0], zh=zh).wait_recv()
-    finish(1, 0)
-    finish(1, 1)
-    pass_on(1, 3)
-    finish(1, 2)
-    pass_on(2, 2)
-    rcopy(att.at[0], att.at[2], att_send, att_recv.at[1], zh=zh).wait_recv()
-    finish(2, 0)
-    finish(2, 1)
-    pass_on(1, 4)
-    rcopy(wt.at[0:3], wt.at[0:3], w_send, w_recv, x=x).wait_recv()
-    finish(1, 3)
-    pass_on(2, 3)
-    finish(2, 2)
-    pass_on(0, 3)
-    finish(1, 4)
-    multiply_all(1)
-    send_grad(1)
+    partner_has(0, 3)
     finish(0, 3)
-    finish(2, 3)
-    for off in (0, 1, 3):
-        multiply(0, xo_of(off))
-    pass_on(2, 4)
-    finish(2, 4)
-    multiply_all(2)
-    send_grad(2)
+    over_x(2)
+    multiply(0, 1)
+    multiply(0, 3)
     pass_on(0, 4)
+    partner_has(0, 4)
     finish(0, 4)
-    multiply(0, xo_of(2))
+    multiply(0, 2)
 
     for load in loads[5:]:
         load.wait()
-    for half in (0, 1):
-        piece = dw_in.at[:, half]
-        rcopy(piece, piece, dw_send, dw_recv.at[half], x=x).wait_recv()
-    for half in (0, 1):
-        total = dwacc[2 * x + half]
-        for rel in range(NX - 1):
-            total = total + dw_in[rel, half].astype(F32)
-        dwsum[pl.ds(HALF_ROWS * half, HALF_ROWS), :] = total
     for c, start, size in row_chunks():
         rows = pl.ds(start, size)
-        grad = dwsum[rows, :]
+        grad = dwacc[rows, :]
         low_first = jnp.minimum(down(frow, start, size), fcol[...].reshape(1, HD))
         low_second = jnp.minimum(down(srow, start, size), scol[...].reshape(1, HD))
         first = fc[rows, :].astype(F32) * low_first
@@ -505,25 +534,20 @@
 
     def back_rows(i):
         rows, cols = pl.ds(128 * i, 128), pl.ds(0, 128 * (i + 1))
-        total = acct[0, :, rows]
+        total = own[0, :, rows]
         for s in range(2):
             total = total + ga_in[s, :, rows].astype(F32)
         grad_half = total.astype(BF16).T
         grad_probs = lax.dot_general(grad_half, vv[cols, :], NT, preferred_element_type=F32)
         row_dot = jnp.sum(
-            grad_half.astype(F32) * att[0, rows, :].astype(F32), axis=-1, keepdims=True
+            grad_half.astype(F32) * att[0, x, rows, :].astype(F32), axis=-1, keepdims=True
         )
         grad_scores = (prob[rows, cols] * (grad_probs - row_dot)).astype(BF16)
         gq_out[rows, :] = (
             jnp.dot(grad_scores, kk[cols, :], preferred_element_type=F32) * SCALE
         ).astype(BF16)
 
-    rcopy(x_in, x_in, x_send, x_recv, x=x).wait_recv()
-    cst[1] = jnp.maximum(cst[0], jnp.max(x_in[...], axis=0))
-    for slot in (1, 2):
-        o = other(slot)
-        rcopy(cst.at[1], zh_in.at[slot_of(zh, o) - 1], zh_send, zh_recv, zh=o).start()
-    rcopy(y_in, y_in, y_send, y_recv, y=y).wait_recv()
+    came(y_in, y_recv)
     mine[...] = jnp.maximum(st[...], jnp.max(y_in[...], axis=0))
     for rel in range(1, NZL * NC):
         dl, dk = rel // NC, rel % NC
@@ -531,33 +555,40 @@
         rcopy(
             mine, zl_in.at[back], zl_send, zl_recv, zl=mod(zl + dl, NZL), core=lax.rem(k + dk, NC)
         ).start()
-    rcopy(ga_in, ga_in, ga_send, ga_recv, zh=zh).wait_recv()
+    came(x_in, x_recv)
+    cst[1] = jnp.maximum(cst[0], jnp.max(x_in[...], axis=0))
+    for slot in (1, 2):
+        o = other(slot)
+        rcopy(cst.at[1], zh_in.at[slot_of(zh, o) - 1], zh_send, zh_recv, zh=o).start()
+    over_x(0)
+    came(ga_in, ga_recv)
     for i in range(3):
         back_rows(i)
-    rcopy(zh_in, zh_in, zh_send, zh_recv, zh=zh).wait_recv()
+    came(zl_in, zl_recv)
+    rows_out[...] = jnp.maximum(mine[...], jnp.max(zl_in[...], axis=0))
+    came(zh_in, zh_recv)
     cols_out[...] = jnp.maximum(cst[1], jnp.max(zh_in[...], axis=0))
-    rcopy(zl_in, zl_in, zl_send, zl_recv, zl=zl).wait_recv()
-    rows_out[...] = jnp.maximum(mine[...], jnp.max(zl_in[...], axis=0))
-
-    def units_left(sem, each, c):
-        pieces = gz.at[0, 0:c, 0 : UNIT * each, :]
-        rcopy(pieces, pieces, sem, w_recv, zl=zl).wait_send()
-
-    wait_units(8 - stayed, 8, functools.partial(units_left, spread_send, 1))
-    wait_units(landing, 6, functools.partial(units_left, relay_send, 9))
-    for whole, sem in (
+
+    def left(ref, send):
+        rcopy(ref, ref, send, zh_recv, core=k).wait_send()
+
+    left(gz.at[0, 0, 0 : UNIT * 8, :], spread_send)
+    wait_units(
+        landing, 6, lambda c: left(gz.at[0, 0:c, 0 : UNIT * NZH * (NZL - 1), :], relay_send)
+    )
+    for whole, send in (
         (gz.at[:, 0:7], ring_send),
         (gz.at[:, 0:8], core_send),
-        (att.at[0:2], att_send),
-        (wt.at[0:3], w_send),
+        (att.at[0, 0:2], att_send),
+        (att.at[:, 0:3], attx_send),
+        (gx_in, gx_send),
         (ga_in, ga_send),
-        (dw_in, dw_send),
         (y_in, y_send),
         (zl_in, zl_send),
         (x_in, x_send),
         (zh_in, zh_send),
     ):
-        rcopy(whole, whole, sem, w_recv, zl=zl).wait_send()
+        left(whole, send)
 
 
 def codes(gq, nw, fnew, snew, rows, cols, gq_out, nw_out, nfc_out, nfr_out, nfcol_out, nsc_out, nsr_out, nscol_out):
@@ -607,15 +638,14 @@
             pltpu.VMEM((HD,), F32),
             pltpu.VMEM((HD, SEQ), BF16),
             pltpu.VMEM((NZH, 4 * NX, QROWS, SEQ), BF16),
-            pltpu.VMEM((NX, HD, ROWS), BF16),
-            pltpu.VMEM((NZH, SEQ, HD), BF16),
+            pltpu.VMEM((HD, ROWS), BF16),
+            pltpu.VMEM((NZH, NX, SEQ, HD), BF16),
             pltpu.VMEM((SEQ, SEQ), F32),
             pltpu.VMEM((NZH, HD, SEQ), F32),
+            pltpu.VMEM((NZH, NX, HD, SEQ), BF16),
+            pltpu.VMEM((NZH, NX - 1, HD, SEQ), BF16),
             pltpu.VMEM((2, HD, SEQ), BF16),
             pltpu.VMEM((2, HD, SEQ), BF16),
-            pltpu.VMEM((2 * NX, HALF_ROWS, HD), F32),
-            pltpu.VMEM((2 * NX, HALF_ROWS, HD), BF16),
-            pltpu.VMEM((NX - 1, 2, HALF_ROWS, HD), BF16),
             pltpu.VMEM((PADROWS, HD), F32),
             pltpu.VMEM((2, 8, HD), F32),
             pltpu.VMEM((NY - 1, 2, 8, HD), F32),
@@ -630,17 +660,17 @@
             dma((NZH,)),
             dma((NZH,)),
             dma,
-            dma((2, NZH, 4)),
+            dma((2, NZH, 4, 2)),
             dma,
             dma((NZH, 5)),
             dma,
             dma((2,)),
             dma,
-            dma,
-            dma,
-            dma,
-            dma,
-            dma((2,)),
+            dma((NZH,)),
+            dma,
+            dma((NZH,)),
+            dma,
+            dma,
             dma,
             dma,
             dma,

time: 94.8 us -> 92.9 us (0.980)
  Pallas kernels: 94 us -> 92.1 us
    pallas_call x1, Pallas kernels: 92.9 us -> 91 us  [per_device(): pl.pallas_call(body, name='whole', out_shape=(shape((SEQ, HD), BF16), sha...]
where the time goes in v5:
time: 92.9 us; the launch traced here: 92.7 us
  Pallas kernels  92.1 us (99%)
    pallas_call x1, Pallas kernels, per_device(): pl.pallas_call(body, name='whole', out_shape=(shape((SEQ, HD), BF16), sha...  91 us

profile of v5, /device:TPU:1, one launch (start us, length us, event | category | flops | bytes accessed | tf_op | source)
XLA Modules:
  0.0 92.7 jit_solution(6628541007674530042)
XLA Ops:
  0.6 91.0 %whole.1 = (bf16[384,128]{1,0:T(8,128)(2,1)S(1)}, f32[688,128]{1,0:T(8,128)S(1)}, f32[688,128]{1,0:T(8,128)S(1)}, f32[688,128]{1,0:T(8,128)S(1)}, f32[2,8,128]{2,1,0:T(8,128)S(1)}, /*index=5*/f32[2,128]{1,0:T(2,128)S(1)}) custom-call(bf16[384,128]{1,0:T(8,128)(2,1)} %q_hbm.1, bf16[384,1024]{1,0:T(8,128)(2,1)} %k_hbm.1, bf16[384,1024]{1,0:T(8,128)(2,1)} %v_hbm.1, ...), custom_call_target="tpu_custom_call" | custom-call | tf_op jit(solution)/shard_map/whole/pallas_call | solution.py:614
  91.6 1.1 %codes.1 = (bf16[384,128]{1,0:T(8,128)(2,1)}, f32[688,128]{1,0:T(8,128)}, bf16[688,128]{1,0:T(8,128)(2,1)}, f32[688]{0:T(1024)}, f32[128]{0:T(128)}, /*index=5*/...) custom-call(bf16[384,128]{1,0:T(8,128)(2,1)S(1)} %get-tuple-element.14.gq, f32[688,128]{1,0:T(8,128)S(1)} %get-tuple-element.15.nw, ...), custom_call_target="tpu_custom_call" | custom-call | tf_op jit(solution)/shard_map/codes/pallas_call | solution.py:692

commit v6 on v4

v6 whole, which is shorter than its diff:
```python
import functools

import jax
import jax.numpy as jnp
from jax import lax
from jax.experimental import pallas as pl
from jax.experimental.pallas import tpu as pltpu
from jax.sharding import Mesh
from jax.sharding import PartitionSpec as P

NX, NZH, NY, NZL, NC = 4, 3, 8, 4, 2
AXES = ("x", "zh", "y", "zl", "core")
DP = ("x", "zh")
TENSOR = ("y", "zl", "core")
MESH = pl.DeviceIdType.MESH

HD = 128
SEQ = 384
ROWS = 688
UNIT = 16
UNITS = ROWS // UNIT
ALL_UNITS = 512
HOMES = NY * NC
SLOTS = 4
SLOT = 3 * UNITS
SCALE = HD ** (-0.5)

beta_first = 0.9
beta_second = 0.95
learning = 0.01
decay_rate = 0.1
adam_eps = 1e-08
code_eps = 1e-06
correct_first = 1.0 - 0.9**10
correct_second = 1.0 - 0.95**10

F32 = jnp.float32
BF16 = jnp.bfloat16
NT = (((1,), (1,)), ((), ()))


def mod(a, n):
    return lax.rem(a + n, n)


def row_chunks():
    return [(c, 128 * c, min(128, ROWS - 128 * c)) for c in range(6)]


def lane_rows(values):
    highest = jnp.max(values, axis=1, keepdims=True)
    out = []
    for c, start, size in row_chunks():
        eye = lax.broadcasted_iota(jnp.int32, (size, 128), 0) == lax.broadcasted_iota(
            jnp.int32, (size, 128), 1
        )
        out.append(
            jnp.max(jnp.where(eye, highest[start : start + size], 0.0), axis=0, keepdims=True)
        )
    out.append(jnp.zeros((2, 128), F32))
    return jnp.concatenate(out, axis=0)


def down(vector, start, size):
    row = vector[pl.ds(start, size)].reshape(1, size)
    if size < 128:
        row = jnp.concatenate([row, jnp.zeros((1, 128 - size), F32)], axis=1)
    return down_rows(row)[:size]


def down_rows(row):
    return jnp.broadcast_to(row, (128, 128)).T


def body(
    q_hbm,
    k_hbm,
    v_hbm,
    g_hbm,
    w_hbm,
    fc_hbm,
    frow_hbm,
    fcol_hbm,
    sc_hbm,
    srow_hbm,
    scol_hbm,
    gq_out,
    nw_out,
    fnew_out,
    snew_out,
    rows_out,
    cols_out,
    q,
    kk,
    vv,
    g,
    w,
    fc,
    sc,
    frow,
    fcol,
    srow,
    scol,
    gt,
    gz,
    wt,
    att,
    prob,
    acct,
    ga_stage,
    ga_in,
    dwacc,
    dw_stage,
    dw_in,
    st,
    y_in,
    zl_in,
    mine,
    cst,
    x_in,
    zh_in,
    in_sem,
    spread_send,
    relay_send,
    far_recv,
    near_recv,
    ring_send,
    ring_recv,
    core_send,
    core_recv,
    att_send,
    att_recv,
    w_send,
    w_recv,
    ga_send,
    ga_recv,
    dw_send,
    dw_recv,
    y_send,
    y_recv,
    zl_send,
    zl_recv,
    x_send,
    x_recv,
    zh_send,
    zh_recv,
):
    x, zh, y, zl, k = (lax.axis_index(a) for a in AXES)
    t = 8 * y + 2 * zl + k
    pair = lax.div(y, 2)

    def rcopy(src, dst, send, recv, **dev):
        return pltpu.make_async_remote_copy(
            src_ref=src, dst_ref=dst, send_sem=send, recv_sem=recv, device_id=dev, device_id_type=MESH
        )

    def came(ref, recv):
        rcopy(ref, ref, core_send, recv, core=k).wait_recv()

    def sequence_of(source, plane):
        return jnp.where(source == plane, 0, source + (source < plane).astype(jnp.int32))

    def other(sequence):
        return sequence - 1 + (sequence - 1 >= zh).astype(jnp.int32)

    heads = pl.ds(pl.multiple_of(y * HD, HD), HD)
    loads = [
        pltpu.make_async_copy(src, dst, in_sem.at[i])
        for i, (src, dst) in enumerate(
            [
                (g_hbm, g),
                (q_hbm, q),
                (k_hbm.at[:, heads], kk),
                (v_hbm.at[:, heads], vv),
                (w_hbm, w),
                (fc_hbm, fc),
                (sc_hbm, sc),
                (frow_hbm, frow),
                (fcol_hbm, fcol),
                (srow_hbm, srow),
                (scol_hbm, scol),
            ]
        )
    ]
    for load in loads:
        load.start()

    me = 2 * y + k

    def rows_of(u):
        return pl.ds(pl.multiple_of(UNIT * u, UNIT), UNIT)

    def goes_to(u):
        unit = 8 * t + u
        d = lax.div(unit, UNITS)
        xd, zd = lax.div(d, NZH), lax.rem(d, NZH)
        ahead = mod(xd - x, NX)
        sequence = sequence_of(zh, zd)
        turn = 2 * (ahead - 1) + sequence - 1
        slot = jnp.where(ahead == 0, 3, jnp.where(sequence == 0, 0, 1 + lax.div(turn + 3, 3) - 1))
        index = jnp.where(
            ahead == 0,
            lax.rem(sequence + 2, 3),
            jnp.where(sequence == 0, ahead - 1, lax.rem(turn + 3, 3)),
        )
        e = UNITS * index + unit - UNITS * d
        h = jnp.minimum(lax.div(e, 8), HOMES - 1)
        home = dict(
            zh=zd,
            y=lax.div(h, 2),
            zl=lax.rem(zl + 2 * lax.rem(u, 2), NZL),
            core=lax.rem(h, 2),
        )
        here = (zd == zh) & (h == me) & (home["zl"] == zl)
        return slot, SLOT * slot + e, home, here

    def unit_of(slot, j):
        e = 8 * me + j
        index, r = lax.div(e, UNITS), lax.rem(e, UNITS)
        if slot == 0:
            xd, z = mod(x + 1 + index, NX), zh
        elif slot == 3:
            xd, z = x, jnp.where(index == 2, zh, other(index + 1))
        else:
            turn = 3 * (slot - 1) + index
            xd, z = mod(x + 1 + lax.div(turn, 2), NX), other(1 + lax.rem(turn, 2))
        unit = UNITS * (NZH * xd + zh) + r
        mine_too = (j < 8) | (me == HOMES - 1)
        return z, lax.div(unit, 8), lax.rem(unit, 8), mine_too & (unit < ALL_UNITS), mine_too

    def lands_here(slot, j):
        z, column, u, there, _ = unit_of(slot, j)
        line = lax.rem(lax.rem(lax.div(column, 2), NZL) + 2 * lax.rem(u, 2), NZL)
        return there & (line == zl), there & (line != zl), (z == zh) & (column == t)

    def count(flags):
        return sum(f.astype(jnp.int32) for f in flags)

    landing = [count(lands_here(s, j)[0] for j in range(9)) for s in range(SLOTS)]
    coming = [count(lands_here(s, j)[1] for j in range(9)) for s in range(SLOTS)]
    staying = [
        count(lands_here(s, j)[0] & lands_here(s, j)[2] for j in range(9)) for s in range(SLOTS)
    ]

    barrier = pltpu.get_barrier_semaphore()

    def greet(**dev):
        pl.semaphore_signal(barrier, inc=1, device_id=dev, device_id_type=MESH)

    def greet_home(u, carry):
        slot, place, home, here = goes_to(u)
        pl.when(jnp.logical_not(here))(functools.partial(greet, **home))
        return carry

    def greet_sources(slot, j, carry):
        z, column, u, there, _ = unit_of(slot, j)
        lands, _, same = lands_here(slot, j)

        @pl.when(lands & jnp.logical_not(same))
        def _():
            greet(zh=z, y=lax.div(column, 8), zl=lax.rem(lax.div(column, 2), NZL), core=lax.rem(column, 2))

        return carry

    lax.fori_loop(0, 8, greet_home, 0)
    for slot in range(SLOTS):
        lax.fori_loop(0, 9, functools.partial(greet_sources, slot), 0)
    for dz in (1, 2):
        greet(zh=mod(zh + dz, NZH))
    for dx in range(1, NX):
        greet(x=mod(x + dx, NX))
    for dy in range(1, NY):
        greet(y=mod(y + dy, NY))
    for rel in range(1, NZL * NC):
        greet(zl=mod(zl + rel // NC, NZL), core=lax.rem(k + rel % NC, NC))
    greeted = 8 + sum(landing) - 2 * sum(staying) + 2 + 3 + 7 + 7

    loads[0].wait()
    gt[...] = g[...].T

    for slot in range(SLOTS):

        def clear(j, carry):
            _, _, _, there, mine_too = unit_of(slot, j)

            @pl.when(mine_too & jnp.logical_not(there))
            def _():
                gz[SLOT * slot + 8 * me + j] = jnp.zeros((UNIT, SEQ), BF16)

            return carry

        lax.fori_loop(0, 9, clear, 0)

    pl.semaphore_wait(barrier, greeted)

    def spread(wanted, u, carry):
        slot, place, home, here = goes_to(u)

        @pl.when((slot == wanted) & here)
        def _():
            gz[place] = gt[rows_of(u), :]

        @pl.when((slot == wanted) & jnp.logical_not(here))
        def _():
            rcopy(gt.at[rows_of(u), :], gz.at[place], spread_send, far_recv.at[slot], **home).start()

        return carry

    for slot in range(SLOTS):
        lax.fori_loop(0, 8, functools.partial(spread, slot), 0)

    loads[4].wait()
    wt[3] = w[...].astype(BF16).T
    for dx in (1, 3, 2):
        rcopy(wt.at[3], wt.at[NX - 1 - dx], w_send, w_recv, x=mod(x + dx, NX)).start()

    for i in (1, 2, 3):
        loads[i].wait()
    for i in range(3):
        rows, cols = pl.ds(128 * i, 128), pl.ds(0, 128 * (i + 1))
        scores = (
            lax.dot_general(q[rows, :], kk[cols, :], NT, preferred_element_type=F32) * SCALE
        )
        future = lax.broadcasted_iota(jnp.int32, scores.shape, 1) > (
            lax.broadcasted_iota(jnp.int32, scores.shape, 0) + 128 * i
        )
        scores = jnp.where(future, -1e30, scores)
        exponent = jnp.exp(scores - jnp.max(scores, axis=-1, keepdims=True))
        probabilities = exponent / jnp.sum(exponent, axis=-1, keepdims=True)
        prob[rows, cols] = probabilities
        att[0, rows, :] = jnp.dot(
            probabilities.astype(BF16), vv[cols, :], preferred_element_type=F32
        ).astype(BF16)

    def send_att():
        for sequence in (1, 2):
            o = other(sequence)
            there = sequence_of(zh, o)
            rcopy(att.at[0], att.at[there], att_send, att_recv.at[there - 1], zh=o).start()

    def wait_units(n, most, wait):
        for c in range(1, most + 1):
            pl.when(n == c)(functools.partial(wait, c))

    def units_came(recv, c):
        came(gz.at[0:c], recv)

    def relay(slot):
        wait_units(
            landing[slot] - staying[slot], 9, functools.partial(units_came, far_recv.at[slot])
        )

        def give(j, carry):
            piece = gz.at[SLOT * slot + 8 * me + j]

            @pl.when(lands_here(slot, j)[0])
            def _():
                for dl in (1, 3, 2):
                    rcopy(
                        piece, piece, relay_send.at[slot], near_recv.at[slot], zl=mod(zl + dl, NZL)
                    ).start()

            return carry

        lax.fori_loop(0, 9, give, 0)

    def reach(way, slot):
        return 4 if way == slot % 2 else 3

    def from_source(way, hops):
        return mod(y - hops, NY) if way == 0 else mod(y + hops, NY)

    def parts_of(slot, source, core):
        start = SLOT * slot + 8 * (2 * source + core)
        last = (source == NY - 1) & (core == 1)
        return (
            ((start, 4, None),),
            ((start + 4, 4, jnp.logical_not(last)), (start + 4, 5, last)),
        )

    def each_size(sizes, act):
        for start, units, when in sizes:
            ref = gz.at[pl.ds(start, units)]
            if when is None:
                act(ref)
            else:
                pl.when(when)(functools.partial(act, ref))

    def forward(way, slot, hops, part):
        def go(piece):
            rcopy(
                piece,
                piece,
                ring_send,
                ring_recv.at[way, slot, hops, part],
                y=mod(y + 1, NY) if way == 0 else mod(y - 1, NY),
            ).start()

        each_size(parts_of(slot, from_source(way, hops), k)[part], go)

    def to_partner(way, slot, hops, part):
        def go(piece):
            rcopy(piece, piece, core_send, core_recv.at[way, slot, hops], core=1 - k).start()

        each_size(parts_of(slot, from_source(way, hops), k)[part], go)

    def start_ring(slot):
        wait_units(coming[slot], 9, functools.partial(units_came, near_recv.at[slot]))
        for part in (0, 1):
            for way in (0, 1):
                forward(way, slot, 0, part)
        for part in (0, 1):
            to_partner(0, slot, 0, part)

    def pass_on(slot, hops):
        for part in (0, 1):
            for way in (0, 1):
                if hops <= reach(way, slot):
                    each_size(
                        parts_of(slot, from_source(way, hops), k)[part],
                        lambda piece: came(piece, ring_recv.at[way, slot, hops - 1, part]),
                    )
                    if hops < reach(way, slot):
                        forward(way, slot, hops, part)
                    to_partner(way, slot, hops, part)

    def partner_has(slot):
        for hops in range(5):
            for way in (0, 1):
                if (hops > 0 or way == 0) and hops <= reach(way, slot):
                    last = (from_source(way, hops) == NY - 1) & (k == 0)
                    recv = core_recv.at[way, slot, hops]
                    pl.when(last)(functools.partial(came, gz.at[0:9], recv))
                    pl.when(jnp.logical_not(last))(functools.partial(came, gz.at[0:8], recv))

    def block_of(slot, index):
        return gz[pl.ds(SLOT * slot + UNITS * index, UNITS)].reshape(ROWS, SEQ)

    def member(slot, index):
        if slot == 0:
            return index, 0
        if slot == 3:
            return 3, (index + 1) % 3
        turn = 3 * (slot - 1) + index
        return turn // 2, 1 + turn % 2

    started = set()

    def weight_term(slot, index):
        rows, sequence = member(slot, index)
        term = jnp.dot(block_of(slot, index), att[sequence], preferred_element_type=F32)
        dwacc[rows] = dwacc[rows] + term if ("w", rows) in started else term
        started.add(("w", rows))

    def multiply(slot, index):
        rows, sequence = member(slot, index)
        term = jnp.dot(wt[rows], block_of(slot, index), preferred_element_type=F32)
        acct[sequence] = acct[sequence] + term if ("g", sequence) in started else term
        started.add(("g", sequence))

    def send_term(rows):
        dw_stage[rows] = dwacc[rows].astype(BF16)
        rcopy(
            dw_stage.at[rows], dw_in.at[NX - 2 - rows], dw_send, dw_recv, x=mod(x + 1 + rows, NX)
        ).start()

    def send_grad(sequence):
        ga_stage[sequence - 1] = acct[sequence].astype(BF16)
        o = other(sequence)
        rcopy(
            ga_stage.at[sequence - 1], ga_in.at[sequence_of(zh, o) - 1], ga_send, ga_recv, zh=o
        ).start()

    relay(0)
    start_ring(0)
    relay(1)
    relay(2)
    relay(3)
    pass_on(0, 1)
    start_ring(1)
    pass_on(0, 2)
    start_ring(2)
    send_att()
    pass_on(1, 1)
    pass_on(0, 3)
    start_ring(3)
    pass_on(2, 1)
    pass_on(1, 2)
    pass_on(0, 4)
    pass_on(3, 1)
    partner_has(0)
    weight_term(0, 0)
    weight_term(0, 1)
    pass_on(2, 2)
    weight_term(0, 2)
    came(wt.at[0:3], w_recv)
    multiply(0, 0)
    pass_on(1, 3)
    multiply(0, 1)
    multiply(0, 2)
    pass_on(1, 4)
    pass_on(3, 2)
    came(att.at[1], att_recv.at[0])
    came(att.at[2], att_recv.at[1])
    partner_has(1)
    weight_term(1, 0)
    weight_term(1, 1)
    send_term(0)
    pass_on(2, 3)
    weight_term(1, 2)
    multiply(1, 0)
    multiply(1, 1)
    pass_on(2, 4)
    multiply(1, 2)
    pass_on(3, 3)
    partner_has(2)
    weight_term(2, 0)
    send_term(1)
    weight_term(2, 1)
    weight_term(2, 2)
    send_term(2)
    pass_on(3, 4)
    for index in range(3):
        multiply(2, index)
    partner_has(3)
    for index in range(3):
        weight_term(3, index)

    for load in loads[5:]:
        load.wait()
    came(dw_in, dw_recv)
    for c, start, size in row_chunks():
        rows = pl.ds(start, size)
        grad = dwacc[3, rows, :]
        for i in range(NX - 1):
            grad = grad + dw_in[i, rows, :].astype(F32)
        low_first = jnp.minimum(down(frow, start, size), fcol[...].reshape(1, HD))
        low_second = jnp.minimum(down(srow, start, size), scol[...].reshape(1, HD))
        first = fc[rows, :].astype(F32) * low_first
        second = sc[rows, :].astype(F32) * low_second
        first_new = beta_first * first + (1.0 - beta_first) * grad
        second_new = beta_second * second + (1.0 - beta_second) * grad * grad
        step_size = first_new / correct_first / (jnp.sqrt(second_new / correct_second) + adam_eps)
        weight = w[rows, :]
        nw_out[rows, :] = weight - learning * (step_size + decay_rate * weight)
        fnew_out[rows, :] = first_new
        snew_out[rows, :] = second_new

    first_abs, second_abs = jnp.abs(fnew_out[...]), jnp.abs(snew_out[...])
    st[0] = lane_rows(first_abs)
    st[1] = lane_rows(second_abs)
    for dy in range(1, NY):
        rcopy(st, y_in.at[NY - dy - 1], y_send, y_recv, y=mod(y + dy, NY)).start()
    cst[0, 0:1, :] = jnp.max(first_abs, axis=0, keepdims=True)
    cst[0, 1:2, :] = jnp.max(second_abs, axis=0, keepdims=True)
    for dx in range(1, NX):
        rcopy(cst.at[0], x_in.at[NX - dx - 1], x_send, x_recv, x=mod(x + dx, NX)).start()

    multiply(3, 0)
    send_grad(1)
    multiply(3, 1)
    send_grad(2)
    multiply(3, 2)

    def back_rows(i):
        rows, cols = pl.ds(128 * i, 128), pl.ds(0, 128 * (i + 1))
        total = acct[0, :, rows]
        for s in range(2):
            total = total + ga_in[s, :, rows].astype(F32)
        grad_half = total.astype(BF16).T
        grad_probs = lax.dot_general(grad_half, vv[cols, :], NT, preferred_element_type=F32)
        row_dot = jnp.sum(
            grad_half.astype(F32) * att[0, rows, :].astype(F32), axis=-1, keepdims=True
        )
        grad_scores = (prob[rows, cols] * (grad_probs - row_dot)).astype(BF16)
        gq_out[rows, :] = (
            jnp.dot(grad_scores, kk[cols, :], preferred_element_type=F32) * SCALE
        ).astype(BF16)

    came(x_in, x_recv)
    cst[1] = jnp.maximum(cst[0], jnp.max(x_in[...], axis=0))
    for sequence in (1, 2):
        o = other(sequence)
        rcopy(cst.at[1], zh_in.at[sequence_of(zh, o) - 1], zh_send, zh_recv, zh=o).start()
    came(y_in, y_recv)
    mine[...] = jnp.maximum(st[...], jnp.max(y_in[...], axis=0))
    for rel in range(1, NZL * NC):
        dl, dk = rel // NC, rel % NC
        back = NC * ((NZL - dl) % NZL) + dk - 1
        rcopy(
            mine, zl_in.at[back], zl_send, zl_recv, zl=mod(zl + dl, NZL), core=lax.rem(k + dk, NC)
        ).start()
    came(ga_in, ga_recv)
    for i in range(3):
        back_rows(i)
    came(zl_in, zl_recv)
    rows_out[...] = jnp.maximum(mine[...], jnp.max(zl_in[...], axis=0))
    came(zh_in, zh_recv)
    cols_out[...] = jnp.maximum(cst[1], jnp.max(zh_in[...], axis=0))

    def left(ref, send):
        rcopy(ref, ref, send, zh_recv, core=k).wait_send()

    wait_units(8 - sum(staying), 8, lambda c: left(gz.at[0:c], spread_send))
    for slot in range(SLOTS):
        wait_units(landing[slot], 9, lambda c: left(gz.at[0 : 3 * c], relay_send.at[slot]))
    longer = count(
        (from_source(way, hops) == NY - 1) & (k == 1)
        for slot in range(SLOTS)
        for way in (0, 1)
        for hops in range(reach(way, slot))
    )
    for c in range(9):
        pl.when(longer == c)(functools.partial(left, gz.at[0 : 56 * SLOTS + c], ring_send))
    for c in (0, 1):
        pl.when(k == c)(functools.partial(left, gz.at[0 : 64 * SLOTS + SLOTS * c], core_send))
    for whole, send in (
        (att.at[0:2], att_send),
        (wt.at[0:3], w_send),
        (ga_in, ga_send),
        (dw_in, dw_send),
        (y_in, y_send),
        (zl_in, zl_send),
        (x_in, x_send),
        (zh_in, zh_send),
    ):
        left(whole, send)


def codes(gq, nw, fnew, snew, rows, cols, gq_out, nw_out, nfc_out, nfr_out, nfcol_out, nsc_out, nsr_out, nscol_out):
    gq_out[...] = gq[...]
    nw_out[...] = nw[...]
    nfcol_out[...] = cols[0]
    nscol_out[...] = cols[1]
    for c, start, size in row_chunks():
        at = pl.ds(start, size)
        nfr_out[at] = rows[0, c, 0:size]
        nsr_out[at] = rows[1, c, 0:size]
        low_first = jnp.minimum(down_rows(rows[0, c : c + 1, :])[:size], cols[0:1])
        low_second = jnp.minimum(down_rows(rows[1, c : c + 1, :])[:size], cols[1:2])
        nfc_out[at, :] = (fnew[at, :] / (low_first + code_eps)).astype(BF16)
        nsc_out[at, :] = (snew[at, :] / (low_second + code_eps)).astype(BF16)


def per_device(queries, keys, values, grad_out, weight, fc, frow, fcol, sc, srow, scol):
    shape = jax.ShapeDtypeStruct
    vmem = pl.BlockSpec(memory_space=pltpu.VMEM)
    hbm = pl.BlockSpec(memory_space=pltpu.HBM)
    dma = pltpu.SemaphoreType.DMA
    gq, nw, fnew, snew, rows, cols = pl.pallas_call(
        body,
        name="whole",
        out_shape=(
            shape((SEQ, HD), BF16),
            shape((ROWS, HD), F32),
            shape((ROWS, HD), F32),
            shape((ROWS, HD), F32),
            shape((2, 8, HD), F32),
            shape((2, HD), F32),
        ),
        in_specs=[hbm] * 11,
        out_specs=[vmem] * 6,
        scratch_shapes=[
            pltpu.VMEM((SEQ, HD), BF16),
            pltpu.VMEM((SEQ, HD), BF16),
            pltpu.VMEM((SEQ, HD), BF16),
            pltpu.VMEM((SEQ, HD), BF16),
            pltpu.VMEM((ROWS, HD), F32),
            pltpu.VMEM((ROWS, HD), BF16),
            pltpu.VMEM((ROWS, HD), BF16),
            pltpu.VMEM((ROWS,), F32),
            pltpu.VMEM((HD,), F32),
            pltpu.VMEM((ROWS,), F32),
            pltpu.VMEM((HD,), F32),
            pltpu.VMEM((HD, SEQ), BF16),
            pltpu.VMEM((SLOTS * SLOT, UNIT, SEQ), BF16),
            pltpu.VMEM((NX, HD, ROWS), BF16),
            pltpu.VMEM((NZH, SEQ, HD), BF16),
            pltpu.VMEM((SEQ, SEQ), F32),
            pltpu.VMEM((NZH, HD, SEQ), F32),
            pltpu.VMEM((2, HD, SEQ), BF16),
            pltpu.VMEM((2, HD, SEQ), BF16),
            pltpu.VMEM((NX, ROWS, HD), F32),
            pltpu.VMEM((NX - 1, ROWS, HD), BF16),
            pltpu.VMEM((NX - 1, ROWS, HD), BF16),
            pltpu.VMEM((2, 8, HD), F32),
            pltpu.VMEM((NY - 1, 2, 8, HD), F32),
            pltpu.VMEM((NZL * NC - 1, 2, 8, HD), F32),
            pltpu.VMEM((2, 8, HD), F32),
            pltpu.VMEM((2, 2, HD), F32),
            pltpu.VMEM((NX - 1, 2, HD), F32),
            pltpu.VMEM((NZH - 1, 2, HD), F32),
            dma((11,)),
            dma,
            dma((SLOTS,)),
            dma((SLOTS,)),
            dma((SLOTS,)),
            dma,
            dma((2, SLOTS, 4, 2)),
            dma,
            dma((2, SLOTS, 5)),
            dma,
            dma((2,)),
            dma,
            dma,
            dma,
            dma,
            dma,
            dma,
            dma,
            dma,
            dma,
            dma,
            dma,
            dma,
            dma,
            dma,
        ],
        compiler_params=pltpu.CompilerParams(
            collective_id=0, has_side_effects=True, vmem_limit_bytes=48 * 1024 * 1024
        ),
    )(
        *(
            pltpu.with_memory_space_constraint(a, pltpu.HBM)
            for a in (queries, keys, values, grad_out, weight, fc, frow, fcol, sc, srow, scol)
        )
    )
    return pl.pallas_call(
        codes,
        name="codes",
        out_shape=(
            shape((SEQ, HD), BF16),
            shape((ROWS, HD), F32),
            shape((ROWS, HD), BF16),
            shape((ROWS,), F32),
            shape((HD,), F32),
            shape((ROWS, HD), BF16),
            shape((ROWS,), F32),
            shape((HD,), F32),
        ),
        compiler_params=pltpu.CompilerParams(vmem_limit_bytes=8 * 1024 * 1024),
        in_specs=[vmem] * 6,
        out_specs=[vmem] * 8,
    )(gq, nw, fnew, snew, rows, cols)


def solution(mesh):
    finer = Mesh(mesh.devices.reshape(NX, NZH, NY, NZL, NC), AXES)
    placed = (
        P(DP, TENSOR),
        P(DP, None),
        P(DP, None),
        P(DP, TENSOR),
        P(DP, TENSOR),
        P(DP, TENSOR),
        P(DP),
        P(TENSOR),
        P(DP, TENSOR),
        P(DP),
        P(TENSOR),
    )
    return jax.shard_map(
        per_device,
        mesh=finer,
        in_specs=placed,
        out_specs=(
            P(DP, TENSOR),
            P(DP, TENSOR),
            P(DP, TENSOR),
            P(DP),
            P(TENSOR),
            P(DP, TENSOR),
            P(DP),
            P(TENSOR),
        ),
        check_vma=False,
    )
```

time: 94.8 us -> 95.7 us (level); the launches traced: 94.6 us -> 94.5 us
  no operation moved by 1% of the time
where the time goes in v6:
time: 95.7 us; the launch traced here: 94.5 us
  Pallas kernels  93.9 us (98%)
    pallas_call x1, Pallas kernels, per_device(): pl.pallas_call(body, name='whole', out_shape=(shape((SEQ, HD), BF16), sha...  92.8 us

profile of v6, /device:TPU:1, one launch (start us, length us, event | category | flops | bytes accessed | tf_op | source)
XLA Modules:
  0.0 94.5 jit_solution(1734614275711862345)
XLA Ops:
  0.6 92.8 %whole.1 = (bf16[384,128]{1,0:T(8,128)(2,1)S(1)}, f32[688,128]{1,0:T(8,128)S(1)}, f32[688,128]{1,0:T(8,128)S(1)}, f32[688,128]{1,0:T(8,128)S(1)}, f32[2,8,128]{2,1,0:T(8,128)S(1)}, /*index=5*/f32[2,128]{1,0:T(2,128)S(1)}) custom-call(bf16[384,128]{1,0:T(8,128)(2,1)} %q_hbm.1, bf16[384,1024]{1,0:T(8,128)(2,1)} %k_hbm.1, bf16[384,1024]{1,0:T(8,128)(2,1)} %v_hbm.1, ...), custom_call_target="tpu_custom_call" | custom-call | tf_op jit(solution)/shard_map/whole/pallas_call | solution.py:650
  93.4 1.1 %codes.1 = (bf16[384,128]{1,0:T(8,128)(2,1)}, f32[688,128]{1,0:T(8,128)}, bf16[688,128]{1,0:T(8,128)(2,1)}, f32[688]{0:T(1024)}, f32[128]{0:T(128)}, /*index=5*/...) custom-call(bf16[384,128]{1,0:T(8,128)(2,1)S(1)} %get-tuple-element.14.gq, f32[688,128]{1,0:T(8,128)S(1)} %get-tuple-element.15.nw, ...), custom_call_target="tpu_custom_call" | custom-call | tf_op jit(solution)/shard_map/codes/pallas_call | solution.py:728

commit v7 on v6

--- a/solution.py
+++ b/solution.py
@@ -190,57 +190,77 @@
     def rows_of(u):
         return pl.ds(pl.multiple_of(UNIT * u, UNIT), UNIT)
 
-    def goes_to(u):
-        unit = 8 * t + u
-        d = lax.div(unit, UNITS)
-        xd, zd = lax.div(d, NZH), lax.rem(d, NZH)
-        ahead = mod(xd - x, NX)
-        sequence = sequence_of(zh, zd)
-        turn = 2 * (ahead - 1) + sequence - 1
-        slot = jnp.where(ahead == 0, 3, jnp.where(sequence == 0, 0, 1 + lax.div(turn + 3, 3) - 1))
+    def slot_and_index(ahead, sequence):
+        turn = 2 * ahead + sequence
+        far = (turn >= 6).astype(jnp.int32)
+        slot = jnp.where(ahead == 0, 3, jnp.where(sequence == 0, 0, 1 + far))
         index = jnp.where(
             ahead == 0,
-            lax.rem(sequence + 2, 3),
-            jnp.where(sequence == 0, ahead - 1, lax.rem(turn + 3, 3)),
-        )
-        e = UNITS * index + unit - UNITS * d
-        h = jnp.minimum(lax.div(e, 8), HOMES - 1)
+            sequence - 1 + 3 * (sequence == 0).astype(jnp.int32),
+            jnp.where(sequence == 0, ahead - 1, turn - 3 - 3 * far),
+        )
+        return slot, index
+
+    first_owner = lax.div(8 * t, UNITS)
+    first_row = 8 * t - UNITS * first_owner
+    turnover = UNITS - first_row
+    sides = []
+    for owner in (first_owner, first_owner + 1):
+        xd = lax.div(owner, NZH)
+        zd = owner - NZH * xd
+        slot, index = slot_and_index(mod(xd - x, NX), sequence_of(zh, zd))
+        sides.append((zd, slot, UNITS * index))
+
+    def goes_to(u):
+        over = u >= turnover
+        zd, slot, start = (jnp.where(over, b, a) for a, b in zip(*sides))
+        e = start + first_row + u - jnp.where(over, UNITS, 0)
+        h = jnp.minimum(lax.shift_right_logical(e, 3), HOMES - 1)
         home = dict(
             zh=zd,
-            y=lax.div(h, 2),
-            zl=lax.rem(zl + 2 * lax.rem(u, 2), NZL),
-            core=lax.rem(h, 2),
+            y=lax.shift_right_logical(h, 1),
+            zl=zl ^ (2 * (u & 1)),
+            core=h & 1,
         )
         here = (zd == zh) & (h == me) & (home["zl"] == zl)
         return slot, SLOT * slot + e, home, here
 
-    def unit_of(slot, j):
-        e = 8 * me + j
-        index, r = lax.div(e, UNITS), lax.rem(e, UNITS)
-        if slot == 0:
-            xd, z = mod(x + 1 + index, NX), zh
-        elif slot == 3:
-            xd, z = x, jnp.where(index == 2, zh, other(index + 1))
-        else:
-            turn = 3 * (slot - 1) + index
-            xd, z = mod(x + 1 + lax.div(turn, 2), NX), other(1 + lax.rem(turn, 2))
-        unit = UNITS * (NZH * xd + zh) + r
-        mine_too = (j < 8) | (me == HOMES - 1)
-        return z, lax.div(unit, 8), lax.rem(unit, 8), mine_too & (unit < ALL_UNITS), mine_too
-
-    def lands_here(slot, j):
-        z, column, u, there, _ = unit_of(slot, j)
-        line = lax.rem(lax.rem(lax.div(column, 2), NZL) + 2 * lax.rem(u, 2), NZL)
-        return there & (line == zl), there & (line != zl), (z == zh) & (column == t)
+    first_index = lax.div(8 * me, UNITS)
+    first_place = 8 * me - UNITS * first_index
+    has_last = me == HOMES - 1
+    units = []
+    for slot in range(SLOTS):
+        blocks = []
+        for index in (first_index, first_index + 1):
+            if slot == 0:
+                xd, z = (x + 1 + index) & 3, zh
+            elif slot == 3:
+                xd, z = x, jnp.where(index == 2, zh, other(index + 1))
+            else:
+                turn = 3 * (slot - 1) + index
+                xd, z = (x + 1 + lax.shift_right_logical(turn, 1)) & 3, other(1 + (turn & 1))
+            blocks.append((z, UNITS * (NZH * xd + zh)))
+        held = []
+        for j in range(9):
+            over = first_place + j >= UNITS
+            z, start = (jnp.where(over, b, a) for a, b in zip(*blocks))
+            unit = start + first_place + j - jnp.where(over, UNITS, 0)
+            column = lax.shift_right_logical(unit, 3)
+            line = lax.shift_right_logical(column, 1) & 3
+            there = unit < ALL_UNITS
+            if j == 8:
+                there = there & has_last
+            here = (line ^ (2 * (unit & 1))) == zl
+            source = dict(zh=z, y=lax.shift_right_logical(column, 3), zl=line, core=column & 1)
+            held.append((there, there & here, source, (z == zh) & (column == t)))
+        units.append(held)
 
     def count(flags):
         return sum(f.astype(jnp.int32) for f in flags)
 
-    landing = [count(lands_here(s, j)[0] for j in range(9)) for s in range(SLOTS)]
-    coming = [count(lands_here(s, j)[1] for j in range(9)) for s in range(SLOTS)]
-    staying = [
-        count(lands_here(s, j)[0] & lands_here(s, j)[2] for j in range(9)) for s in range(SLOTS)
-    ]
+    landing = [count(lands for _, lands, _, _ in held) for held in units]
+    coming = [count(there for there, _, _, _ in held) - n for held, n in zip(units, landing)]
+    staying = [count(lands & same for _, lands, _, same in held) for held in units]
 
     barrier = pltpu.get_barrier_semaphore()
 
@@ -252,19 +272,10 @@
         pl.when(jnp.logical_not(here))(functools.partial(greet, **home))
         return carry
 
-    def greet_sources(slot, j, carry):
-        z, column, u, there, _ = unit_of(slot, j)
-        lands, _, same = lands_here(slot, j)
-
-        @pl.when(lands & jnp.logical_not(same))
-        def _():
-            greet(zh=z, y=lax.div(column, 8), zl=lax.rem(lax.div(column, 2), NZL), core=lax.rem(column, 2))
-
-        return carry
-
     lax.fori_loop(0, 8, greet_home, 0)
-    for slot in range(SLOTS):
-        lax.fori_loop(0, 9, functools.partial(greet_sources, slot), 0)
+    for held in units:
+        for _, lands, source, same in held:
+            pl.when(lands & jnp.logical_not(same))(functools.partial(greet, **source))
     for dz in (1, 2):
         greet(zh=mod(zh + dz, NZH))
     for dx in range(1, NX):
@@ -278,18 +289,13 @@
     loads[0].wait()
     gt[...] = g[...].T
 
-    for slot in range(SLOTS):
-
-        def clear(j, carry):
-            _, _, _, there, mine_too = unit_of(slot, j)
-
-            @pl.when(mine_too & jnp.logical_not(there))
+    for slot, held in enumerate(units):
+        for j, (there, _, _, _) in enumerate(held):
+            missing = jnp.logical_not(there)
+
+            @pl.when(missing & has_last if j == 8 else missing)
             def _():
                 gz[SLOT * slot + 8 * me + j] = jnp.zeros((UNIT, SEQ), BF16)
-
-            return carry
-
-        lax.fori_loop(0, 9, clear, 0)
 
     pl.semaphore_wait(barrier, greeted)
 
@@ -350,19 +356,15 @@
             landing[slot] - staying[slot], 9, functools.partial(units_came, far_recv.at[slot])
         )
 
-        def give(j, carry):
+        for j, (_, lands, _, _) in enumerate(units[slot]):
             piece = gz.at[SLOT * slot + 8 * me + j]
 
-            @pl.when(lands_here(slot, j)[0])
+            @pl.when(lands)
             def _():
                 for dl in (1, 3, 2):
                     rcopy(
                         piece, piece, relay_send.at[slot], near_recv.at[slot], zl=mod(zl + dl, NZL)
                     ).start()
-
-            return carry
-
-        lax.fori_loop(0, 9, give, 0)
 
     def reach(way, slot):
         return 4 if way == slot % 2 else 3
@@ -479,50 +481,52 @@
     pass_on(0, 1)
     start_ring(1)
     pass_on(0, 2)
+    pass_on(1, 1)
+    pass_on(0, 3)
     start_ring(2)
     send_att()
-    pass_on(1, 1)
-    pass_on(0, 3)
+    pass_on(1, 2)
+    pass_on(2, 1)
+    pass_on(1, 3)
+    pass_on(2, 2)
     start_ring(3)
-    pass_on(2, 1)
-    pass_on(1, 2)
     pass_on(0, 4)
-    pass_on(3, 1)
+    pass_on(2, 3)
     partner_has(0)
     weight_term(0, 0)
     weight_term(0, 1)
-    pass_on(2, 2)
+    pass_on(3, 1)
     weight_term(0, 2)
     came(wt.at[0:3], w_recv)
     multiply(0, 0)
-    pass_on(1, 3)
     multiply(0, 1)
     multiply(0, 2)
     pass_on(1, 4)
-    pass_on(3, 2)
     came(att.at[1], att_recv.at[0])
     came(att.at[2], att_recv.at[1])
     partner_has(1)
     weight_term(1, 0)
     weight_term(1, 1)
     send_term(0)
-    pass_on(2, 3)
+    pass_on(3, 2)
     weight_term(1, 2)
-    multiply(1, 0)
-    multiply(1, 1)
     pass_on(2, 4)
-    multiply(1, 2)
-    pass_on(3, 3)
     partner_has(2)
     weight_term(2, 0)
     send_term(1)
     weight_term(2, 1)
     weight_term(2, 2)
     send_term(2)
+    pass_on(3, 3)
+    for slot in (1, 2):
+        for index in range(3):
+            multiply(slot, index)
     pass_on(3, 4)
-    for index in range(3):
-        multiply(2, index)
     partner_has(3)
+    multiply(3, 0)
+    send_grad(1)
+    multiply(3, 1)
+    send_grad(2)
     for index in range(3):
         weight_term(3, index)
 
@@ -556,10 +560,6 @@
     for dx in range(1, NX):
         rcopy(cst.at[0], x_in.at[NX - dx - 1], x_send, x_recv, x=mod(x + dx, NX)).start()
 
-    multiply(3, 0)
-    send_grad(1)
-    multiply(3, 1)
-    send_grad(2)
     multiply(3, 2)
 
     def back_rows(i):

time: 95.7 us -> 87.5 us (0.914); the launches traced: 94.5 us -> 87.3 us
  Pallas kernels: 93.9 us -> 86.7 us
    pallas_call x1, Pallas kernels: 92.8 us -> 85.6 us  [per_device(): pl.pallas_call(body, name='whole', out_shape=(shape((SEQ, HD), BF16), sha...]
where the time goes in v7:
time: 87.5 us; the launch traced here: 87.3 us
  Pallas kernels  86.7 us (99%)
    pallas_call x1, Pallas kernels, per_device(): pl.pallas_call(body, name='whole', out_shape=(shape((SEQ, HD), BF16), sha...  85.6 us

profile of v7, /device:TPU:1, one launch (start us, length us, event | category | flops | bytes accessed | tf_op | source)
XLA Modules:
  0.0 87.3 jit_solution(16841385639105642136)
XLA Ops:
  0.6 85.6 %whole.1 = (bf16[384,128]{1,0:T(8,128)(2,1)S(1)}, f32[688,128]{1,0:T(8,128)S(1)}, f32[688,128]{1,0:T(8,128)S(1)}, f32[688,128]{1,0:T(8,128)S(1)}, f32[2,8,128]{2,1,0:T(8,128)S(1)}, /*index=5*/f32[2,128]{1,0:T(2,128)S(1)}) custom-call(bf16[384,128]{1,0:T(8,128)(2,1)} %q_hbm.1, bf16[384,1024]{1,0:T(8,128)(2,1)} %k_hbm.1, bf16[384,1024]{1,0:T(8,128)(2,1)} %v_hbm.1, ...), custom_call_target="tpu_custom_call" | custom-call | tf_op jit(solution)/shard_map/whole/pallas_call | solution.py:650
  86.2 1.1 %codes.1 = (bf16[384,128]{1,0:T(8,128)(2,1)}, f32[688,128]{1,0:T(8,128)}, bf16[688,128]{1,0:T(8,128)(2,1)}, f32[688]{0:T(1024)}, f32[128]{0:T(128)}, /*index=5*/...) custom-call(bf16[384,128]{1,0:T(8,128)(2,1)S(1)} %get-tuple-element.14.gq, f32[688,128]{1,0:T(8,128)S(1)} %get-tuple-element.15.nw, ...), custom_call_target="tpu_custom_call" | custom-call | tf_op jit(solution)/shard_map/codes/pallas_call | solution.py:728

commit v8 on v7

--- a/solution.py
+++ b/solution.py
@@ -23,6 +23,8 @@
 HOMES = NY * NC
 SLOTS = 4
 SLOT = 3 * UNITS
+SPLIT = (0,)
+AHEAD = (2, 1, 3)
 SCALE = HD ** (-0.5)
 
 beta_first = 0.9
@@ -126,6 +128,9 @@
     near_recv,
     ring_send,
     ring_recv,
+    beside_send,
+    beside_recv,
+    shared_recv,
     core_send,
     core_recv,
     att_send,
@@ -185,19 +190,37 @@
     for load in loads:
         load.start()
 
+    barrier = pltpu.get_barrier_semaphore()
+
+    def greet(**dev):
+        pl.semaphore_signal(barrier, inc=1, device_id=dev, device_id_type=MESH)
+
+    for dz in (1, 2):
+        greet(zh=mod(zh + dz, NZH))
+    for dx in range(1, NX):
+        greet(x=mod(x + dx, NX))
+    for dy in range(1, NY):
+        greet(y=mod(y + dy, NY))
+    for rel in range(1, NZL * NC):
+        greet(zl=mod(zl + rel // NC, NZL), core=lax.rem(k + rel % NC, NC))
     me = 2 * y + k
+    side = zl & 1
 
     def rows_of(u):
         return pl.ds(pl.multiple_of(UNIT * u, UNIT), UNIT)
 
+    def ahead_of(turn):
+        return jnp.where(turn == 0, 2, 2 * turn - 1)
+
     def slot_and_index(ahead, sequence):
-        turn = 2 * ahead + sequence
-        far = (turn >= 6).astype(jnp.int32)
+        turn = jnp.where(ahead == 2, 0, lax.shift_right_logical(ahead + 1, 1))
+        pair = 2 * turn + sequence - 1
+        far = (pair >= 3).astype(jnp.int32)
         slot = jnp.where(ahead == 0, 3, jnp.where(sequence == 0, 0, 1 + far))
         index = jnp.where(
             ahead == 0,
             sequence - 1 + 3 * (sequence == 0).astype(jnp.int32),
-            jnp.where(sequence == 0, ahead - 1, turn - 3 - 3 * far),
+            jnp.where(sequence == 0, turn, pair - 3 * far),
         )
         return slot, index
 
@@ -216,12 +239,11 @@
         zd, slot, start = (jnp.where(over, b, a) for a, b in zip(*sides))
         e = start + first_row + u - jnp.where(over, UNITS, 0)
         h = jnp.minimum(lax.shift_right_logical(e, 3), HOMES - 1)
-        home = dict(
-            zh=zd,
-            y=lax.shift_right_logical(h, 1),
-            zl=zl ^ (2 * (u & 1)),
-            core=h & 1,
-        )
+        line = zl ^ (2 * (u & 1))
+        for split in SPLIT:
+            shared = (zl & 2) + (e - 8 * h >= 4).astype(jnp.int32)
+            line = jnp.where(slot == split, shared, line)
+        home = dict(zh=zd, y=lax.shift_right_logical(h, 1), zl=line, core=h & 1)
         here = (zd == zh) & (h == me) & (home["zl"] == zl)
         return slot, SLOT * slot + e, home, here
 
@@ -233,12 +255,13 @@
         blocks = []
         for index in (first_index, first_index + 1):
             if slot == 0:
-                xd, z = (x + 1 + index) & 3, zh
+                xd, z = (x + ahead_of(index)) & 3, zh
             elif slot == 3:
                 xd, z = x, jnp.where(index == 2, zh, other(index + 1))
             else:
                 turn = 3 * (slot - 1) + index
-                xd, z = (x + 1 + lax.shift_right_logical(turn, 1)) & 3, other(1 + (turn & 1))
+                xd = (x + ahead_of(lax.shift_right_logical(turn, 1))) & 3
+                z = other(1 + (turn & 1))
             blocks.append((z, UNITS * (NZH * xd + zh)))
         held = []
         for j in range(9):
@@ -248,24 +271,25 @@
             column = lax.shift_right_logical(unit, 3)
             line = lax.shift_right_logical(column, 1) & 3
             there = unit < ALL_UNITS
+            missing = jnp.logical_not(there)
             if j == 8:
-                there = there & has_last
-            here = (line ^ (2 * (unit & 1))) == zl
+                there, missing = there & has_last, missing & has_last
+            if slot in SPLIT:
+                taken = side == min(j // 4, 1)
+                there, missing = there & taken, missing & taken
+                here = (line & 2) == (zl & 2)
+            else:
+                here = (line ^ (2 * (unit & 1))) == zl
             source = dict(zh=z, y=lax.shift_right_logical(column, 3), zl=line, core=column & 1)
-            held.append((there, there & here, source, (z == zh) & (column == t)))
+            held.append((there, there & here, source, (z == zh) & (column == t), missing))
         units.append(held)
 
     def count(flags):
         return sum(f.astype(jnp.int32) for f in flags)
 
-    landing = [count(lands for _, lands, _, _ in held) for held in units]
-    coming = [count(there for there, _, _, _ in held) - n for held, n in zip(units, landing)]
-    staying = [count(lands & same for _, lands, _, same in held) for held in units]
-
-    barrier = pltpu.get_barrier_semaphore()
-
-    def greet(**dev):
-        pl.semaphore_signal(barrier, inc=1, device_id=dev, device_id_type=MESH)
+    landing = [count(lands for _, lands, _, _, _ in held) for held in units]
+    coming = [count(there for there, _, _, _, _ in held) - n for held, n in zip(units, landing)]
+    staying = [count(lands & same for _, lands, _, same, _ in held) for held in units]
 
     def greet_home(u, carry):
         slot, place, home, here = goes_to(u)
@@ -274,26 +298,17 @@
 
     lax.fori_loop(0, 8, greet_home, 0)
     for held in units:
-        for _, lands, source, same in held:
+        for _, lands, source, same, _ in held:
             pl.when(lands & jnp.logical_not(same))(functools.partial(greet, **source))
-    for dz in (1, 2):
-        greet(zh=mod(zh + dz, NZH))
-    for dx in range(1, NX):
-        greet(x=mod(x + dx, NX))
-    for dy in range(1, NY):
-        greet(y=mod(y + dy, NY))
-    for rel in range(1, NZL * NC):
-        greet(zl=mod(zl + rel // NC, NZL), core=lax.rem(k + rel % NC, NC))
     greeted = 8 + sum(landing) - 2 * sum(staying) + 2 + 3 + 7 + 7
 
     loads[0].wait()
     gt[...] = g[...].T
 
     for slot, held in enumerate(units):
-        for j, (there, _, _, _) in enumerate(held):
-            missing = jnp.logical_not(there)
-
-            @pl.when(missing & has_last if j == 8 else missing)
+        for j, (_, _, _, _, missing) in enumerate(held):
+
+            @pl.when(missing)
             def _():
                 gz[SLOT * slot + 8 * me + j] = jnp.zeros((UNIT, SEQ), BF16)
 
@@ -318,7 +333,7 @@
     loads[4].wait()
     wt[3] = w[...].astype(BF16).T
     for dx in (1, 3, 2):
-        rcopy(wt.at[3], wt.at[NX - 1 - dx], w_send, w_recv, x=mod(x + dx, NX)).start()
+        rcopy(wt.at[3], wt.at[AHEAD.index(NX - dx)], w_send, w_recv, x=mod(x + dx, NX)).start()
 
     for i in (1, 2, 3):
         loads[i].wait()
@@ -356,16 +371,19 @@
             landing[slot] - staying[slot], 9, functools.partial(units_came, far_recv.at[slot])
         )
 
-        for j, (_, lands, _, _) in enumerate(units[slot]):
+        for j, (_, lands, _, _, _) in enumerate(units[slot]):
             piece = gz.at[SLOT * slot + 8 * me + j]
 
             @pl.when(lands)
             def _():
-                for dl in (1, 3, 2):
+                for dl in (2,) if slot in SPLIT else (1, 3, 2):
                     rcopy(
                         piece, piece, relay_send.at[slot], near_recv.at[slot], zl=mod(zl + dl, NZL)
                     ).start()
 
+    def parts(slot):
+        return (0, 1) if slot == SLOTS - 1 else (0,)
+
     def reach(way, slot):
         return 4 if way == slot % 2 else 3
 
@@ -375,6 +393,12 @@
     def parts_of(slot, source, core):
         start = SLOT * slot + 8 * (2 * source + core)
         last = (source == NY - 1) & (core == 1)
+        if slot in SPLIT:
+            longer = last & (side == 1)
+            start = start + 4 * side
+            return (((start, 4, jnp.logical_not(longer)), (start, 5, longer)),)
+        if len(parts(slot)) == 1:
+            return (((start, 8, jnp.logical_not(last)), (start, 9, last)),)
         return (
             ((start, 4, None),),
             ((start + 4, 4, jnp.logical_not(last)), (start + 4, 5, last)),
@@ -402,20 +426,28 @@
 
     def to_partner(way, slot, hops, part):
         def go(piece):
-            rcopy(piece, piece, core_send, core_recv.at[way, slot, hops], core=1 - k).start()
+            rcopy(piece, piece, core_send, core_recv.at[slot, hops // 4], core=1 - k).start()
 
         each_size(parts_of(slot, from_source(way, hops), k)[part], go)
+
+    def to_beside(way, slot, hops):
+        def go(piece):
+            rcopy(piece, piece, beside_send, beside_recv.at[slot], zl=zl ^ 1).start()
+
+        if slot in SPLIT:
+            each_size(parts_of(slot, from_source(way, hops), k)[0], go)
 
     def start_ring(slot):
         wait_units(coming[slot], 9, functools.partial(units_came, near_recv.at[slot]))
-        for part in (0, 1):
+        for part in parts(slot):
             for way in (0, 1):
                 forward(way, slot, 0, part)
-        for part in (0, 1):
+        to_beside(0, slot, 0)
+        for part in parts(slot):
             to_partner(0, slot, 0, part)
 
     def pass_on(slot, hops):
-        for part in (0, 1):
+        for part in parts(slot):
             for way in (0, 1):
                 if hops <= reach(way, slot):
                     each_size(
@@ -424,16 +456,50 @@
                     )
                     if hops < reach(way, slot):
                         forward(way, slot, hops, part)
+                    to_beside(way, slot, hops)
                     to_partner(way, slot, hops, part)
 
+    def beside_came(slot):
+        longer = (k == 1) & (side == 0)
+        pl.when(longer)(functools.partial(came, gz.at[0:33], beside_recv.at[slot]))
+        pl.when(jnp.logical_not(longer))(functools.partial(came, gz.at[0:32], beside_recv.at[slot]))
+        for source in range(NY):
+            start = SLOT * slot + 8 * (2 * source + k) + 4 * (1 - side)
+
+            def go(units):
+                piece = gz.at[pl.ds(start, units)]
+                rcopy(piece, piece, core_send, shared_recv.at[slot], core=1 - k).start()
+
+            if source < NY - 1:
+                go(4)
+            else:
+                pl.when(longer)(functools.partial(go, 5))
+                pl.when(jnp.logical_not(longer))(functools.partial(go, 4))
+
+    def partner_beside(slot):
+        longer = (k == 0) & (side == 0)
+        pl.when(longer)(functools.partial(came, gz.at[0:33], shared_recv.at[slot]))
+        pl.when(jnp.logical_not(longer))(functools.partial(came, gz.at[0:32], shared_recv.at[slot]))
+
+    def partner_near(slot):
+        more = (k == 0) & (y != NY // 2 - 1)
+        each = 8
+        if slot in SPLIT:
+            more, each = more & (side == 1), 4
+        pl.when(more)(functools.partial(came, gz.at[0 : 7 * each + 1], core_recv.at[slot, 0]))
+        pl.when(jnp.logical_not(more))(functools.partial(came, gz.at[0 : 7 * each], core_recv.at[slot, 0]))
+
+    def partner_across(slot):
+        more = (k == 0) & (y == NY // 2 - 1)
+        each = 8
+        if slot in SPLIT:
+            more, each = more & (side == 1), 4
+        pl.when(more)(functools.partial(came, gz.at[0 : each + 1], core_recv.at[slot, 1]))
+        pl.when(jnp.logical_not(more))(functools.partial(came, gz.at[0:each], core_recv.at[slot, 1]))
+
     def partner_has(slot):
-        for hops in range(5):
-            for way in (0, 1):
-                if (hops > 0 or way == 0) and hops <= reach(way, slot):
-                    last = (from_source(way, hops) == NY - 1) & (k == 0)
-                    recv = core_recv.at[way, slot, hops]
-                    pl.when(last)(functools.partial(came, gz.at[0:9], recv))
-                    pl.when(jnp.logical_not(last))(functools.partial(came, gz.at[0:8], recv))
+        partner_near(slot)
+        partner_across(slot)
 
     def block_of(slot, index):
         return gz[pl.ds(SLOT * slot + UNITS * index, UNITS)].reshape(ROWS, SEQ)
@@ -460,10 +526,26 @@
         acct[sequence] = acct[sequence] + term if ("g", sequence) in started else term
         started.add(("g", sequence))
 
+    early = jnp.where(lax.rem(y + NY // 2, NY) <= 2, 2, 0)
+    last_blocks = (early, jnp.where(early == 2, 0, 1), jnp.where(early == 2, 1, 2))
+
+    def last_term(turn):
+        index = last_blocks[turn]
+        term = jnp.dot(
+            block_of(SLOTS - 1, index), att[lax.rem(index + 1, NZH)], preferred_element_type=F32
+        )
+        dwacc[3] = dwacc[3] + term if turn > 0 else term
+
+    def last_multiply(turn):
+        index = last_blocks[turn]
+        term = jnp.dot(wt[3], block_of(SLOTS - 1, index), preferred_element_type=F32)
+        sequence = lax.rem(index + 1, NZH)
+        acct[sequence] = acct[sequence] + term
+
     def send_term(rows):
         dw_stage[rows] = dwacc[rows].astype(BF16)
         rcopy(
-            dw_stage.at[rows], dw_in.at[NX - 2 - rows], dw_send, dw_recv, x=mod(x + 1 + rows, NX)
+            dw_stage.at[rows], dw_in.at[rows], dw_send, dw_recv, x=mod(x + AHEAD[rows], NX)
         ).start()
 
     def send_grad(sequence):
@@ -472,6 +554,18 @@
         rcopy(
             ga_stage.at[sequence - 1], ga_in.at[sequence_of(zh, o) - 1], ga_send, ga_recv, zh=o
         ).start()
+
+    def old_moments():
+        for load in loads[5:]:
+            load.wait()
+        for c, start, size in row_chunks():
+            rows = pl.ds(start, size)
+            low_first = jnp.minimum(down(frow, start, size), fcol[...].reshape(1, HD))
+            low_second = jnp.minimum(down(srow, start, size), scol[...].reshape(1, HD))
+            fnew_out[rows, :] = beta_first * (fc[rows, :].astype(F32) * low_first)
+            snew_out[rows, :] = beta_second * (sc[rows, :].astype(F32) * low_second)
+            weight = w[rows, :]
+            nw_out[rows, :] = weight - learning * (decay_rate * weight)
 
     relay(0)
     start_ring(0)
@@ -482,71 +576,75 @@
     start_ring(1)
     pass_on(0, 2)
     pass_on(1, 1)
-    pass_on(0, 3)
     start_ring(2)
     send_att()
+    pass_on(0, 3)
     pass_on(1, 2)
     pass_on(2, 1)
+    start_ring(3)
+    pass_on(0, 4)
     pass_on(1, 3)
     pass_on(2, 2)
-    start_ring(3)
-    pass_on(0, 4)
+    old_moments()
+    pass_on(3, 1)
+    pass_on(1, 4)
+    beside_came(0)
     pass_on(2, 3)
+    partner_has(1)
     partner_has(0)
-    weight_term(0, 0)
-    weight_term(0, 1)
-    pass_on(3, 1)
-    weight_term(0, 2)
+    partner_beside(0)
     came(wt.at[0:3], w_recv)
     multiply(0, 0)
-    multiply(0, 1)
-    multiply(0, 2)
-    pass_on(1, 4)
     came(att.at[1], att_recv.at[0])
     came(att.at[2], att_recv.at[1])
-    partner_has(1)
     weight_term(1, 0)
+    multiply(0, 2)
+    pass_on(3, 2)
     weight_term(1, 1)
+    weight_term(0, 0)
     send_term(0)
-    pass_on(3, 2)
+    weight_term(0, 2)
+    pass_on(2, 4)
+    multiply(1, 1)
     weight_term(1, 2)
-    pass_on(2, 4)
+    weight_term(0, 1)
     partner_has(2)
+    pass_on(3, 3)
     weight_term(2, 0)
     send_term(1)
     weight_term(2, 1)
     weight_term(2, 2)
     send_term(2)
-    pass_on(3, 3)
-    for slot in (1, 2):
-        for index in range(3):
-            multiply(slot, index)
+    multiply(2, 0)
+    multiply(1, 2)
+    partner_near(3)
+    last_term(0)
     pass_on(3, 4)
-    partner_has(3)
-    multiply(3, 0)
+    multiply(0, 1)
+    last_multiply(0)
+    multiply(2, 1)
+    multiply(2, 2)
+    multiply(1, 0)
+    partner_across(3)
+    last_multiply(1)
+    last_multiply(2)
     send_grad(1)
-    multiply(3, 1)
     send_grad(2)
-    for index in range(3):
-        weight_term(3, index)
-
-    for load in loads[5:]:
-        load.wait()
+    last_term(1)
+    last_term(2)
+
     came(dw_in, dw_recv)
     for c, start, size in row_chunks():
         rows = pl.ds(start, size)
         grad = dwacc[3, rows, :]
         for i in range(NX - 1):
             grad = grad + dw_in[i, rows, :].astype(F32)
-        low_first = jnp.minimum(down(frow, start, size), fcol[...].reshape(1, HD))
-        low_second = jnp.minimum(down(srow, start, size), scol[...].reshape(1, HD))
-        first = fc[rows, :].astype(F32) * low_first
-        second = sc[rows, :].astype(F32) * low_second
-        first_new = beta_first * first + (1.0 - beta_first) * grad
-        second_new = beta_second * second + (1.0 - beta_second) * grad * grad
-        step_size = first_new / correct_first / (jnp.sqrt(second_new / correct_second) + adam_eps)
-        weight = w[rows, :]
-        nw_out[rows, :] = weight - learning * (step_size + decay_rate * weight)
+        first_new = fnew_out[rows, :] + (1.0 - beta_first) * grad
+        second_new = snew_out[rows, :] + (1.0 - beta_second) * grad * grad
+        step_size = (
+            first_new * (1.0 / correct_first) / (jnp.sqrt(second_new * (1.0 / correct_second)) + adam_eps)
+        )
+        nw_out[rows, :] = nw_out[rows, :] - learning * step_size
         fnew_out[rows, :] = first_new
         snew_out[rows, :] = second_new
 
@@ -559,8 +657,6 @@
     cst[0, 1:2, :] = jnp.max(second_abs, axis=0, keepdims=True)
     for dx in range(1, NX):
         rcopy(cst.at[0], x_in.at[NX - dx - 1], x_send, x_recv, x=mod(x + dx, NX)).start()
-
-    multiply(3, 2)
 
     def back_rows(i):
         rows, cols = pl.ds(128 * i, 128), pl.ds(0, 128 * (i + 1))
@@ -603,15 +699,20 @@
 
     wait_units(8 - sum(staying), 8, lambda c: left(gz.at[0:c], spread_send))
     for slot in range(SLOTS):
-        wait_units(landing[slot], 9, lambda c: left(gz.at[0 : 3 * c], relay_send.at[slot]))
+        copies = 1 if slot in SPLIT else 3
+        wait_units(landing[slot], 9, lambda c: left(gz.at[0 : copies * c], relay_send.at[slot]))
     longer = count(
-        (from_source(way, hops) == NY - 1) & (k == 1)
+        (from_source(way, hops) == NY - 1) & (k == 1) & ((side == 1) | (slot not in SPLIT))
         for slot in range(SLOTS)
         for way in (0, 1)
         for hops in range(reach(way, slot))
     )
+    usual = 56 * SLOTS - 28 * len(SPLIT)
     for c in range(9):
-        pl.when(longer == c)(functools.partial(left, gz.at[0 : 56 * SLOTS + c], ring_send))
+        pl.when(longer == c)(functools.partial(left, gz.at[0 : usual + c], ring_send))
+    more = (k == 1) & (side == 1)
+    for flag, each in ((more, 33), (jnp.logical_not(more), 32)):
+        pl.when(flag)(functools.partial(left, gz.at[0 : each * len(SPLIT)], beside_send))
     for c in (0, 1):
         pl.when(k == c)(functools.partial(left, gz.at[0 : 64 * SLOTS + SLOTS * c], core_send))
     for whole, send in (
@@ -698,7 +799,10 @@
             dma,
             dma((2, SLOTS, 4, 2)),
             dma,
-            dma((2, SLOTS, 5)),
+            dma((SLOTS,)),
+            dma((SLOTS,)),
+            dma,
+            dma((SLOTS, 2)),
             dma,
             dma((2,)),
             dma,

time: 87.5 us -> 83.7 us (0.957)
  Pallas kernels: 86.7 us -> 82.9 us
    pallas_call x1, Pallas kernels: 85.6 us -> 81.8 us  [per_device(): pl.pallas_call(body, name='whole', out_shape=(shape((SEQ, HD), BF16), sha...]
where the time goes in v8:
time: 83.7 us; the launch traced here: 83.5 us
  Pallas kernels  82.9 us (99%)
    pallas_call x1, Pallas kernels, per_device(): pl.pallas_call(body, name='whole', out_shape=(shape((SEQ, HD), BF16), sha...  81.8 us

profile of v8, /device:TPU:1, one launch (start us, length us, event | category | flops | bytes accessed | tf_op | source)
XLA Modules:
  0.0 83.5 jit_solution(13017857966514963781)
XLA Ops:
  0.6 81.8 %whole.1 = (bf16[384,128]{1,0:T(8,128)(2,1)S(1)}, f32[688,128]{1,0:T(8,128)S(1)}, f32[688,128]{1,0:T(8,128)S(1)}, f32[688,128]{1,0:T(8,128)S(1)}, f32[2,8,128]{2,1,0:T(8,128)S(1)}, /*index=5*/f32[2,128]{1,0:T(2,128)S(1)}) custom-call(bf16[384,128]{1,0:T(8,128)(2,1)} %q_hbm.1, bf16[384,1024]{1,0:T(8,128)(2,1)} %k_hbm.1, bf16[384,1024]{1,0:T(8,128)(2,1)} %v_hbm.1, ...), custom_call_target="tpu_custom_call" | custom-call | tf_op jit(solution)/shard_map/whole/pallas_call | solution.py:751
  82.4 1.1 %codes.1 = (bf16[384,128]{1,0:T(8,128)(2,1)}, f32[688,128]{1,0:T(8,128)}, bf16[688,128]{1,0:T(8,128)(2,1)}, f32[688]{0:T(1024)}, f32[128]{0:T(128)}, /*index=5*/...) custom-call(bf16[384,128]{1,0:T(8,128)(2,1)S(1)} %get-tuple-element.14.gq, f32[688,128]{1,0:T(8,128)S(1)} %get-tuple-element.15.nw, ...), custom_call_target="tpu_custom_call" | custom-call | tf_op jit(solution)/shard_map/codes/pallas_call | solution.py:832

commit v9 on v8

--- a/solution.py
+++ b/solution.py
@@ -168,6 +168,19 @@
     def other(sequence):
         return sequence - 1 + (sequence - 1 >= zh).astype(jnp.int32)
 
+    barrier = pltpu.get_barrier_semaphore()
+
+    def greet(**dev):
+        pl.semaphore_signal(barrier, inc=1, device_id=dev, device_id_type=MESH)
+
+    for dz in (1, 2):
+        greet(zh=mod(zh + dz, NZH))
+    for dx in range(1, NX):
+        greet(x=mod(x + dx, NX))
+    for dy in range(1, NY):
+        greet(y=mod(y + dy, NY))
+    for rel in range(1, NZL * NC):
+        greet(zl=mod(zl + rel // NC, NZL), core=lax.rem(k + rel % NC, NC))
     heads = pl.ds(pl.multiple_of(y * HD, HD), HD)
     loads = [
         pltpu.make_async_copy(src, dst, in_sem.at[i])
@@ -190,19 +203,6 @@
     for load in loads:
         load.start()
 
-    barrier = pltpu.get_barrier_semaphore()
-
-    def greet(**dev):
-        pl.semaphore_signal(barrier, inc=1, device_id=dev, device_id_type=MESH)
-
-    for dz in (1, 2):
-        greet(zh=mod(zh + dz, NZH))
-    for dx in range(1, NX):
-        greet(x=mod(x + dx, NX))
-    for dy in range(1, NY):
-        greet(y=mod(y + dy, NY))
-    for rel in range(1, NZL * NC):
-        greet(zl=mod(zl + rel // NC, NZL), core=lax.rem(k + rel % NC, NC))
     me = 2 * y + k
     side = zl & 1
 
@@ -418,7 +418,7 @@
                 piece,
                 piece,
                 ring_send,
-                ring_recv.at[way, slot, hops, part],
+                ring_recv.at[way, slot + part, hops],
                 y=mod(y + 1, NY) if way == 0 else mod(y - 1, NY),
             ).start()
 
@@ -432,7 +432,7 @@
 
     def to_beside(way, slot, hops):
         def go(piece):
-            rcopy(piece, piece, beside_send, beside_recv.at[slot], zl=zl ^ 1).start()
+            rcopy(piece, piece, beside_send, beside_recv.at[SPLIT.index(slot)], zl=zl ^ 1).start()
 
         if slot in SPLIT:
             each_size(parts_of(slot, from_source(way, hops), k)[0], go)
@@ -452,7 +452,7 @@
                 if hops <= reach(way, slot):
                     each_size(
                         parts_of(slot, from_source(way, hops), k)[part],
-                        lambda piece: came(piece, ring_recv.at[way, slot, hops - 1, part]),
+                        lambda piece: came(piece, ring_recv.at[way, slot + part, hops - 1]),
                     )
                     if hops < reach(way, slot):
                         forward(way, slot, hops, part)
@@ -461,14 +461,14 @@
 
     def beside_came(slot):
         longer = (k == 1) & (side == 0)
-        pl.when(longer)(functools.partial(came, gz.at[0:33], beside_recv.at[slot]))
-        pl.when(jnp.logical_not(longer))(functools.partial(came, gz.at[0:32], beside_recv.at[slot]))
+        pl.when(longer)(functools.partial(came, gz.at[0:33], beside_recv.at[SPLIT.index(slot)]))
+        pl.when(jnp.logical_not(longer))(functools.partial(came, gz.at[0:32], beside_recv.at[SPLIT.index(slot)]))
         for source in range(NY):
             start = SLOT * slot + 8 * (2 * source + k) + 4 * (1 - side)
 
             def go(units):
                 piece = gz.at[pl.ds(start, units)]
-                rcopy(piece, piece, core_send, shared_recv.at[slot], core=1 - k).start()
+                rcopy(piece, piece, core_send, shared_recv.at[SPLIT.index(slot)], core=1 - k).start()
 
             if source < NY - 1:
                 go(4)
@@ -478,8 +478,8 @@
 
     def partner_beside(slot):
         longer = (k == 0) & (side == 0)
-        pl.when(longer)(functools.partial(came, gz.at[0:33], shared_recv.at[slot]))
-        pl.when(jnp.logical_not(longer))(functools.partial(came, gz.at[0:32], shared_recv.at[slot]))
+        pl.when(longer)(functools.partial(came, gz.at[0:33], shared_recv.at[SPLIT.index(slot)]))
+        pl.when(jnp.logical_not(longer))(functools.partial(came, gz.at[0:32], shared_recv.at[SPLIT.index(slot)]))
 
     def partner_near(slot):
         more = (k == 0) & (y != NY // 2 - 1)
@@ -501,46 +501,60 @@
         partner_near(slot)
         partner_across(slot)
 
-    def block_of(slot, index):
-        return gz[pl.ds(SLOT * slot + UNITS * index, UNITS)].reshape(ROWS, SEQ)
-
     def member(slot, index):
         if slot == 0:
             return index, 0
-        if slot == 3:
-            return 3, (index + 1) % 3
         turn = 3 * (slot - 1) + index
         return turn // 2, 1 + turn % 2
 
-    started = set()
-
-    def weight_term(slot, index):
-        rows, sequence = member(slot, index)
-        term = jnp.dot(block_of(slot, index), att[sequence], preferred_element_type=F32)
-        dwacc[rows] = dwacc[rows] + term if ("w", rows) in started else term
-        started.add(("w", rows))
-
-    def multiply(slot, index):
-        rows, sequence = member(slot, index)
-        term = jnp.dot(wt[rows], block_of(slot, index), preferred_element_type=F32)
-        acct[sequence] = acct[sequence] + term if ("g", sequence) in started else term
-        started.add(("g", sequence))
+    started = {("g", 0)}
+
+    def add_to(ref, key, term):
+        ref[...] = ref[...] + term if key in started else term
+        started.add(key)
+
+    def side_by_side(slot, indices):
+        blocks = [gz[pl.ds(SLOT * slot + UNITS * i, UNITS)].reshape(ROWS, SEQ) for i in indices]
+        return jnp.concatenate(blocks, axis=1) if len(blocks) > 1 else blocks[0]
+
+    def one_below_another(sequences):
+        parts = [att[s] for s in sequences]
+        return jnp.concatenate(parts, axis=0) if len(parts) > 1 else parts[0]
+
+    def weight_term(slot, *indices):
+        members = [member(slot, i) for i in indices]
+        rows = members[0][0]
+        term = jnp.dot(
+            side_by_side(slot, indices),
+            one_below_another([sequence for _, sequence in members]),
+            preferred_element_type=F32,
+        )
+        add_to(dwacc.at[rows], ("w", rows), term)
+
+    def multiply(slot, *indices):
+        members = [member(slot, i) for i in indices]
+        term = jnp.dot(wt[members[0][0]], side_by_side(slot, indices), preferred_element_type=F32)
+        for i, (_, sequence) in enumerate(members):
+            add_to(acct.at[sequence], ("g", sequence), term[:, SEQ * i : SEQ * (i + 1)])
 
     early = jnp.where(lax.rem(y + NY // 2, NY) <= 2, 2, 0)
     last_blocks = (early, jnp.where(early == 2, 0, 1), jnp.where(early == 2, 1, 2))
 
-    def last_term(turn):
-        index = last_blocks[turn]
+    def last_term(*turns):
+        indices = [last_blocks[turn] for turn in turns]
         term = jnp.dot(
-            block_of(SLOTS - 1, index), att[lax.rem(index + 1, NZH)], preferred_element_type=F32
-        )
-        dwacc[3] = dwacc[3] + term if turn > 0 else term
-
-    def last_multiply(turn):
-        index = last_blocks[turn]
-        term = jnp.dot(wt[3], block_of(SLOTS - 1, index), preferred_element_type=F32)
-        sequence = lax.rem(index + 1, NZH)
-        acct[sequence] = acct[sequence] + term
+            side_by_side(SLOTS - 1, indices),
+            one_below_another([lax.rem(i + 1, NZH) for i in indices]),
+            preferred_element_type=F32,
+        )
+        add_to(dwacc.at[3], ("w", 3), term)
+
+    def last_multiply(*turns):
+        indices = [last_blocks[turn] for turn in turns]
+        term = jnp.dot(wt[3], side_by_side(SLOTS - 1, indices), preferred_element_type=F32)
+        for i, index in enumerate(indices):
+            sequence = lax.rem(index + 1, NZH)
+            acct[sequence] = acct[sequence] + term[:, SEQ * i : SEQ * (i + 1)]
 
     def send_term(rows):
         dw_stage[rows] = dwacc[rows].astype(BF16)
@@ -548,14 +562,21 @@
             dw_stage.at[rows], dw_in.at[rows], dw_send, dw_recv, x=mod(x + AHEAD[rows], NX)
         ).start()
 
-    def send_grad(sequence):
-        ga_stage[sequence - 1] = acct[sequence].astype(BF16)
-        o = other(sequence)
-        rcopy(
-            ga_stage.at[sequence - 1], ga_in.at[sequence_of(zh, o) - 1], ga_send, ga_recv, zh=o
-        ).start()
+    def send_grads():
+        for i in range(3):
+            for sequence in (1, 2):
+                o = other(sequence)
+                ga_stage[sequence - 1, i] = acct[sequence, :, 128 * i : 128 * (i + 1)].astype(BF16)
+                rcopy(
+                    ga_stage.at[sequence - 1, i],
+                    ga_in.at[sequence_of(zh, o) - 1, i],
+                    ga_send,
+                    ga_recv.at[i],
+                    zh=o,
+                ).start()
 
     def old_moments():
+        acct[0] = jnp.zeros((HD, SEQ), F32)
         for load in loads[5:]:
             load.wait()
         for c, start, size in row_chunks():
@@ -590,48 +611,38 @@
     pass_on(1, 4)
     beside_came(0)
     pass_on(2, 3)
+    pass_on(3, 2)
     partner_has(1)
+    came(att.at[1], att_recv.at[0])
+    came(att.at[2], att_recv.at[1])
+    weight_term(1, 0, 1)
     partner_has(0)
     partner_beside(0)
-    came(wt.at[0:3], w_recv)
-    multiply(0, 0)
-    came(att.at[1], att_recv.at[0])
-    came(att.at[2], att_recv.at[1])
-    weight_term(1, 0)
-    multiply(0, 2)
-    pass_on(3, 2)
-    weight_term(1, 1)
     weight_term(0, 0)
     send_term(0)
+    pass_on(2, 4)
+    weight_term(1, 2)
     weight_term(0, 2)
-    pass_on(2, 4)
-    multiply(1, 1)
-    weight_term(1, 2)
+    pass_on(3, 3)
     weight_term(0, 1)
     partner_has(2)
-    pass_on(3, 3)
     weight_term(2, 0)
     send_term(1)
-    weight_term(2, 1)
-    weight_term(2, 2)
+    weight_term(2, 1, 2)
     send_term(2)
-    multiply(2, 0)
+    came(wt.at[0:3], w_recv)
+    multiply(1, 0, 1)
     multiply(1, 2)
     partner_near(3)
     last_term(0)
     pass_on(3, 4)
-    multiply(0, 1)
+    multiply(2, 0)
+    multiply(2, 1, 2)
     last_multiply(0)
-    multiply(2, 1)
-    multiply(2, 2)
-    multiply(1, 0)
     partner_across(3)
-    last_multiply(1)
-    last_multiply(2)
-    send_grad(1)
-    send_grad(2)
-    last_term(1)
-    last_term(2)
+    last_multiply(1, 2)
+    send_grads()
+    last_term(1, 2)
 
     came(dw_in, dw_recv)
     for c, start, size in row_chunks():
@@ -658,11 +669,16 @@
     for dx in range(1, NX):
         rcopy(cst.at[0], x_in.at[NX - dx - 1], x_send, x_recv, x=mod(x + dx, NX)).start()
 
+    multiply(0, 0)
+    multiply(0, 1)
+    multiply(0, 2)
+
     def back_rows(i):
         rows, cols = pl.ds(128 * i, 128), pl.ds(0, 128 * (i + 1))
+        came(ga_in.at[:, i], ga_recv.at[i])
         total = acct[0, :, rows]
         for s in range(2):
-            total = total + ga_in[s, :, rows].astype(F32)
+            total = total + ga_in[s, i].astype(F32)
         grad_half = total.astype(BF16).T
         grad_probs = lax.dot_general(grad_half, vv[cols, :], NT, preferred_element_type=F32)
         row_dot = jnp.sum(
@@ -686,7 +702,6 @@
         rcopy(
             mine, zl_in.at[back], zl_send, zl_recv, zl=mod(zl + dl, NZL), core=lax.rem(k + dk, NC)
         ).start()
-    came(ga_in, ga_recv)
     for i in range(3):
         back_rows(i)
     came(zl_in, zl_recv)
@@ -779,8 +794,8 @@
             pltpu.VMEM((NZH, SEQ, HD), BF16),
             pltpu.VMEM((SEQ, SEQ), F32),
             pltpu.VMEM((NZH, HD, SEQ), F32),
-            pltpu.VMEM((2, HD, SEQ), BF16),
-            pltpu.VMEM((2, HD, SEQ), BF16),
+            pltpu.VMEM((2, 3, HD, HD), BF16),
+            pltpu.VMEM((2, 3, HD, HD), BF16),
             pltpu.VMEM((NX, ROWS, HD), F32),
             pltpu.VMEM((NX - 1, ROWS, HD), BF16),
             pltpu.VMEM((NX - 1, ROWS, HD), BF16),
@@ -797,10 +812,10 @@
             dma((SLOTS,)),
             dma((SLOTS,)),
             dma,
-            dma((2, SLOTS, 4, 2)),
-            dma,
-            dma((SLOTS,)),
-            dma((SLOTS,)),
+            dma((2, SLOTS + 1, 4)),
+            dma,
+            dma((len(SPLIT),)),
+            dma((len(SPLIT),)),
             dma,
             dma((SLOTS, 2)),
             dma,
@@ -808,7 +823,7 @@
             dma,
             dma,
             dma,
-            dma,
+            dma((3,)),
             dma,
             dma,
             dma,

time: 83.7 us -> 82.5 us (0.986)
  Pallas kernels: 82.9 us -> 81.8 us
    pallas_call x1, Pallas kernels: 81.8 us -> 80.7 us  [per_device(): pl.pallas_call(body, name='whole', out_shape=(shape((SEQ, HD), BF16), sha...]
where the time goes in v9:
time: 82.5 us; the launch traced here: 82.4 us
  Pallas kernels  81.8 us (99%)
    pallas_call x1, Pallas kernels, per_device(): pl.pallas_call(body, name='whole', out_shape=(shape((SEQ, HD), BF16), sha...  80.7 us

profile of v9, /device:TPU:1, one launch (start us, length us, event | category | flops | bytes accessed | tf_op | source)
XLA Modules:
  0.0 82.4 jit_solution(3170802223275929793)
XLA Ops:
  0.6 80.7 %whole.1 = (bf16[384,128]{1,0:T(8,128)(2,1)S(1)}, f32[688,128]{1,0:T(8,128)S(1)}, f32[688,128]{1,0:T(8,128)S(1)}, f32[688,128]{1,0:T(8,128)S(1)}, f32[2,8,128]{2,1,0:T(8,128)S(1)}, /*index=5*/f32[2,128]{1,0:T(2,128)S(1)}) custom-call(bf16[384,128]{1,0:T(8,128)(2,1)} %q_hbm.1, bf16[384,1024]{1,0:T(8,128)(2,1)} %k_hbm.1, bf16[384,1024]{1,0:T(8,128)(2,1)} %v_hbm.1, ...), custom_call_target="tpu_custom_call" | custom-call | tf_op jit(solution)/shard_map/whole/pallas_call | solution.py:766
  81.3 1.1 %codes.1 = (bf16[384,128]{1,0:T(8,128)(2,1)}, f32[688,128]{1,0:T(8,128)}, bf16[688,128]{1,0:T(8,128)(2,1)}, f32[688]{0:T(1024)}, f32[128]{0:T(128)}, /*index=5*/...) custom-call(bf16[384,128]{1,0:T(8,128)(2,1)S(1)} %get-tuple-element.14.gq, f32[688,128]{1,0:T(8,128)S(1)} %get-tuple-element.15.nw, ...), custom_call_target="tpu_custom_call" | custom-call | tf_op jit(solution)/shard_map/codes/pallas_call | solution.py:847

commit v10 on v9

--- a/solution.py
+++ b/solution.py
@@ -247,6 +247,13 @@
         here = (zd == zh) & (h == me) & (home["zl"] == zl)
         return slot, SLOT * slot + e, home, here
 
+    def greet_home(u, carry):
+        slot, place, home, here = goes_to(u)
+        pl.when(jnp.logical_not(here))(functools.partial(greet, **home))
+        return carry
+
+    lax.fori_loop(0, 8, greet_home, 0)
+
     first_index = lax.div(8 * me, UNITS)
     first_place = 8 * me - UNITS * first_index
     has_last = me == HOMES - 1
@@ -291,12 +298,6 @@
     coming = [count(there for there, _, _, _, _ in held) - n for held, n in zip(units, landing)]
     staying = [count(lands & same for _, lands, _, same, _ in held) for held in units]
 
-    def greet_home(u, carry):
-        slot, place, home, here = goes_to(u)
-        pl.when(jnp.logical_not(here))(functools.partial(greet, **home))
-        return carry
-
-    lax.fori_loop(0, 8, greet_home, 0)
     for held in units:
         for _, lands, source, same, _ in held:
             pl.when(lands & jnp.logical_not(same))(functools.partial(greet, **source))
@@ -305,30 +306,22 @@
     loads[0].wait()
     gt[...] = g[...].T
 
-    for slot, held in enumerate(units):
-        for j, (_, _, _, _, missing) in enumerate(held):
-
-            @pl.when(missing)
-            def _():
-                gz[SLOT * slot + 8 * me + j] = jnp.zeros((UNIT, SEQ), BF16)
-
     pl.semaphore_wait(barrier, greeted)
 
-    def spread(wanted, u, carry):
+    def spread(u, carry):
         slot, place, home, here = goes_to(u)
 
-        @pl.when((slot == wanted) & here)
+        @pl.when(here)
         def _():
             gz[place] = gt[rows_of(u), :]
 
-        @pl.when((slot == wanted) & jnp.logical_not(here))
+        @pl.when(jnp.logical_not(here))
         def _():
             rcopy(gt.at[rows_of(u), :], gz.at[place], spread_send, far_recv.at[slot], **home).start()
 
         return carry
 
-    for slot in range(SLOTS):
-        lax.fori_loop(0, 8, functools.partial(spread, slot), 0)
+    lax.fori_loop(0, 8, spread, 0)
 
     loads[4].wait()
     wt[3] = w[...].astype(BF16).T
@@ -352,6 +345,13 @@
         att[0, rows, :] = jnp.dot(
             probabilities.astype(BF16), vv[cols, :], preferred_element_type=F32
         ).astype(BF16)
+
+    for slot, held in enumerate(units):
+        for j, (_, _, _, _, missing) in enumerate(held):
+
+            @pl.when(missing)
+            def _():
+                gz[SLOT * slot + 8 * me + j] = jnp.zeros((UNIT, SEQ), BF16)
 
     def send_att():
         for sequence in (1, 2):
@@ -689,26 +689,6 @@
             jnp.dot(grad_scores, kk[cols, :], preferred_element_type=F32) * SCALE
         ).astype(BF16)
 
-    came(x_in, x_recv)
-    cst[1] = jnp.maximum(cst[0], jnp.max(x_in[...], axis=0))
-    for sequence in (1, 2):
-        o = other(sequence)
-        rcopy(cst.at[1], zh_in.at[sequence_of(zh, o) - 1], zh_send, zh_recv, zh=o).start()
-    came(y_in, y_recv)
-    mine[...] = jnp.maximum(st[...], jnp.max(y_in[...], axis=0))
-    for rel in range(1, NZL * NC):
-        dl, dk = rel // NC, rel % NC
-        back = NC * ((NZL - dl) % NZL) + dk - 1
-        rcopy(
-            mine, zl_in.at[back], zl_send, zl_recv, zl=mod(zl + dl, NZL), core=lax.rem(k + dk, NC)
-        ).start()
-    for i in range(3):
-        back_rows(i)
-    came(zl_in, zl_recv)
-    rows_out[...] = jnp.maximum(mine[...], jnp.max(zl_in[...], axis=0))
-    came(zh_in, zh_recv)
-    cols_out[...] = jnp.maximum(cst[1], jnp.max(zh_in[...], axis=0))
-
     def left(ref, send):
         rcopy(ref, ref, send, zh_recv, core=k).wait_send()
 
@@ -733,8 +713,32 @@
     for whole, send in (
         (att.at[0:2], att_send),
         (wt.at[0:3], w_send),
+        (dw_in, dw_send),
+    ):
+        left(whole, send)
+
+    came(x_in, x_recv)
+    cst[1] = jnp.maximum(cst[0], jnp.max(x_in[...], axis=0))
+    for sequence in (1, 2):
+        o = other(sequence)
+        rcopy(cst.at[1], zh_in.at[sequence_of(zh, o) - 1], zh_send, zh_recv, zh=o).start()
+    came(y_in, y_recv)
+    mine[...] = jnp.maximum(st[...], jnp.max(y_in[...], axis=0))
+    for rel in range(1, NZL * NC):
+        dl, dk = rel // NC, rel % NC
+        back = NC * ((NZL - dl) % NZL) + dk - 1
+        rcopy(
+            mine, zl_in.at[back], zl_send, zl_recv, zl=mod(zl + dl, NZL), core=lax.rem(k + dk, NC)
+        ).start()
+    for i in range(3):
+        back_rows(i)
+    came(zl_in, zl_recv)
+    rows_out[...] = jnp.maximum(mine[...], jnp.max(zl_in[...], axis=0))
+    came(zh_in, zh_recv)
+    cols_out[...] = jnp.maximum(cst[1], jnp.max(zh_in[...], axis=0))
+
+    for whole, send in (
         (ga_in, ga_send),
-        (dw_in, dw_send),
         (y_in, y_send),
         (zl_in, zl_send),
         (x_in, x_send),
@@ -743,19 +747,57 @@
         left(whole, send)
 
 
-def codes(gq, nw, fnew, snew, rows, cols, gq_out, nw_out, nfc_out, nfr_out, nfcol_out, nsc_out, nsr_out, nscol_out):
-    gq_out[...] = gq[...]
-    nw_out[...] = nw[...]
-    nfcol_out[...] = cols[0]
-    nscol_out[...] = cols[1]
-    for c, start, size in row_chunks():
-        at = pl.ds(start, size)
-        nfr_out[at] = rows[0, c, 0:size]
-        nsr_out[at] = rows[1, c, 0:size]
-        low_first = jnp.minimum(down_rows(rows[0, c : c + 1, :])[:size], cols[0:1])
-        low_second = jnp.minimum(down_rows(rows[1, c : c + 1, :])[:size], cols[1:2])
-        nfc_out[at, :] = (fnew[at, :] / (low_first + code_eps)).astype(BF16)
-        nsc_out[at, :] = (snew[at, :] / (low_second + code_eps)).astype(BF16)
+def codes(
+    gq,
+    nw,
+    fnew,
+    snew,
+    rows,
+    cols,
+    gq_out,
+    nw_out,
+    nfc_out,
+    nfr_out,
+    nfcol_out,
+    nsc_out,
+    nsr_out,
+    nscol_out,
+    first_code,
+    second_code,
+    first_rows,
+    second_rows,
+    first_cols,
+    second_cols,
+    sem,
+):
+    copies = []
+
+    def out(src, dst):
+        copy = pltpu.make_async_copy(src, dst, sem.at[len(copies)])
+        copy.start()
+        copies.append(copy)
+
+    out(gq, gq_out)
+    out(nw, nw_out)
+    for moment, (new, code, code_out, maxima, maxima_out, col, col_out) in enumerate(
+        (
+            (fnew, first_code, nfc_out, first_rows, nfr_out, first_cols, nfcol_out),
+            (snew, second_code, nsc_out, second_rows, nsr_out, second_cols, nscol_out),
+        )
+    ):
+        col[...] = cols[moment]
+        for c, start, size in row_chunks():
+            at = pl.ds(start, size)
+            maxima[at] = rows[moment, c, 0:size]
+            low = jnp.minimum(
+                down_rows(rows[moment, c : c + 1, :])[:size], cols[moment : moment + 1]
+            )
+            code[at, :] = (new[at, :] / (low + code_eps)).astype(BF16)
+        out(code, code_out)
+        out(maxima, maxima_out)
+        out(col, col_out)
+    for copy in copies:
+        copy.wait()
 
 
 def per_device(queries, keys, values, grad_out, weight, fc, frow, fcol, sc, srow, scol):
@@ -859,7 +901,16 @@
         ),
         compiler_params=pltpu.CompilerParams(vmem_limit_bytes=8 * 1024 * 1024),
         in_specs=[vmem] * 6,
-        out_specs=[vmem] * 8,
+        out_specs=[hbm] * 8,
+        scratch_shapes=[
+            pltpu.VMEM((ROWS, HD), BF16),
+            pltpu.VMEM((ROWS, HD), BF16),
+            pltpu.VMEM((ROWS,), F32),
+            pltpu.VMEM((ROWS,), F32),
+            pltpu.VMEM((HD,), F32),
+            pltpu.VMEM((HD,), F32),
+            dma((8,)),
+        ],
     )(gq, nw, fnew, snew, rows, cols)
 
 

time: 82.5 us -> 81.9 us (level)
  no operation moved by 1% of the time
where the time goes in v10:
time: 81.9 us; the launch traced here: 81.7 us
  Pallas kernels  81.1 us (99%)
    pallas_call x1, Pallas kernels, per_device(): pl.pallas_call(body, name='whole', out_shape=(shape((SEQ, HD), BF16), sha...  80 us

profile of v10, /device:TPU:1, one launch (start us, length us, event | category | flops | bytes accessed | tf_op | source)
XLA Modules:
  0.0 81.7 jit_solution(14249443329534867820)
XLA Ops:
  0.6 80.0 %whole.1 = (bf16[384,128]{1,0:T(8,128)(2,1)S(1)}, f32[688,128]{1,0:T(8,128)S(1)}, f32[688,128]{1,0:T(8,128)S(1)}, f32[688,128]{1,0:T(8,128)S(1)}, f32[2,8,128]{2,1,0:T(8,128)S(1)}, /*index=5*/f32[2,128]{1,0:T(2,128)S(1)}) custom-call(bf16[384,128]{1,0:T(8,128)(2,1)} %q_hbm.1, bf16[384,1024]{1,0:T(8,128)(2,1)} %k_hbm.1, bf16[384,1024]{1,0:T(8,128)(2,1)} %v_hbm.1, ...), custom_call_target="tpu_custom_call" | custom-call | tf_op jit(solution)/shard_map/whole/pallas_call | solution.py:808
  80.7 1.0 %codes.1 = (bf16[384,128]{1,0:T(8,128)(2,1)}, f32[688,128]{1,0:T(8,128)}, bf16[688,128]{1,0:T(8,128)(2,1)}, f32[688]{0:T(1024)}, f32[128]{0:T(128)}, /*index=5*/...) custom-call(bf16[384,128]{1,0:T(8,128)(2,1)S(1)} %get-tuple-element.14.gq, f32[688,128]{1,0:T(8,128)S(1)} %get-tuple-element.15.nw, ...), custom_call_target="tpu_custom_call" | custom-call | tf_op jit(solution)/shard_map/codes/pallas_call | solution.py:889

commit v11 on v10

--- a/solution.py
+++ b/solution.py
@@ -224,36 +224,6 @@
         )
         return slot, index
 
-    first_owner = lax.div(8 * t, UNITS)
-    first_row = 8 * t - UNITS * first_owner
-    turnover = UNITS - first_row
-    sides = []
-    for owner in (first_owner, first_owner + 1):
-        xd = lax.div(owner, NZH)
-        zd = owner - NZH * xd
-        slot, index = slot_and_index(mod(xd - x, NX), sequence_of(zh, zd))
-        sides.append((zd, slot, UNITS * index))
-
-    def goes_to(u):
-        over = u >= turnover
-        zd, slot, start = (jnp.where(over, b, a) for a, b in zip(*sides))
-        e = start + first_row + u - jnp.where(over, UNITS, 0)
-        h = jnp.minimum(lax.shift_right_logical(e, 3), HOMES - 1)
-        line = zl ^ (2 * (u & 1))
-        for split in SPLIT:
-            shared = (zl & 2) + (e - 8 * h >= 4).astype(jnp.int32)
-            line = jnp.where(slot == split, shared, line)
-        home = dict(zh=zd, y=lax.shift_right_logical(h, 1), zl=line, core=h & 1)
-        here = (zd == zh) & (h == me) & (home["zl"] == zl)
-        return slot, SLOT * slot + e, home, here
-
-    def greet_home(u, carry):
-        slot, place, home, here = goes_to(u)
-        pl.when(jnp.logical_not(here))(functools.partial(greet, **home))
-        return carry
-
-    lax.fori_loop(0, 8, greet_home, 0)
-
     first_index = lax.div(8 * me, UNITS)
     first_place = 8 * me - UNITS * first_index
     has_last = me == HOMES - 1
@@ -278,18 +248,21 @@
             column = lax.shift_right_logical(unit, 3)
             line = lax.shift_right_logical(column, 1) & 3
             there = unit < ALL_UNITS
-            missing = jnp.logical_not(there)
             if j == 8:
-                there, missing = there & has_last, missing & has_last
+                there = there & has_last
             if slot in SPLIT:
                 taken = side == min(j // 4, 1)
-                there, missing = there & taken, missing & taken
+                there = there & taken
                 here = (line & 2) == (zl & 2)
             else:
                 here = (line ^ (2 * (unit & 1))) == zl
             source = dict(zh=z, y=lax.shift_right_logical(column, 3), zl=line, core=column & 1)
-            held.append((there, there & here, source, (z == zh) & (column == t), missing))
+            held.append((there, there & here, source, (z == zh) & (column == t), unit))
         units.append(held)
+
+    for held in units:
+        for _, lands, source, same, _ in held:
+            pl.when(lands & jnp.logical_not(same))(functools.partial(greet, **source))
 
     def count(flags):
         return sum(f.astype(jnp.int32) for f in flags)
@@ -297,11 +270,30 @@
     landing = [count(lands for _, lands, _, _, _ in held) for held in units]
     coming = [count(there for there, _, _, _, _ in held) - n for held, n in zip(units, landing)]
     staying = [count(lands & same for _, lands, _, same, _ in held) for held in units]
-
-    for held in units:
-        for _, lands, source, same, _ in held:
-            pl.when(lands & jnp.logical_not(same))(functools.partial(greet, **source))
-    greeted = 8 + sum(landing) - 2 * sum(staying) + 2 + 3 + 7 + 7
+    greeted = 8 - sum(staying) + 2 + 3 + 7 + 7
+
+    first_owner = lax.div(8 * t, UNITS)
+    first_row = 8 * t - UNITS * first_owner
+    turnover = UNITS - first_row
+    sides = []
+    for owner in (first_owner, first_owner + 1):
+        xd = lax.div(owner, NZH)
+        zd = owner - NZH * xd
+        slot, index = slot_and_index(mod(xd - x, NX), sequence_of(zh, zd))
+        sides.append((zd, slot, UNITS * index))
+
+    def goes_to(u):
+        over = u >= turnover
+        zd, slot, start = (jnp.where(over, b, a) for a, b in zip(*sides))
+        e = start + first_row + u - jnp.where(over, UNITS, 0)
+        h = jnp.minimum(lax.shift_right_logical(e, 3), HOMES - 1)
+        line = zl ^ (2 * (u & 1))
+        for split in SPLIT:
+            shared = (zl & 2) + (e - 8 * h >= 4).astype(jnp.int32)
+            line = jnp.where(slot == split, shared, line)
+        home = dict(zh=zd, y=lax.shift_right_logical(h, 1), zl=line, core=h & 1)
+        here = (zd == zh) & (h == me) & (home["zl"] == zl)
+        return slot, SLOT * slot + e, home, here
 
     loads[0].wait()
     gt[...] = g[...].T
@@ -347,7 +339,12 @@
         ).astype(BF16)
 
     for slot, held in enumerate(units):
-        for j, (_, _, _, _, missing) in enumerate(held):
+        for j, (_, _, _, _, unit) in enumerate(held):
+            missing = unit >= ALL_UNITS
+            if j == 8:
+                missing = missing & has_last
+            if slot in SPLIT:
+                missing = missing & (side == min(j // 4, 1))
 
             @pl.when(missing)
             def _():

time: 81.9 us -> 81.5 us (level)
  no operation moved by 1% of the time
where the time goes in v11:
time: 81.5 us; the launch traced here: 81.3 us
  Pallas kernels  80.7 us (99%)
    pallas_call x1, Pallas kernels, per_device(): pl.pallas_call(body, name='whole', out_shape=(shape((SEQ, HD), BF16), sha...  79.7 us

profile of v11, /device:TPU:1, one launch (start us, length us, event | category | flops | bytes accessed | tf_op | source)
XLA Modules:
  0.0 81.3 jit_solution(12279861341150384528)
XLA Ops:
  0.6 79.7 %whole.1 = (bf16[384,128]{1,0:T(8,128)(2,1)S(1)}, f32[688,128]{1,0:T(8,128)S(1)}, f32[688,128]{1,0:T(8,128)S(1)}, f32[688,128]{1,0:T(8,128)S(1)}, f32[2,8,128]{2,1,0:T(8,128)S(1)}, /*index=5*/f32[2,128]{1,0:T(2,128)S(1)}) custom-call(bf16[384,128]{1,0:T(8,128)(2,1)} %q_hbm.1, bf16[384,1024]{1,0:T(8,128)(2,1)} %k_hbm.1, bf16[384,1024]{1,0:T(8,128)(2,1)} %v_hbm.1, ...), custom_call_target="tpu_custom_call" | custom-call | tf_op jit(solution)/shard_map/whole/pallas_call | solution.py:805
  80.3 1.0 %codes.1 = (bf16[384,128]{1,0:T(8,128)(2,1)}, f32[688,128]{1,0:T(8,128)}, bf16[688,128]{1,0:T(8,128)(2,1)}, f32[688]{0:T(1024)}, f32[128]{0:T(128)}, /*index=5*/...) custom-call(bf16[384,128]{1,0:T(8,128)(2,1)S(1)} %get-tuple-element.14.gq, f32[688,128]{1,0:T(8,128)S(1)} %get-tuple-element.15.nw, ...), custom_call_target="tpu_custom_call" | custom-call | tf_op jit(solution)/shard_map/codes/pallas_call | solution.py:886

commit v12 on v11

--- a/solution.py
+++ b/solution.py
@@ -203,7 +203,17 @@
     for load in loads:
         load.start()
 
-    me = 2 * y + k
+    turned = (
+        (2 * x + NY - 1 + (zh == 2).astype(jnp.int32)) & (NY - 1),
+        jnp.int32(0),
+        (2 * x + 1 + (zh > 0).astype(jnp.int32)) & (NY - 1),
+        jnp.int32(0),
+    )
+
+    def seat(slot, column):
+        return (column + NY - turned[slot]) & (NY - 1)
+
+    homes = [2 * seat(slot, y) + k for slot in range(SLOTS)]
     side = zl & 1
 
     def rows_of(u):
@@ -224,11 +234,11 @@
         )
         return slot, index
 
-    first_index = lax.div(8 * me, UNITS)
-    first_place = 8 * me - UNITS * first_index
-    has_last = me == HOMES - 1
     units = []
     for slot in range(SLOTS):
+        first_index = lax.div(8 * homes[slot], UNITS)
+        first_place = 8 * homes[slot] - UNITS * first_index
+        has_last = homes[slot] == HOMES - 1
         blocks = []
         for index in (first_index, first_index + 1):
             if slot == 0:
@@ -276,23 +286,29 @@
     first_row = 8 * t - UNITS * first_owner
     turnover = UNITS - first_row
     sides = []
+
+    def turn_of(slot, zd):
+        first = 2 * x + NY - 1 + (zd == 2).astype(jnp.int32)
+        third = 2 * x + 1 + (zd > 0).astype(jnp.int32)
+        return jnp.where(slot == 0, first, jnp.where(slot == 2, third, 0))
+
     for owner in (first_owner, first_owner + 1):
         xd = lax.div(owner, NZH)
         zd = owner - NZH * xd
         slot, index = slot_and_index(mod(xd - x, NX), sequence_of(zh, zd))
-        sides.append((zd, slot, UNITS * index))
+        sides.append((zd, slot, UNITS * index, turn_of(slot, zd)))
 
     def goes_to(u):
         over = u >= turnover
-        zd, slot, start = (jnp.where(over, b, a) for a, b in zip(*sides))
+        zd, slot, start, turn = (jnp.where(over, b, a) for a, b in zip(*sides))
         e = start + first_row + u - jnp.where(over, UNITS, 0)
         h = jnp.minimum(lax.shift_right_logical(e, 3), HOMES - 1)
         line = zl ^ (2 * (u & 1))
         for split in SPLIT:
             shared = (zl & 2) + (e - 8 * h >= 4).astype(jnp.int32)
             line = jnp.where(slot == split, shared, line)
-        home = dict(zh=zd, y=lax.shift_right_logical(h, 1), zl=line, core=h & 1)
-        here = (zd == zh) & (h == me) & (home["zl"] == zl)
+        home = dict(zh=zd, y=(lax.shift_right_logical(h, 1) + turn) & (NY - 1), zl=line, core=h & 1)
+        here = (zd == zh) & (home["y"] == y) & (home["core"] == k) & (home["zl"] == zl)
         return slot, SLOT * slot + e, home, here
 
     loads[0].wait()
@@ -342,13 +358,13 @@
         for j, (_, _, _, _, unit) in enumerate(held):
             missing = unit >= ALL_UNITS
             if j == 8:
-                missing = missing & has_last
+                missing = missing & (homes[slot] == HOMES - 1)
             if slot in SPLIT:
                 missing = missing & (side == min(j // 4, 1))
 
             @pl.when(missing)
             def _():
-                gz[SLOT * slot + 8 * me + j] = jnp.zeros((UNIT, SEQ), BF16)
+                gz[SLOT * slot + 8 * homes[slot] + j] = jnp.zeros((UNIT, SEQ), BF16)
 
     def send_att():
         for sequence in (1, 2):
@@ -369,7 +385,7 @@
         )
 
         for j, (_, lands, _, _, _) in enumerate(units[slot]):
-            piece = gz.at[SLOT * slot + 8 * me + j]
+            piece = gz.at[SLOT * slot + 8 * homes[slot] + j]
 
             @pl.when(lands)
             def _():
@@ -388,8 +404,8 @@
         return mod(y - hops, NY) if way == 0 else mod(y + hops, NY)
 
     def parts_of(slot, source, core):
-        start = SLOT * slot + 8 * (2 * source + core)
-        last = (source == NY - 1) & (core == 1)
+        start = SLOT * slot + 8 * (2 * seat(slot, source) + core)
+        last = (seat(slot, source) == NY - 1) & (core == 1)
         if slot in SPLIT:
             longer = last & (side == 1)
             start = start + 4 * side
@@ -479,7 +495,7 @@
         pl.when(jnp.logical_not(longer))(functools.partial(came, gz.at[0:32], shared_recv.at[SPLIT.index(slot)]))
 
     def partner_near(slot):
-        more = (k == 0) & (y != NY // 2 - 1)
+        more = (k == 0) & (seat(slot, y) != NY // 2 - 1)
         each = 8
         if slot in SPLIT:
             more, each = more & (side == 1), 4
@@ -487,7 +503,7 @@
         pl.when(jnp.logical_not(more))(functools.partial(came, gz.at[0 : 7 * each], core_recv.at[slot, 0]))
 
     def partner_across(slot):
-        more = (k == 0) & (y == NY // 2 - 1)
+        more = (k == 0) & (seat(slot, y) == NY // 2 - 1)
         each = 8
         if slot in SPLIT:
             more, each = more & (side == 1), 4
@@ -694,7 +710,7 @@
         copies = 1 if slot in SPLIT else 3
         wait_units(landing[slot], 9, lambda c: left(gz.at[0 : copies * c], relay_send.at[slot]))
     longer = count(
-        (from_source(way, hops) == NY - 1) & (k == 1) & ((side == 1) | (slot not in SPLIT))
+        (seat(slot, from_source(way, hops)) == NY - 1) & (k == 1) & ((side == 1) | (slot not in SPLIT))
         for slot in range(SLOTS)
         for way in (0, 1)
         for hops in range(reach(way, slot))

time: 81.5 us -> 81.3 us (level)
  no operation moved by 1% of the time
where the time goes in v12:
time: 81.3 us; the launch traced here: 81.1 us
  Pallas kernels  80.4 us (99%)
    pallas_call x1, Pallas kernels, per_device(): pl.pallas_call(body, name='whole', out_shape=(shape((SEQ, HD), BF16), sha...  79.4 us

profile of v12, /device:TPU:1, one launch (start us, length us, event | category | flops | bytes accessed | tf_op | source)
XLA Modules:
  0.0 81.1 jit_solution(10160340667289447992)
XLA Ops:
  0.6 79.4 %whole.1 = (bf16[384,128]{1,0:T(8,128)(2,1)S(1)}, f32[688,128]{1,0:T(8,128)S(1)}, f32[688,128]{1,0:T(8,128)S(1)}, f32[688,128]{1,0:T(8,128)S(1)}, f32[2,8,128]{2,1,0:T(8,128)S(1)}, /*index=5*/f32[2,128]{1,0:T(2,128)S(1)}) custom-call(bf16[384,128]{1,0:T(8,128)(2,1)} %q_hbm.1, bf16[384,1024]{1,0:T(8,128)(2,1)} %k_hbm.1, bf16[384,1024]{1,0:T(8,128)(2,1)} %v_hbm.1, ...), custom_call_target="tpu_custom_call" | custom-call | tf_op jit(solution)/shard_map/whole/pallas_call | solution.py:821
  80.0 1.0 %codes.1 = (bf16[384,128]{1,0:T(8,128)(2,1)}, f32[688,128]{1,0:T(8,128)}, bf16[688,128]{1,0:T(8,128)(2,1)}, f32[688]{0:T(1024)}, f32[128]{0:T(128)}, /*index=5*/...) custom-call(bf16[384,128]{1,0:T(8,128)(2,1)S(1)} %get-tuple-element.14.gq, f32[688,128]{1,0:T(8,128)S(1)} %get-tuple-element.15.nw, ...), custom_call_target="tpu_custom_call" | custom-call | tf_op jit(solution)/shard_map/codes/pallas_call | solution.py:902

commit v13 on v12

--- a/solution.py
+++ b/solution.py
@@ -389,7 +389,7 @@
 
             @pl.when(lands)
             def _():
-                for dl in (2,) if slot in SPLIT else (1, 3, 2):
+                for dl in (2,) if slot in SPLIT else (1, 2, 3):
                     rcopy(
                         piece, piece, relay_send.at[slot], near_recv.at[slot], zl=mod(zl + dl, NZL)
                     ).start()
@@ -575,18 +575,21 @@
             dw_stage.at[rows], dw_in.at[rows], dw_send, dw_recv, x=mod(x + AHEAD[rows], NX)
         ).start()
 
-    def send_grads():
+    def send_grad(sequence, i):
+        o = other(sequence)
+        ga_stage[sequence - 1, i] = acct[sequence, :, 128 * i : 128 * (i + 1)].astype(BF16)
+        rcopy(
+            ga_stage.at[sequence - 1, i],
+            ga_in.at[sequence_of(zh, o) - 1, i],
+            ga_send,
+            ga_recv.at[i],
+            zh=o,
+        ).start()
+
+    def send_grads(*sequences):
         for i in range(3):
-            for sequence in (1, 2):
-                o = other(sequence)
-                ga_stage[sequence - 1, i] = acct[sequence, :, 128 * i : 128 * (i + 1)].astype(BF16)
-                rcopy(
-                    ga_stage.at[sequence - 1, i],
-                    ga_in.at[sequence_of(zh, o) - 1, i],
-                    ga_send,
-                    ga_recv.at[i],
-                    zh=o,
-                ).start()
+            for sequence in sequences:
+                send_grad(sequence, i)
 
     def old_moments():
         acct[0] = jnp.zeros((HD, SEQ), F32)
@@ -652,9 +655,13 @@
     multiply(2, 0)
     multiply(2, 1, 2)
     last_multiply(0)
+    pl.when(early == 0)(functools.partial(send_grads, 1))
     partner_across(3)
-    last_multiply(1, 2)
-    send_grads()
+    last_multiply(1)
+    pl.when(early == 0)(functools.partial(send_grads, 2))
+    pl.when(early == 2)(functools.partial(send_grads, 1))
+    last_multiply(2)
+    pl.when(early == 2)(functools.partial(send_grads, 2))
     last_term(1, 2)
 
     came(dw_in, dw_recv)

time: 81.3 us -> 80.2 us (0.986)
  Pallas kernels: 80.4 us -> 79.4 us
    pallas_call x1, Pallas kernels: 79.4 us -> 78.4 us  [per_device(): pl.pallas_call(body, name='whole', out_shape=(shape((SEQ, HD), BF16), sha...]
where the time goes in v13:
time: 80.2 us; the launch traced here: 80.1 us
  Pallas kernels  79.4 us (99%)
    pallas_call x1, Pallas kernels, per_device(): pl.pallas_call(body, name='whole', out_shape=(shape((SEQ, HD), BF16), sha...  78.4 us

profile of v13, /device:TPU:1, one launch (start us, length us, event | category | flops | bytes accessed | tf_op | source)
XLA Modules:
  0.0 80.1 jit_solution(13636907048037516384)
XLA Ops:
  0.6 78.4 %whole.1 = (bf16[384,128]{1,0:T(8,128)(2,1)S(1)}, f32[688,128]{1,0:T(8,128)S(1)}, f32[688,128]{1,0:T(8,128)S(1)}, f32[688,128]{1,0:T(8,128)S(1)}, f32[2,8,128]{2,1,0:T(8,128)S(1)}, /*index=5*/f32[2,128]{1,0:T(2,128)S(1)}) custom-call(bf16[384,128]{1,0:T(8,128)(2,1)} %q_hbm.1, bf16[384,1024]{1,0:T(8,128)(2,1)} %k_hbm.1, bf16[384,1024]{1,0:T(8,128)(2,1)} %v_hbm.1, ...), custom_call_target="tpu_custom_call" | custom-call | tf_op jit(solution)/shard_map/whole/pallas_call | solution.py:828
  79.1 1.0 %codes.1 = (bf16[384,128]{1,0:T(8,128)(2,1)}, f32[688,128]{1,0:T(8,128)}, bf16[688,128]{1,0:T(8,128)(2,1)}, f32[688]{0:T(1024)}, f32[128]{0:T(128)}, /*index=5*/...) custom-call(bf16[384,128]{1,0:T(8,128)(2,1)S(1)} %get-tuple-element.14.gq, f32[688,128]{1,0:T(8,128)S(1)} %get-tuple-element.15.nw, ...), custom_call_target="tpu_custom_call" | custom-call | tf_op jit(solution)/shard_map/codes/pallas_call | solution.py:909

commit v14 on v13

--- a/solution.py
+++ b/solution.py
@@ -570,10 +570,16 @@
             acct[sequence] = acct[sequence] + term[:, SEQ * i : SEQ * (i + 1)]
 
     def send_term(rows):
-        dw_stage[rows] = dwacc[rows].astype(BF16)
-        rcopy(
-            dw_stage.at[rows], dw_in.at[rows], dw_send, dw_recv, x=mod(x + AHEAD[rows], NX)
-        ).start()
+        for start, size in ((0, 352), (352, ROWS - 352)):
+            part = pl.ds(start, size)
+            dw_stage[rows, part, :] = dwacc[rows, part, :].astype(BF16)
+            rcopy(
+                dw_stage.at[rows, part],
+                dw_in.at[rows, part],
+                dw_send,
+                dw_recv,
+                x=mod(x + AHEAD[rows], NX),
+            ).start()
 
     def send_grad(sequence, i):
         o = other(sequence)

time: 80.2 us -> 80.2 us (level)
  no operation moved by 1% of the time
where the time goes in v14:
time: 80.2 us; the launch traced here: 80.1 us
  Pallas kernels  79.5 us (99%)
    pallas_call x1, Pallas kernels, per_device(): pl.pallas_call(body, name='whole', out_shape=(shape((SEQ, HD), BF16), sha...  78.4 us

profile of v14, /device:TPU:1, one launch (start us, length us, event | category | flops | bytes accessed | tf_op | source)
XLA Modules:
  0.0 80.1 jit_solution(13001207411633459481)
XLA Ops:
  0.6 78.4 %whole.1 = (bf16[384,128]{1,0:T(8,128)(2,1)S(1)}, f32[688,128]{1,0:T(8,128)S(1)}, f32[688,128]{1,0:T(8,128)S(1)}, f32[688,128]{1,0:T(8,128)S(1)}, f32[2,8,128]{2,1,0:T(8,128)S(1)}, /*index=5*/f32[2,128]{1,0:T(2,128)S(1)}) custom-call(bf16[384,128]{1,0:T(8,128)(2,1)} %q_hbm.1, bf16[384,1024]{1,0:T(8,128)(2,1)} %k_hbm.1, bf16[384,1024]{1,0:T(8,128)(2,1)} %v_hbm.1, ...), custom_call_target="tpu_custom_call" | custom-call | tf_op jit(solution)/shard_map/whole/pallas_call | solution.py:834
  79.1 1.0 %codes.1 = (bf16[384,128]{1,0:T(8,128)(2,1)}, f32[688,128]{1,0:T(8,128)}, bf16[688,128]{1,0:T(8,128)(2,1)}, f32[688]{0:T(1024)}, f32[128]{0:T(128)}, /*index=5*/...) custom-call(bf16[384,128]{1,0:T(8,128)(2,1)S(1)} %get-tuple-element.14.gq, f32[688,128]{1,0:T(8,128)S(1)} %get-tuple-element.15.nw, ...), custom_call_target="tpu_custom_call" | custom-call | tf_op jit(solution)/shard_map/codes/pallas_call | solution.py:915

commit v15 on v14

--- a/solution.py
+++ b/solution.py
@@ -656,12 +656,12 @@
     multiply(1, 0, 1)
     multiply(1, 2)
     partner_near(3)
-    last_term(0)
     pass_on(3, 4)
     multiply(2, 0)
     multiply(2, 1, 2)
     last_multiply(0)
     pl.when(early == 0)(functools.partial(send_grads, 1))
+    last_term(0)
     partner_across(3)
     last_multiply(1)
     pl.when(early == 0)(functools.partial(send_grads, 2))

time: 80.2 us -> 80.2 us (level)
  no operation moved by 1% of the time
where the time goes in v15:
time: 80.2 us; the launch traced here: 80 us
  Pallas kernels  79.4 us (99%)
    pallas_call x1, Pallas kernels, per_device(): pl.pallas_call(body, name='whole', out_shape=(shape((SEQ, HD), BF16), sha...  78.4 us

profile of v15, /device:TPU:1, one launch (start us, length us, event | category | flops | bytes accessed | tf_op | source)
XLA Modules:
  0.0 80.0 jit_solution(4249200031047784608)
XLA Ops:
  0.6 78.4 %whole.1 = (bf16[384,128]{1,0:T(8,128)(2,1)S(1)}, f32[688,128]{1,0:T(8,128)S(1)}, f32[688,128]{1,0:T(8,128)S(1)}, f32[688,128]{1,0:T(8,128)S(1)}, f32[2,8,128]{2,1,0:T(8,128)S(1)}, /*index=5*/f32[2,128]{1,0:T(2,128)S(1)}) custom-call(bf16[384,128]{1,0:T(8,128)(2,1)} %q_hbm.1, bf16[384,1024]{1,0:T(8,128)(2,1)} %k_hbm.1, bf16[384,1024]{1,0:T(8,128)(2,1)} %v_hbm.1, ...), custom_call_target="tpu_custom_call" | custom-call | tf_op jit(solution)/shard_map/whole/pallas_call | solution.py:834
  79.0 1.0 %codes.1 = (bf16[384,128]{1,0:T(8,128)(2,1)}, f32[688,128]{1,0:T(8,128)}, bf16[688,128]{1,0:T(8,128)(2,1)}, f32[688]{0:T(1024)}, f32[128]{0:T(128)}, /*index=5*/...) custom-call(bf16[384,128]{1,0:T(8,128)(2,1)S(1)} %get-tuple-element.14.gq, f32[688,128]{1,0:T(8,128)S(1)} %get-tuple-element.15.nw, ...), custom_call_target="tpu_custom_call" | custom-call | tf_op jit(solution)/shard_map/codes/pallas_call | solution.py:915

commit v16 on v15

--- a/solution.py
+++ b/solution.py
@@ -331,40 +331,43 @@
 
     lax.fori_loop(0, 8, spread, 0)
 
-    loads[4].wait()
-    wt[3] = w[...].astype(BF16).T
-    for dx in (1, 3, 2):
-        rcopy(wt.at[3], wt.at[AHEAD.index(NX - dx)], w_send, w_recv, x=mod(x + dx, NX)).start()
-
-    for i in (1, 2, 3):
-        loads[i].wait()
-    for i in range(3):
-        rows, cols = pl.ds(128 * i, 128), pl.ds(0, 128 * (i + 1))
-        scores = (
-            lax.dot_general(q[rows, :], kk[cols, :], NT, preferred_element_type=F32) * SCALE
-        )
-        future = lax.broadcasted_iota(jnp.int32, scores.shape, 1) > (
-            lax.broadcasted_iota(jnp.int32, scores.shape, 0) + 128 * i
-        )
-        scores = jnp.where(future, -1e30, scores)
-        exponent = jnp.exp(scores - jnp.max(scores, axis=-1, keepdims=True))
-        probabilities = exponent / jnp.sum(exponent, axis=-1, keepdims=True)
-        prob[rows, cols] = probabilities
-        att[0, rows, :] = jnp.dot(
-            probabilities.astype(BF16), vv[cols, :], preferred_element_type=F32
-        ).astype(BF16)
-
-    for slot, held in enumerate(units):
-        for j, (_, _, _, _, unit) in enumerate(held):
-            missing = unit >= ALL_UNITS
-            if j == 8:
-                missing = missing & (homes[slot] == HOMES - 1)
-            if slot in SPLIT:
-                missing = missing & (side == min(j // 4, 1))
-
-            @pl.when(missing)
-            def _():
-                gz[SLOT * slot + 8 * homes[slot] + j] = jnp.zeros((UNIT, SEQ), BF16)
+    def send_weights():
+        loads[4].wait()
+        wt[3] = w[...].astype(BF16).T
+        for dx in (1, 3, 2):
+            rcopy(wt.at[3], wt.at[AHEAD.index(NX - dx)], w_send, w_recv, x=mod(x + dx, NX)).start()
+
+    def attend():
+        for i in (1, 2, 3):
+            loads[i].wait()
+        for i in range(3):
+            rows, cols = pl.ds(128 * i, 128), pl.ds(0, 128 * (i + 1))
+            scores = (
+                lax.dot_general(q[rows, :], kk[cols, :], NT, preferred_element_type=F32) * SCALE
+            )
+            future = lax.broadcasted_iota(jnp.int32, scores.shape, 1) > (
+                lax.broadcasted_iota(jnp.int32, scores.shape, 0) + 128 * i
+            )
+            scores = jnp.where(future, -1e30, scores)
+            exponent = jnp.exp(scores - jnp.max(scores, axis=-1, keepdims=True))
+            probabilities = exponent / jnp.sum(exponent, axis=-1, keepdims=True)
+            prob[rows, cols] = probabilities
+            att[0, rows, :] = jnp.dot(
+                probabilities.astype(BF16), vv[cols, :], preferred_element_type=F32
+            ).astype(BF16)
+
+    def fill():
+        for slot, held in enumerate(units):
+            for j, (_, _, _, _, unit) in enumerate(held):
+                missing = unit >= ALL_UNITS
+                if j == 8:
+                    missing = missing & (homes[slot] == HOMES - 1)
+                if slot in SPLIT:
+                    missing = missing & (side == min(j // 4, 1))
+
+                @pl.when(missing)
+                def _():
+                    gz[SLOT * slot + 8 * homes[slot] + j] = jnp.zeros((UNIT, SEQ), BF16)
 
     def send_att():
         for sequence in (1, 2):
@@ -610,8 +613,11 @@
             weight = w[rows, :]
             nw_out[rows, :] = weight - learning * (decay_rate * weight)
 
+    send_weights()
+    fill()
     relay(0)
     start_ring(0)
+    attend()
     relay(1)
     relay(2)
     relay(3)

time: 80.2 us -> 80.4 us (level)
  no operation moved by 1% of the time
where the time goes in v16:
time: 80.4 us; the launch traced here: 80 us
  Pallas kernels  79.3 us (99%)
    pallas_call x1, Pallas kernels, per_device(): pl.pallas_call(body, name='whole', out_shape=(shape((SEQ, HD), BF16), sha...  78.3 us

profile of v16, /device:TPU:1, one launch (start us, length us, event | category | flops | bytes accessed | tf_op | source)
XLA Modules:
  0.0 80.0 jit_solution(6769025893098429201)
XLA Ops:
  0.6 78.3 %whole.1 = (bf16[384,128]{1,0:T(8,128)(2,1)S(1)}, f32[688,128]{1,0:T(8,128)S(1)}, f32[688,128]{1,0:T(8,128)S(1)}, f32[688,128]{1,0:T(8,128)S(1)}, f32[2,8,128]{2,1,0:T(8,128)S(1)}, /*index=5*/f32[2,128]{1,0:T(2,128)S(1)}) custom-call(bf16[384,128]{1,0:T(8,128)(2,1)} %q_hbm.1, bf16[384,1024]{1,0:T(8,128)(2,1)} %k_hbm.1, bf16[384,1024]{1,0:T(8,128)(2,1)} %v_hbm.1, ...), custom_call_target="tpu_custom_call" | custom-call | tf_op jit(solution)/shard_map/whole/pallas_call | solution.py:840
  78.9 1.0 %codes.1 = (bf16[384,128]{1,0:T(8,128)(2,1)}, f32[688,128]{1,0:T(8,128)}, bf16[688,128]{1,0:T(8,128)(2,1)}, f32[688]{0:T(1024)}, f32[128]{0:T(128)}, /*index=5*/...) custom-call(bf16[384,128]{1,0:T(8,128)(2,1)S(1)} %get-tuple-element.14.gq, f32[688,128]{1,0:T(8,128)S(1)} %get-tuple-element.15.nw, ...), custom_call_target="tpu_custom_call" | custom-call | tf_op jit(solution)/shard_map/codes/pallas_call | solution.py:921
